TPU v7x, 256 devices: a whole 4x4x8 slice. The times are simulated.
256 devices in a mesh: dp: 8 (over x, core), mp: 32 (over y, z).
Axes of the slice: x: 4, y: 4, z: 8, core: 2. Of those that a mesh axis runs over, the one named last changes fastest.
Arguments:
- gradients: bfloat16 [8, 4096, 16384], P('dp', None, 'mp'), may hold values from -40 to 40
- owner_table: int32 [512], replicated, may hold values from 0 to 31, as said below
Outputs:
- root_stacks: float32 [32, 24, 512, 512], P('mp', 'dp')
- slab_roots: float32 [16, 512, 16384], P(None, 'dp', 'mp')
Inputs may be any that keep to these rules, and one draw needn't show every extreme that they name: `owner_table`: statistic m * 16 + i belongs to column slab m. No owner is named by more than 24 statistics and some owner by exactly 24; among the 16 statistics of one column slab no owner is named more than 1 times, and some slab names some owner exactly 1 times.
All inputs are finite; a program needn't handle non-finite values.
Results may differ from a plain program's by a relative error of at most 0.0017.
Values may be sent and summed in bfloat16 or wider, within the bound.
No kernel may reach another device: no remote copies, remote signals or barrier semaphores. Data moves between devices by JAX's collectives and lax.ppermute only.
A program may use at most 320 MiB of HBM per device.

v0:
```python
import functools

import jax
import jax.numpy as jnp
from jax import lax
from jax.experimental import pallas as pl
from jax.experimental.pallas import tpu as pltpu
from jax.sharding import PartitionSpec as P


CAP = 24
BLOCK = 512
TILE = 128
DEVICES = 8
UPPER = [(0, 0), (0, 1), (0, 2), (0, 3), (1, 1), (1, 2), (1, 3), (2, 2), (2, 3), (3, 3)]
PACKED_ROWS = len(UPPER) * TILE
CHUNK = PACKED_ROWS // DEVICES
PIECE = CHUNK // 2
ROWS = BLOCK // DEVICES
ORDERS = ((1, 2, 0, 3), (3, 2, 0, 1))
FIRST_BITS = (2, 6)
SECOND_BITS = (6, 2)
VMEM_LIMIT = 24 * 2**20
GRAM_VMEM_LIMIT = 24 * 2**20
INTERPRET = False
F32 = jnp.float32
BF16 = jnp.bfloat16


def rows_of(block):
    return slice(block * TILE, (block + 1) * TILE)


def dot(first, second, dims=((1,), (0,))):
    return lax.dot_general(first, second, (dims, ((), ())), preferred_element_type=F32)


def iota(shape, axis):
    return lax.broadcasted_iota(jnp.int32, shape, axis)


def whole(memory_space=pltpu.VMEM):
    return pl.BlockSpec(memory_space=memory_space)


def params(limit=None):
    return pltpu.CompilerParams(vmem_limit_bytes=limit or VMEM_LIMIT)


def position(code_ref, model_count):
    return code_ref[0] // model_count, code_ref[0] % model_count


def cost(flops, moved):
    return pl.CostEstimate(flops=int(flops), bytes_accessed=int(moved), transcendentals=0)


def gram_kernel(model_count, code_ref, block_ref, own_ref, away_ref, stack_ref):
    block = block_ref[0]
    half = BLOCK // 2
    device, _ = position(code_ref, model_count)
    core = device & 1
    along = device >> 1
    for side in range(2):
        dims = ((1,), (1,)) if side == 0 else ((0,), (0,))
        low = block[:half] if side == 0 else block[:, :half]
        high = block[half:] if side == 0 else block[:, half:]
        right = dot(block, high, dims).astype(BF16)
        corner = dot(low, low, dims).astype(BF16)
        for index, (row, column) in enumerate(UPPER):
            if column >= 2:
                piece = right[rows_of(row), rows_of(column - 2)]
            else:
                piece = corner[rows_of(row), rows_of(column)]
            stack_ref[rows_of(index)] = piece
        for chip in range(4):
            offset = chip ^ along
            for part in range(2):
                place = jnp.int32(0)
                for spot, value in enumerate(ORDERS[part]):
                    place = jnp.where(offset == value, spot, place)
                even = stack_ref[pl.ds((4 * chip + part) * PIECE, PIECE)]
                odd = stack_ref[pl.ds((4 * chip + 2 + part) * PIECE, PIECE)]
                own_ref[part, place, side] = jnp.where(core == 0, even, odd)
                away_ref[part, place, side] = jnp.where(core == 0, odd, even)


def gram_blocks(blocks, code, model_count, first, count):
    shape = jax.ShapeDtypeStruct((2, 4, 2 * count, PIECE, TILE), BF16)
    out_spec = pl.BlockSpec((2, 4, 2, PIECE, TILE), lambda step, code_ref: (0, 0, step, 0, 0))
    return pl.pallas_call(
        functools.partial(gram_kernel, model_count),
        out_shape=(shape, shape),
        grid_spec=pltpu.PrefetchScalarGridSpec(
            num_scalar_prefetch=1,
            grid=(count,),
            in_specs=[
                pl.BlockSpec((1, BLOCK, BLOCK), lambda step, code_ref: (first + step, 0, 0))
            ],
            out_specs=[out_spec, out_spec],
            scratch_shapes=[pltpu.VMEM((PACKED_ROWS, TILE), BF16)],
        ),
        interpret=INTERPRET,
        compiler_params=params(GRAM_VMEM_LIMIT),
        cost_estimate=cost(3 * count * BLOCK**3, count * 5 * 2**18),
    )(code, blocks)


def plan_kernel(model_count, code_ref, table_ref, plan_ref):
    _, model = position(code_ref, model_count)
    for slot in range(CAP + 1):
        plan_ref[slot] = 0
    per_slab = table_ref.shape[0] // model_count

    def slab_step(slab, count):
        named = jnp.int32(0)
        for stat in range(per_slab):
            named = named | jnp.where(table_ref[slab * per_slab + stat] == model, 1, 0)

        @pl.when(named > 0)
        def _():
            plan_ref[count] = slab

        return count + named

    plan_ref[CAP] = lax.fori_loop(0, model_count, slab_step, jnp.int32(0))


def make_plan(code, owner_table, model_count):
    return pl.pallas_call(
        functools.partial(plan_kernel, model_count),
        in_specs=[whole(pltpu.SMEM), whole(pltpu.SMEM)],
        out_specs=whole(pltpu.SMEM),
        out_shape=jax.ShapeDtypeStruct((CAP + 1,), jnp.int32),
        interpret=INTERPRET,
        compiler_params=params(2**20),
        name="make_plan",
        cost_estimate=cost(2**22, 2**12),
    )(code, owner_table)


def sum_kernel(model_count, code_ref, table_ref, *refs):
    sources = refs[:8]
    outgoing_ref, *home_refs = refs[8 : 9 + DEVICES]
    mine_ref, send_ref, out_sems, home_sems = refs[9 + DEVICES :]
    device, model = position(code_ref, model_count)
    count = sources[0].shape[0]
    per_slab = 2 * count
    for group in range(2):
        for part in range(2):
            partial_ref, last_ref = sources[4 * group + 2 * part : 4 * group + 2 * part + 2]
            value = partial_ref[...] + last_ref[0].astype(F32)
            mine_ref[group * count : (group + 1) * count, part * PIECE : (part + 1) * PIECE] = (
                value.astype(BF16)
            )
    for owner in range(model_count):
        send_ref[owner] = 0
    for stat in range(per_slab):
        send_ref[table_ref[model * per_slab + stat]] = stat
    copies = []
    for owner in range(model_count):
        copies.append(
            pltpu.make_async_copy(
                mine_ref.at[send_ref[owner]], outgoing_ref.at[owner], out_sems.at[owner]
            )
        )
    for bits, home_ref in enumerate(home_refs):
        home = device ^ bits
        copies.append(
            pltpu.make_async_copy(mine_ref.at[pl.ds(2 * home, 2)], home_ref, home_sems.at[bits])
        )
    for copy in copies:
        copy.start()
    for copy in copies:
        copy.wait()


def sum_and_send(code, owner_table, sources, model_count):
    count = sources[0].shape[0]
    home = jax.ShapeDtypeStruct((2, CHUNK, TILE), BF16)
    return pl.pallas_call(
        functools.partial(sum_kernel, model_count),
        in_specs=[whole(pltpu.SMEM), whole(pltpu.SMEM)] + [whole()] * 8,
        out_specs=[whole(pltpu.HBM)] * (1 + DEVICES),
        out_shape=[jax.ShapeDtypeStruct((model_count, CHUNK, TILE), BF16)] + [home] * DEVICES,
        scratch_shapes=[
            pltpu.VMEM((2 * count, CHUNK, TILE), BF16),
            pltpu.SMEM((model_count,), jnp.int32),
            pltpu.SemaphoreType.DMA((model_count,)),
            pltpu.SemaphoreType.DMA((DEVICES,)),
        ],
        interpret=INTERPRET,
        compiler_params=params(),
        name="sum_and_send",
        cost_estimate=cost(2**21, 2**22),
    )(code, owner_table, *sources)


def slot_kernel(plan_ref, source_ref, out_ref, sems):
    copies = []
    for slot in range(CAP):
        copies.append(
            pltpu.make_async_copy(source_ref.at[plan_ref[slot]], out_ref.at[slot], sems.at[slot])
        )
    for copy in copies:
        copy.start()
    for copy in copies:
        copy.wait()


def slot_pick(plan, incoming):
    return pl.pallas_call(
        slot_kernel,
        in_specs=[whole(pltpu.SMEM), whole()],
        out_specs=whole(pltpu.HBM),
        out_shape=jax.ShapeDtypeStruct((CAP, CHUNK, TILE), BF16),
        scratch_shapes=[pltpu.SemaphoreType.DMA((CAP,))],
        interpret=INTERPRET,
        compiler_params=params(8 * 2**20),
        name="slot_pick",
        cost_estimate=cost(2**21, 2**22),
    )(plan, incoming)


def total(value):
    return jnp.sum(jnp.sum(value, axis=0, keepdims=True), axis=1, keepdims=True)


def root_of(chunk_piece, data_count, stat_ref, pair_ref):
    for index, (row, column) in enumerate(UPPER):
        start, stop = index * TILE, (index + 1) * TILE
        while start < stop:
            chunk = start // CHUNK
            end = min(stop, (chunk + 1) * CHUNK)
            piece = chunk_piece(chunk, start - chunk * CHUNK, end - chunk * CHUNK)
            base = row * TILE + start - index * TILE
            stat_ref[base : base + end - start, rows_of(column)] = piece
            start = end
        if row != column:
            stat_ref[rows_of(column), rows_of(row)] = stat_ref[rows_of(row), rows_of(column)].T
    on_diagonal = iota((BLOCK, BLOCK), 0) == iota((BLOCK, BLOCK), 1)
    statistic = stat_ref[...] * (1.0 / data_count)
    diagonal_mean = total(jnp.where(on_diagonal, statistic, 0.0)) * (1.0 / BLOCK)
    damped = statistic + jnp.where(on_diagonal, 0.1 * diagonal_mean, 0.0)
    mean_square = total(damped * damped) * (1.0 / BLOCK**2)
    norm_scale = BLOCK * jnp.sqrt(mean_square + 1e-06)
    root_scale = lax.rsqrt(jnp.sqrt(norm_scale))
    first = damped * (1.0 / norm_scale)
    first_small = first.astype(BF16)
    part = (dot(first_small, first_small) * 0.0625 - 0.625 * first).astype(BF16)
    twice = 1.5625 * first + dot(part, first_small)
    twice_small = twice.astype(BF16)
    pair_ref[:BLOCK] = part
    pair_ref[BLOCK:] = twice_small
    both = dot(pair_ref[...], twice_small)
    second = 1.5625 * twice + both[:BLOCK]
    pair = (both[BLOCK:] * 0.0625 - 0.3125 * (first + second)).astype(BF16)
    second_small = second.astype(BF16)
    part = (dot(second_small, second_small) * 0.0625 - 0.625 * second).astype(BF16)
    twice = 1.5625 * second + dot(part, second_small)
    third = 1.5625 * twice + dot(part, twice.astype(BF16))
    rest = 1.25 * pair.astype(F32) - 0.390625 * third - 0.25 * dot(pair, third.astype(BF16))
    return rest * root_scale, 1.953125 * root_scale, on_diagonal


def home_kernel(data_count, model_count, code_ref, *refs):
    sources, row_refs = refs[:DEVICES], refs[DEVICES : 2 * DEVICES]
    rows_ref, stack_ref, stat_ref, pair_ref = refs[2 * DEVICES :]
    device, _ = position(code_ref, model_count)
    row_ids = iota((BLOCK, BLOCK), 0)
    spare = (row_ids % ROWS == 1) & (iota((BLOCK, BLOCK), 1) == row_ids - 1)
    for stat in range(2):
        for bits, ref in enumerate(sources):
            stack_ref[device ^ bits] = ref[stat].astype(F32)
        rest, identity_part, on_diagonal = root_of(
            lambda chunk, start, stop: stack_ref[chunk, start:stop], data_count, stat_ref, pair_ref
        )
        rest_mean = total(jnp.where(on_diagonal, rest, 0.0)) * (1.0 / BLOCK)
        center = (identity_part + rest_mean).astype(BF16).astype(F32)
        rest = rest + jnp.where(on_diagonal, identity_part - center, 0.0)
        sent = jnp.where(spare, center, rest).astype(BF16)
        for home in range(DEVICES):
            rows_ref[home] = sent[home * ROWS : (home + 1) * ROWS]
        for bits, row_ref in enumerate(row_refs):
            row_ref[stat] = rows_ref[device ^ bits]


def home_roots(code, sources, data_count, model_count):
    return pl.pallas_call(
        functools.partial(home_kernel, data_count, model_count),
        in_specs=[whole(pltpu.SMEM)] + [whole()] * DEVICES,
        out_specs=[whole()] * DEVICES,
        out_shape=[jax.ShapeDtypeStruct((2, ROWS, BLOCK), BF16)] * DEVICES,
        scratch_shapes=[
            pltpu.VMEM((DEVICES, ROWS, BLOCK), BF16),
            pltpu.VMEM((DEVICES, CHUNK, TILE), F32),
            pltpu.VMEM((BLOCK, BLOCK), F32),
            pltpu.VMEM((2 * BLOCK, BLOCK), BF16),
        ],
        interpret=INTERPRET,
        compiler_params=params(),
        name="home_roots",
        cost_estimate=cost(2 * 8 * 2 * BLOCK**3, 2**22),
    )(code, *sources)


def owner_kernel(data_count, model_count, code_ref, plan_ref, source_ref, out_ref, stat_ref, pair_ref):
    device, _ = position(code_ref, model_count)
    slot = pl.program_id(0)
    keep = pl.num_programs(0) * device + slot < plan_ref[CAP]

    @pl.when(keep)
    def _():
        rest, identity_part, on_diagonal = root_of(
            lambda chunk, start, stop: source_ref[chunk, 0, start:stop].astype(F32),
            data_count,
            stat_ref,
            pair_ref,
        )
        out_ref[0] = rest + jnp.where(on_diagonal, identity_part, 0.0)

    @pl.when(jnp.logical_not(keep))
    def _():
        out_ref[...] = jnp.zeros_like(out_ref)


def owner_roots(code, plan, source, data_count, model_count):
    slots = source.shape[1]
    return pl.pallas_call(
        functools.partial(owner_kernel, data_count, model_count),
        grid=(slots,),
        in_specs=[
            whole(pltpu.SMEM),
            whole(pltpu.SMEM),
            pl.BlockSpec((DEVICES, 1, CHUNK, TILE), lambda slot: (0, slot, 0, 0)),
        ],
        out_specs=pl.BlockSpec((1, BLOCK, BLOCK), lambda slot: (slot, 0, 0)),
        out_shape=jax.ShapeDtypeStruct((slots, BLOCK, BLOCK), F32),
        scratch_shapes=[
            pltpu.VMEM((BLOCK, BLOCK), F32),
            pltpu.VMEM((2 * BLOCK, BLOCK), BF16),
        ],
        interpret=INTERPRET,
        compiler_params=params(),
        name="owner_roots",
        cost_estimate=cost(3 * 8 * 2 * BLOCK**3, 2**22),
    )(code, plan, source)


def finish_kernel(model_count, code_ref, *refs):
    out_ref = refs[-1]
    device, _ = position(code_ref, model_count)
    first = device * ROWS
    row_ids = iota((ROWS, BLOCK), 0)
    column_ids = iota((ROWS, BLOCK), 1) - first
    spare = (row_ids == 1) & (column_ids == 0)
    mirror = (row_ids == 0) & (column_ids == 1)
    on_diagonal = row_ids == column_ids
    for bits, ref in enumerate(refs[:-1]):
        home = device ^ bits
        for stat in range(2):
            value = ref[stat].astype(F32)
            center = total(jnp.where(spare[:8], value[:8], 0.0))
            mirrored = total(jnp.where(mirror[:8], value[:8], 0.0))
            value = jnp.where(spare, mirrored, value)
            out_ref[2 * home + stat] = value + jnp.where(on_diagonal, center, 0.0)


def finish_rows(code, rows, model_count):
    return pl.pallas_call(
        functools.partial(finish_kernel, model_count),
        in_specs=[whole(pltpu.SMEM)] + [whole()] * DEVICES,
        out_specs=whole(),
        out_shape=jax.ShapeDtypeStruct((2 * DEVICES, ROWS, BLOCK), F32),
        interpret=INTERPRET,
        compiler_params=params(),
        name="finish_rows",
        cost_estimate=cost(2**21, 2**22),
    )(code, *rows)


def exchange(value, bits, data_count):
    return lax.ppermute(value, "dp", [(d, d ^ bits) for d in range(data_count)])


def exchange_all(values, data_count):
    return [values[0]] + [
        exchange(values[bits], bits, data_count) for bits in range(1, data_count)
    ]


def program(gradients, owner_table):
    data_count = lax.axis_size("dp")
    model_count = lax.axis_size("mp")
    row_blocks = gradients.shape[1] // BLOCK
    blocks = gradients[0].reshape(row_blocks, BLOCK, BLOCK)
    code = (lax.axis_index("dp") * model_count + lax.axis_index("mp")).reshape(1)

    sources = []
    for group in range(2):
        own, away = gram_blocks(blocks, code, model_count, group * row_blocks // 2, row_blocks // 2)
        got = exchange(away, 1, data_count)
        for part in range(2):
            first = own[part, :2].astype(F32) + got[part, :2].astype(F32)
            step = exchange(first.astype(BF16), FIRST_BITS[part], data_count)
            second = own[part, 3:].astype(F32) + got[part, 3:].astype(F32) + step[1:].astype(F32)
            last = exchange(second.astype(BF16), SECOND_BITS[part], data_count)
            sources.append(
                own[part, 2].astype(F32) + got[part, 2].astype(F32) + step[0].astype(F32)
            )
            sources.append(last)

    plan = make_plan(code, owner_table, model_count)
    outgoing, *home = sum_and_send(code, owner_table, sources, model_count)
    incoming = lax.all_to_all(outgoing, "mp", split_axis=0, concat_axis=0, tiled=True)

    rows = list(home_roots(code, exchange_all(home, data_count), data_count, model_count))
    incoming, rows[0] = lax.optimization_barrier((incoming, rows[0]))
    rows = exchange_all(rows, data_count)
    slab_roots = finish_rows(code, rows, model_count)

    slots = slot_pick(plan, incoming)
    stacked = lax.all_to_all(slots, "dp", split_axis=0, concat_axis=0, tiled=True)
    stacked = stacked.reshape(data_count, CAP // data_count, CHUNK, TILE)
    root_stacks = owner_roots(code, plan, stacked, data_count, model_count)
    return (root_stacks[None], slab_roots)


def solution(mesh):
    placed = (P("dp", None, "mp"), P())
    return jax.shard_map(
        program,
        mesh=mesh,
        in_specs=placed,
        out_specs=(P("mp", "dp", None, None), P(None, "dp", "mp")),
        check_vma=False,
    )
```

profile of v0, /device:TPU:1, one launch (start us, length us, event | category | flops | bytes accessed | tf_op | source)
XLA Modules:
  0.0 130.1 jit_solution(10554494668696857935)
XLA Ops:
  0.6 2.2 %copy-done.1 = bf16[1,4096,512]{2,1,0:T(8,128)(2,1)S(1)} copy-done((bf16[1,4096,512]{2,1,0:T(8,128)(2,1)S(1)}, bf16[1,4096,512]{2,1,0:T(8,128)(2,1)}, u32[]{:S(2)}) %copy-start.1) | copy-done | bytes 4194328
  2.8 3.1 %shard_map.42 = (bf16[2,4,8,80,128]{4,3,2,1,0:T(8,128)(2,1)S(1)}, bf16[2,4,8,80,128]{4,3,2,1,0:T(8,128)(2,1)S(1)}) custom-call(s32[1]{0:T(128)} %bitcast.code_ref, bf16[8,512,512]{2,1,0:T(8,128)(2,1)S(1)} %bitcast.57), custom_call_target="tpu_custom_call" | custom-call | flops 1610612736 | bytes 5242880 | tf_op jit(solution)/shard_map/pallas_call | solution.py:91
  5.9 3.3 %collective-permute-start.5 = (bf16[2,4,8,80,128]{4,3,2,1,0:T(8,128)(2,1)S(1)}, bf16[2,4,8,80,128]{4,3,2,1,0:T(8,128)(2,1)S(1)}, u32[]{:S(2)}, u32[]{:S(2)}) collective-permute-start(bf16[2,4,8,80,128]{4,3,2,1,0:T(8,128)(2,1)S(1)} %get-tuple-element.28), channel_id=1, source_target_pairs={{0,32},{32,0},{64,96},{96,64},{128,160},{160,128},{192,224},{224,1... | collective-permute-start | bytes 3932168 | tf_op jit(solution)/shard_map/ppermute | solution.py:383
  9.2 3.1 %shard_map.41 = (bf16[2,4,8,80,128]{4,3,2,1,0:T(8,128)(2,1)S(1)}, bf16[2,4,8,80,128]{4,3,2,1,0:T(8,128)(2,1)S(1)}) custom-call(s32[1]{0:T(128)} %bitcast.code_ref, bf16[8,512,512]{2,1,0:T(8,128)(2,1)S(1)} %bitcast.58), custom_call_target="tpu_custom_call" | custom-call | flops 1610612736 | bytes 5242880 | tf_op jit(solution)/shard_map/pallas_call | solution.py:91
  13.4 2.0 %collective-permute-done = bf16[2,4,8,80,128]{4,3,2,1,0:T(8,128)(2,1)S(1)} collective-permute-done((bf16[2,4,8,80,128]{4,3,2,1,0:T(8,128)(2,1)S(1)}, bf16[2,4,8,80,128]{4,3,2,1,0:T(8,128)(2,1)S(1)}, u32[]{:S(2)}, u32[]{:S(2)}) %collective-permute-start) | collective-permute-done | bytes 1310752 | tf_op jit(solution)/shard_map/ppermute | solution.py:383
  16.5 6.2 %collective-permute-done.8 = bf16[2,8,80,128]{3,2,1,0:T(8,128)(2,1)S(1)} collective-permute-done((bf16[2,8,80,128]{3,2,1,0:T(8,128)(2,1)S(1)}, bf16[2,8,80,128]{3,2,1,0:T(8,128)(2,1)S(1)}, u32[]{:S(2)}, u32[]{:S(2)}) %collective-permute-start.8) | collective-permute-done | bytes 327712 | tf_op jit(solution)/shard_map/ppermute | solution.py:383
  22.9 1.5 %collective-permute-start.7 = (bf16[1,8,80,128]{3,2,1,0:T(8,128)(2,1)S(1)}, bf16[1,8,80,128]{3,2,1,0:T(8,128)(2,1)S(1)}, u32[]{:S(2)}, u32[]{:S(2)}) collective-permute-start(bf16[1,8,80,128]{3,2,1,0:T(8,128)(2,1)S(1)} %get-tuple-element.49), channel_id=1, source_target_pairs={{0,192},{32,224},{64,128},{96,160},{128,64},{160,96},{192,0},{224,... | collective-permute-start | bytes 491528 | tf_op jit(solution)/shard_map/ppermute | solution.py:383
  24.4 5.3 %collective-permute-done.3 = bf16[2,8,80,128]{3,2,1,0:T(8,128)(2,1)S(1)} collective-permute-done((bf16[2,8,80,128]{3,2,1,0:T(8,128)(2,1)S(1)}, bf16[2,8,80,128]{3,2,1,0:T(8,128)(2,1)S(1)}, u32[]{:S(2)}, u32[]{:S(2)}) %collective-permute-start.3) | collective-permute-done | bytes 327712 | tf_op jit(solution)/shard_map/ppermute | solution.py:383
  30.0 1.4 %collective-permute-start.2 = (bf16[1,8,80,128]{3,2,1,0:T(8,128)(2,1)S(1)}, bf16[1,8,80,128]{3,2,1,0:T(8,128)(2,1)S(1)}, u32[]{:S(2)}, u32[]{:S(2)}) collective-permute-start(bf16[1,8,80,128]{3,2,1,0:T(8,128)(2,1)S(1)} %get-tuple-element.55), channel_id=1, source_target_pairs={{0,192},{32,224},{64,128},{96,160},{128,64},{160,96},{192,0},{224,... | collective-permute-start | bytes 491528 | tf_op jit(solution)/shard_map/ppermute | solution.py:383
  33.2 2.3 %collective-permute-done.4.refs_3_ = bf16[1,8,80,128]{3,2,1,0:T(8,128)(2,1)S(1)} collective-permute-done((bf16[1,8,80,128]{3,2,1,0:T(8,128)(2,1)S(1)}, bf16[1,8,80,128]{3,2,1,0:T(8,128)(2,1)S(1)}, u32[]{:S(2)}, u32[]{:S(2)}) %collective-permute-start.4) | collective-permute-done | bytes 163872 | tf_op jit(solution)/shard_map/ppermute | solution.py:383
  35.6 2.2 %sum_and_send.1 = (bf16[32,160,128]{2,1,0:T(8,128)(2,1)}, bf16[2,160,128]{2,1,0:T(8,128)(2,1)S(1)}, bf16[2,160,128]{2,1,0:T(8,128)(2,1)S(1)}, bf16[2,160,128]{2,...) custom-call(s32[1]{0:T(128)} %bitcast.code_ref, ...), custom_call_target="tpu_custom_call" | custom-call | flops 2097152 | bytes 4194304 | tf_op jit(solution)/shard_map/sum_and_send/pallas_call | solution.py:181
  37.8 11.3 %all-to-all-start = ((bf16[32,160,128]{2,1,0:T(8,128)(2,1)}), bf16[32,160,128]{2,1,0:T(8,128)(2,1)S(1)}, u32[]{:S(2)}, u32[]{:S(2)}) async-start(bf16[32,160,128]{2,1,0:T(8,128)(2,1)} %get-tuple-element.29), calls=%async_computation | async-start | bytes 2621440 | tf_op jit(solution)/shard_map/all_to_all | solution.py:415
  49.1 3.4 %collective-permute-start.10 = (bf16[2,160,128]{2,1,0:T(8,128)(2,1)S(1)}, bf16[2,160,128]{2,1,0:T(8,128)(2,1)S(1)}, u32[]{:S(2)}, u32[]{:S(2)}) collective-permute-start(bf16[2,160,128]{2,1,0:T(8,128)(2,1)S(1)} %get-tuple-element.31), channel_id=1, source_target_pairs={{0,32},{32,0},{64,96},{96,64},{128,160},{160,128},{192,224},{224,1... | collective-permute-start | bytes 245768 | tf_op jit(solution)/shard_map/ppermute | solution.py:383
  55.2 2.3 %collective-permute-start.14 = (bf16[2,160,128]{2,1,0:T(8,128)(2,1)S(1)}, bf16[2,160,128]{2,1,0:T(8,128)(2,1)S(1)}, u32[]{:S(2)}, u32[]{:S(2)}) collective-permute-start(bf16[2,160,128]{2,1,0:T(8,128)(2,1)S(1)} %get-tuple-element.35), channel_id=1, source_target_pairs={{0,160},{32,128},{64,224},{96,192},{128,32},{160,0},{192,96},{224,... | collective-permute-start | bytes 245768 | tf_op jit(solution)/shard_map/ppermute | solution.py:383
  58.4 2.1 %collective-permute-start.16 = (bf16[2,160,128]{2,1,0:T(8,128)(2,1)S(1)}, bf16[2,160,128]{2,1,0:T(8,128)(2,1)S(1)}, u32[]{:S(2)}, u32[]{:S(2)}) collective-permute-start(bf16[2,160,128]{2,1,0:T(8,128)(2,1)S(1)} %get-tuple-element.37), channel_id=1, source_target_pairs={{0,224},{32,192},{64,160},{96,128},{128,96},{160,64},{192,32},{224... | collective-permute-start | bytes 245768 | tf_op jit(solution)/shard_map/ppermute | solution.py:383
  60.5 2.0 %make_plan.1.plan_ref = s32[25]{0:T(128)S(1)} custom-call(s32[1]{0:T(128)} %bitcast.code_ref, s32[512]{0:T(512)S(1)} %copy-done), custom_call_target="tpu_custom_call" | custom-call | flops 4194304 | bytes 4096 | tf_op jit(solution)/shard_map/make_plan/pallas_call | solution.py:130
  62.9 1.7 %collective-permute-done.15.refs_6_ = bf16[2,160,128]{2,1,0:T(8,128)(2,1)S(1)} collective-permute-done((bf16[2,160,128]{2,1,0:T(8,128)(2,1)S(1)}, bf16[2,160,128]{2,1,0:T(8,128)(2,1)S(1)}, u32[]{:S(2)}, u32[]{:S(2)}) %collective-permute-start.15) | collective-permute-done | bytes 81952 | tf_op jit(solution)/shard_map/ppermute | solution.py:383
  64.6 1.8 %collective-permute-done.16.refs_7_ = bf16[2,160,128]{2,1,0:T(8,128)(2,1)S(1)} collective-permute-done((bf16[2,160,128]{2,1,0:T(8,128)(2,1)S(1)}, bf16[2,160,128]{2,1,0:T(8,128)(2,1)S(1)}, u32[]{:S(2)}, u32[]{:S(2)}) %collective-permute-start.16) | collective-permute-done | bytes 81952 | tf_op jit(solution)/shard_map/ppermute | solution.py:383
  66.4 6.0 %home_roots.1 = (bf16[2,64,512]{2,1,0:T(8,128)(2,1)S(1)}, bf16[2,64,512]{2,1,0:T(8,128)(2,1)S(1)}, bf16[2,64,512]{2,1,0:T(8,128)(2,1)S(1)}, bf16[2,64,512]{2,1,0...) custom-call(s32[1]{0:T(128)} %bitcast.code_ref, ...), custom_call_target="tpu_custom_call" | custom-call | flops 4294967296 | bytes 4194304 | tf_op jit(solution)/shard_map/home_roots/pallas_call | solution.py:289
  72.4 4.2 %all-to-all-done.source_ref = bf16[32,160,128]{2,1,0:T(8,128)(2,1)S(1)} async-done(((bf16[32,160,128]{2,1,0:T(8,128)(2,1)}), bf16[32,160,128]{2,1,0:T(8,128)(2,1)S(1)}, u32[]{:S(2)}, u32[]{:S(2)}) %all-to-all-start) | async-done | bytes 1310752 | tf_op jit(solution)/shard_map/all_to_all | solution.py:415
  76.6 1.7 %slot_pick.1 = bf16[24,160,128]{2,1,0:T(8,128)(2,1)} custom-call(s32[25]{0:T(128)S(1)} %make_plan.1.plan_ref, bf16[32,160,128]{2,1,0:T(8,128)(2,1)S(1)} %all-to-all-done.source_ref), custom_call_target="tpu_custom_call" | custom-call | flops 2097152 | bytes 4194304 | tf_op jit(solution)/shard_map/slot_pick/pallas_call | solution.py:212
  78.3 11.0 %all-to-all-start.1 = ((bf16[24,160,128]{2,1,0:T(8,128)(2,1)}), bf16[24,160,128]{2,1,0:T(8,128)(2,1)S(1)}, u32[]{:S(2)}, u32[]{:S(2)}) async-start(bf16[24,160,128]{2,1,0:T(8,128)(2,1)} %slot_pick.1), calls=%async_computation.1 | async-start | bytes 1966080 | tf_op jit(solution)/shard_map/all_to_all | solution.py:423
  89.5 1.6 %collective-permute-start.18 = (bf16[2,64,512]{2,1,0:T(8,128)(2,1)S(1)}, bf16[2,64,512]{2,1,0:T(8,128)(2,1)S(1)}, u32[]{:S(2)}, u32[]{:S(2)}) collective-permute-start(bf16[2,64,512]{2,1,0:T(8,128)(2,1)S(1)} %get-tuple-element.42), channel_id=1, source_target_pairs={{0,64},{32,96},{64,0},{96,32},{128,192},{160,224},{192,128},{224,1... | collective-permute-start | bytes 393224 | tf_op jit(solution)/shard_map/ppermute | solution.py:383
  91.4 2.9 %collective-permute-start.20 = (bf16[2,64,512]{2,1,0:T(8,128)(2,1)S(1)}, bf16[2,64,512]{2,1,0:T(8,128)(2,1)S(1)}, u32[]{:S(2)}, u32[]{:S(2)}) collective-permute-start(bf16[2,64,512]{2,1,0:T(8,128)(2,1)S(1)} %get-tuple-element.44), channel_id=1, source_target_pairs={{0,128},{32,160},{64,192},{96,224},{128,0},{160,32},{192,64},{224,... | collective-permute-start | bytes 393224 | tf_op jit(solution)/shard_map/ppermute | solution.py:383
  94.6 2.7 %collective-permute-start.22 = (bf16[2,64,512]{2,1,0:T(8,128)(2,1)S(1)}, bf16[2,64,512]{2,1,0:T(8,128)(2,1)S(1)}, u32[]{:S(2)}, u32[]{:S(2)}) collective-permute-start(bf16[2,64,512]{2,1,0:T(8,128)(2,1)S(1)} %get-tuple-element.46), channel_id=1, source_target_pairs={{0,192},{32,224},{64,128},{96,160},{128,64},{160,96},{192,0},{224,... | collective-permute-start | bytes 393224 | tf_op jit(solution)/shard_map/ppermute | solution.py:383
  97.3 7.6 %collective-permute-done.18.refs_2_ = bf16[2,64,512]{2,1,0:T(8,128)(2,1)S(1)} collective-permute-done((bf16[2,64,512]{2,1,0:T(8,128)(2,1)S(1)}, bf16[2,64,512]{2,1,0:T(8,128)(2,1)S(1)}, u32[]{:S(2)}, u32[]{:S(2)}) %collective-permute-start.18) | collective-permute-done | bytes 131104 | tf_op jit(solution)/shard_map/ppermute | solution.py:383
  104.9 3.2 %collective-permute-start.23 = (bf16[2,64,512]{2,1,0:T(8,128)(2,1)S(1)}, bf16[2,64,512]{2,1,0:T(8,128)(2,1)S(1)}, u32[]{:S(2)}, u32[]{:S(2)}) collective-permute-start(bf16[2,64,512]{2,1,0:T(8,128)(2,1)S(1)} %get-tuple-element.47), channel_id=1, source_target_pairs={{0,224},{32,192},{64,160},{96,128},{128,96},{160,64},{192,32},{224... | collective-permute-start | bytes 393224 | tf_op jit(solution)/shard_map/ppermute | solution.py:383
  108.6 3.5 %collective-permute-done.20.refs_4_ = bf16[2,64,512]{2,1,0:T(8,128)(2,1)S(1)} collective-permute-done((bf16[2,64,512]{2,1,0:T(8,128)(2,1)S(1)}, bf16[2,64,512]{2,1,0:T(8,128)(2,1)S(1)}, u32[]{:S(2)}, u32[]{:S(2)}) %collective-permute-start.20) | collective-permute-done | bytes 131104 | tf_op jit(solution)/shard_map/ppermute | solution.py:383
  112.1 3.1 %collective-permute-done.21.refs_5_ = bf16[2,64,512]{2,1,0:T(8,128)(2,1)S(1)} collective-permute-done((bf16[2,64,512]{2,1,0:T(8,128)(2,1)S(1)}, bf16[2,64,512]{2,1,0:T(8,128)(2,1)S(1)}, u32[]{:S(2)}, u32[]{:S(2)}) %collective-permute-start.21) | collective-permute-done | bytes 131104 | tf_op jit(solution)/shard_map/ppermute | solution.py:383
  115.3 2.4 %collective-permute-done.23.refs_7_ = bf16[2,64,512]{2,1,0:T(8,128)(2,1)S(1)} collective-permute-done((bf16[2,64,512]{2,1,0:T(8,128)(2,1)S(1)}, bf16[2,64,512]{2,1,0:T(8,128)(2,1)S(1)}, u32[]{:S(2)}, u32[]{:S(2)}) %collective-permute-start.23) | collective-permute-done | bytes 131104 | tf_op jit(solution)/shard_map/ppermute | solution.py:383
  117.6 1.7 %finish_rows.1 = f32[16,64,512]{2,1,0:T(8,128)} custom-call(s32[1]{0:T(128)} %bitcast.code_ref, bf16[2,64,512]{2,1,0:T(8,128)(2,1)S(1)} %get-tuple-element.40.refs_0_, bf16[2,64,512]{2,1,0:T(8,128)(2,1)S(1)} %collective-permute-done.17.refs_1_, bf16[2,64,512]{2,1,0:T(8,128)(2,1)S(1)} %collective-permute-done.18.refs_2_, ...), custom_call_target="tpu_custom_call" | custom-call | flops 2097152 | bytes 4194304 | tf_op jit(solution)/shard_map/finish_rows/pallas_call | solution.py:370
  119.4 10.7 %owner_roots.1 = f32[3,512,512]{2,1,0:T(8,128)} custom-call(s32[1]{0:T(128)} %bitcast.code_ref, s32[25]{0:T(128)S(1)} %make_plan.1.plan_ref, bf16[8,3,160,128]{3,2,1,0:T(8,128)(2,1)S(1)} %bitcast.56), custom_call_target="tpu_custom_call" | custom-call | flops 6442450944 | bytes 4194304 | tf_op jit(solution)/shard_map/owner_roots/pallas_call | solution.py:329
  (38 shorter events, 9.8 us)
Async XLA Ops:
  0.6 2.2 %copy-start.1 = (bf16[1,4096,512]{2,1,0:T(8,128)(2,1)S(1)}, bf16[1,4096,512]{2,1,0:T(8,128)(2,1)}, u32[]{:S(2)}) copy-start(bf16[1,4096,512]{2,1,0:T(8,128)(2,1)} %param.2) | copy-start | bytes 12582916
  5.9 6.5 %collective-permute-start.5 = (bf16[2,4,8,80,128]{4,3,2,1,0:T(8,128)(2,1)S(1)}, bf16[2,4,8,80,128]{4,3,2,1,0:T(8,128)(2,1)S(1)}, u32[]{:S(2)}, u32[]{:S(2)}) collective-permute-start(bf16[2,4,8,80,128]{4,3,2,1,0:T(8,128)(2,1)S(1)} %get-tuple-element.28), channel_id=1, source_target_pairs={{0,32},{32,0},{64,96},{96,64},{128,160},{160,128},{192,224},{224,1... | collective-permute-start | bytes 3932168 | tf_op jit(solution)/shard_map/ppermute | solution.py:383
  12.3 3.1 %collective-permute-start = (bf16[2,4,8,80,128]{4,3,2,1,0:T(8,128)(2,1)S(1)}, bf16[2,4,8,80,128]{4,3,2,1,0:T(8,128)(2,1)S(1)}, u32[]{:S(2)}, u32[]{:S(2)}) collective-permute-start(bf16[2,4,8,80,128]{4,3,2,1,0:T(8,128)(2,1)S(1)} %get-tuple-element.26), channel_id=1, source_target_pairs={{0,32},{32,0},{64,96},{96,64},{128,160},{160,128},{192,224},{224,1... | collective-permute-start | bytes 3932168 | tf_op jit(solution)/shard_map/ppermute | solution.py:383
  12.6 10.1 %collective-permute-start.8 = (bf16[2,8,80,128]{3,2,1,0:T(8,128)(2,1)S(1)}, bf16[2,8,80,128]{3,2,1,0:T(8,128)(2,1)S(1)}, u32[]{:S(2)}, u32[]{:S(2)}) collective-permute-start(bf16[2,8,80,128]{3,2,1,0:T(8,128)(2,1)S(1)} %get-tuple-element.52), channel_id=1, source_target_pairs={{0,192},{32,224},{64,128},{96,160},{128,64},{160,96},{192,0},{224,... | collective-permute-start | bytes 983048 | tf_op jit(solution)/shard_map/ppermute | solution.py:383
  13.4 9.2 %collective-permute-start.6 = (bf16[2,8,80,128]{3,2,1,0:T(8,128)(2,1)S(1)}, bf16[2,8,80,128]{3,2,1,0:T(8,128)(2,1)S(1)}, u32[]{:S(2)}, u32[]{:S(2)}) collective-permute-start(bf16[2,8,80,128]{3,2,1,0:T(8,128)(2,1)S(1)} %get-tuple-element.53), channel_id=1, source_target_pairs={{0,64},{32,96},{64,0},{96,32},{128,192},{160,224},{192,128},{224,1... | collective-permute-start | bytes 983048 | tf_op jit(solution)/shard_map/ppermute | solution.py:383
  15.6 14.1 %collective-permute-start.3 = (bf16[2,8,80,128]{3,2,1,0:T(8,128)(2,1)S(1)}, bf16[2,8,80,128]{3,2,1,0:T(8,128)(2,1)S(1)}, u32[]{:S(2)}, u32[]{:S(2)}) collective-permute-start(bf16[2,8,80,128]{3,2,1,0:T(8,128)(2,1)S(1)} %get-tuple-element.58), channel_id=1, source_target_pairs={{0,192},{32,224},{64,128},{96,160},{128,64},{160,96},{192,0},{224,... | collective-permute-start | bytes 983048 | tf_op jit(solution)/shard_map/ppermute | solution.py:383
  16.4 13.3 %collective-permute-start.1 = (bf16[2,8,80,128]{3,2,1,0:T(8,128)(2,1)S(1)}, bf16[2,8,80,128]{3,2,1,0:T(8,128)(2,1)S(1)}, u32[]{:S(2)}, u32[]{:S(2)}) collective-permute-start(bf16[2,8,80,128]{3,2,1,0:T(8,128)(2,1)S(1)} %get-tuple-element.59), channel_id=1, source_target_pairs={{0,64},{32,96},{64,0},{96,32},{128,192},{160,224},{192,128},{224,1... | collective-permute-start | bytes 983048 | tf_op jit(solution)/shard_map/ppermute | solution.py:383
  22.8 9.7 %collective-permute-start.9 = (bf16[1,8,80,128]{3,2,1,0:T(8,128)(2,1)S(1)}, bf16[1,8,80,128]{3,2,1,0:T(8,128)(2,1)S(1)}, u32[]{:S(2)}, u32[]{:S(2)}) collective-permute-start(bf16[1,8,80,128]{3,2,1,0:T(8,128)(2,1)S(1)} %get-tuple-element.48), channel_id=1, source_target_pairs={{0,64},{32,96},{64,0},{96,32},{128,192},{160,224},{192,128},{224,1... | collective-permute-start | bytes 491528 | tf_op jit(solution)/shard_map/ppermute | solution.py:383
  22.9 10.3 %collective-permute-start.7 = (bf16[1,8,80,128]{3,2,1,0:T(8,128)(2,1)S(1)}, bf16[1,8,80,128]{3,2,1,0:T(8,128)(2,1)S(1)}, u32[]{:S(2)}, u32[]{:S(2)}) collective-permute-start(bf16[1,8,80,128]{3,2,1,0:T(8,128)(2,1)S(1)} %get-tuple-element.49), channel_id=1, source_target_pairs={{0,192},{32,224},{64,128},{96,160},{128,64},{160,96},{192,0},{224,... | collective-permute-start | bytes 491528 | tf_op jit(solution)/shard_map/ppermute | solution.py:383
  29.8 5.7 %collective-permute-start.4 = (bf16[1,8,80,128]{3,2,1,0:T(8,128)(2,1)S(1)}, bf16[1,8,80,128]{3,2,1,0:T(8,128)(2,1)S(1)}, u32[]{:S(2)}, u32[]{:S(2)}) collective-permute-start(bf16[1,8,80,128]{3,2,1,0:T(8,128)(2,1)S(1)} %get-tuple-element.54), channel_id=1, source_target_pairs={{0,64},{32,96},{64,0},{96,32},{128,192},{160,224},{192,128},{224,1... | collective-permute-start | bytes 491528 | tf_op jit(solution)/shard_map/ppermute | solution.py:383
  29.9 5.7 %copy-start = (s32[512]{0:T(512)S(1)}, s32[512]{0:T(512)}, u32[]{:S(2)}) copy-start(s32[512]{0:T(512)} %table_ref.3) | copy-start | bytes 6148
  30.0 5.6 %collective-permute-start.2 = (bf16[1,8,80,128]{3,2,1,0:T(8,128)(2,1)S(1)}, bf16[1,8,80,128]{3,2,1,0:T(8,128)(2,1)S(1)}, u32[]{:S(2)}, u32[]{:S(2)}) collective-permute-start(bf16[1,8,80,128]{3,2,1,0:T(8,128)(2,1)S(1)} %get-tuple-element.55), channel_id=1, source_target_pairs={{0,192},{32,224},{64,128},{96,160},{128,64},{160,96},{192,0},{224,... | collective-permute-start | bytes 491528 | tf_op jit(solution)/shard_map/ppermute | solution.py:383
  37.8 38.8 %all-to-all-start = ((bf16[32,160,128]{2,1,0:T(8,128)(2,1)}), bf16[32,160,128]{2,1,0:T(8,128)(2,1)S(1)}, u32[]{:S(2)}, u32[]{:S(2)}) async-start(bf16[32,160,128]{2,1,0:T(8,128)(2,1)} %get-tuple-element.29), calls=%async_computation | async-start | bytes 2621440 | tf_op jit(solution)/shard_map/all_to_all | solution.py:415
  49.1 8.4 %collective-permute-start.10 = (bf16[2,160,128]{2,1,0:T(8,128)(2,1)S(1)}, bf16[2,160,128]{2,1,0:T(8,128)(2,1)S(1)}, u32[]{:S(2)}, u32[]{:S(2)}) collective-permute-start(bf16[2,160,128]{2,1,0:T(8,128)(2,1)S(1)} %get-tuple-element.31), channel_id=1, source_target_pairs={{0,32},{32,0},{64,96},{96,64},{128,160},{160,128},{192,224},{224,1... | collective-permute-start | bytes 245768 | tf_op jit(solution)/shard_map/ppermute | solution.py:383
  52.5 5.9 %collective-permute-start.11 = (bf16[2,160,128]{2,1,0:T(8,128)(2,1)S(1)}, bf16[2,160,128]{2,1,0:T(8,128)(2,1)S(1)}, u32[]{:S(2)}, u32[]{:S(2)}) collective-permute-start(bf16[2,160,128]{2,1,0:T(8,128)(2,1)S(1)} %get-tuple-element.32), channel_id=1, source_target_pairs={{0,64},{32,96},{64,0},{96,32},{128,192},{160,224},{192,128},{224,1... | collective-permute-start | bytes 245768 | tf_op jit(solution)/shard_map/ppermute | solution.py:383
  52.9 9.6 %collective-permute-start.12 = (bf16[2,160,128]{2,1,0:T(8,128)(2,1)S(1)}, bf16[2,160,128]{2,1,0:T(8,128)(2,1)S(1)}, u32[]{:S(2)}, u32[]{:S(2)}) collective-permute-start(bf16[2,160,128]{2,1,0:T(8,128)(2,1)S(1)} %get-tuple-element.33), channel_id=1, source_target_pairs={{0,96},{32,64},{64,32},{96,0},{128,224},{160,192},{192,160},{224,1... | collective-permute-start | bytes 245768 | tf_op jit(solution)/shard_map/ppermute | solution.py:383
  54.3 8.2 %collective-permute-start.13 = (bf16[2,160,128]{2,1,0:T(8,128)(2,1)S(1)}, bf16[2,160,128]{2,1,0:T(8,128)(2,1)S(1)}, u32[]{:S(2)}, u32[]{:S(2)}) collective-permute-start(bf16[2,160,128]{2,1,0:T(8,128)(2,1)S(1)} %get-tuple-element.34), channel_id=1, source_target_pairs={{0,128},{32,160},{64,192},{96,224},{128,0},{160,32},{192,64},{224,... | collective-permute-start | bytes 245768 | tf_op jit(solution)/shard_map/ppermute | solution.py:383
  55.2 7.6 %collective-permute-start.14 = (bf16[2,160,128]{2,1,0:T(8,128)(2,1)S(1)}, bf16[2,160,128]{2,1,0:T(8,128)(2,1)S(1)}, u32[]{:S(2)}, u32[]{:S(2)}) collective-permute-start(bf16[2,160,128]{2,1,0:T(8,128)(2,1)S(1)} %get-tuple-element.35), channel_id=1, source_target_pairs={{0,160},{32,128},{64,224},{96,192},{128,32},{160,0},{192,96},{224,... | collective-permute-start | bytes 245768 | tf_op jit(solution)/shard_map/ppermute | solution.py:383
  57.5 7.0 %collective-permute-start.15 = (bf16[2,160,128]{2,1,0:T(8,128)(2,1)S(1)}, bf16[2,160,128]{2,1,0:T(8,128)(2,1)S(1)}, u32[]{:S(2)}, u32[]{:S(2)}) collective-permute-start(bf16[2,160,128]{2,1,0:T(8,128)(2,1)S(1)} %get-tuple-element.36), channel_id=1, source_target_pairs={{0,192},{32,224},{64,128},{96,160},{128,64},{160,96},{192,0},{224,... | collective-permute-start | bytes 245768 | tf_op jit(solution)/shard_map/ppermute | solution.py:383
  58.4 8.0 %collective-permute-start.16 = (bf16[2,160,128]{2,1,0:T(8,128)(2,1)S(1)}, bf16[2,160,128]{2,1,0:T(8,128)(2,1)S(1)}, u32[]{:S(2)}, u32[]{:S(2)}) collective-permute-start(bf16[2,160,128]{2,1,0:T(8,128)(2,1)S(1)} %get-tuple-element.37), channel_id=1, source_target_pairs={{0,224},{32,192},{64,160},{96,128},{128,96},{160,64},{192,32},{224... | collective-permute-start | bytes 245768 | tf_op jit(solution)/shard_map/ppermute | solution.py:383
  78.3 41.1 %all-to-all-start.1 = ((bf16[24,160,128]{2,1,0:T(8,128)(2,1)}), bf16[24,160,128]{2,1,0:T(8,128)(2,1)S(1)}, u32[]{:S(2)}, u32[]{:S(2)}) async-start(bf16[24,160,128]{2,1,0:T(8,128)(2,1)} %slot_pick.1), calls=%async_computation.1 | async-start | bytes 1966080 | tf_op jit(solution)/shard_map/all_to_all | solution.py:423
  89.3 5.3 %collective-permute-start.17 = (bf16[2,64,512]{2,1,0:T(8,128)(2,1)S(1)}, bf16[2,64,512]{2,1,0:T(8,128)(2,1)S(1)}, u32[]{:S(2)}, u32[]{:S(2)}) collective-permute-start(bf16[2,64,512]{2,1,0:T(8,128)(2,1)S(1)} %get-tuple-element.41), channel_id=1, source_target_pairs={{0,32},{32,0},{64,96},{96,64},{128,160},{160,128},{192,224},{224,1... | collective-permute-start | bytes 393224 | tf_op jit(solution)/shard_map/ppermute | solution.py:383
  89.5 15.4 %collective-permute-start.18 = (bf16[2,64,512]{2,1,0:T(8,128)(2,1)S(1)}, bf16[2,64,512]{2,1,0:T(8,128)(2,1)S(1)}, u32[]{:S(2)}, u32[]{:S(2)}) collective-permute-start(bf16[2,64,512]{2,1,0:T(8,128)(2,1)S(1)} %get-tuple-element.42), channel_id=1, source_target_pairs={{0,64},{32,96},{64,0},{96,32},{128,192},{160,224},{192,128},{224,1... | collective-permute-start | bytes 393224 | tf_op jit(solution)/shard_map/ppermute | solution.py:383
  91.0 17.5 %collective-permute-start.19 = (bf16[2,64,512]{2,1,0:T(8,128)(2,1)S(1)}, bf16[2,64,512]{2,1,0:T(8,128)(2,1)S(1)}, u32[]{:S(2)}, u32[]{:S(2)}) collective-permute-start(bf16[2,64,512]{2,1,0:T(8,128)(2,1)S(1)} %get-tuple-element.43), channel_id=1, source_target_pairs={{0,96},{32,64},{64,32},{96,0},{128,224},{160,192},{192,160},{224,1... | collective-permute-start | bytes 393224 | tf_op jit(solution)/shard_map/ppermute | solution.py:383
  91.4 20.7 %collective-permute-start.20 = (bf16[2,64,512]{2,1,0:T(8,128)(2,1)S(1)}, bf16[2,64,512]{2,1,0:T(8,128)(2,1)S(1)}, u32[]{:S(2)}, u32[]{:S(2)}) collective-permute-start(bf16[2,64,512]{2,1,0:T(8,128)(2,1)S(1)} %get-tuple-element.44), channel_id=1, source_target_pairs={{0,128},{32,160},{64,192},{96,224},{128,0},{160,32},{192,64},{224,... | collective-permute-start | bytes 393224 | tf_op jit(solution)/shard_map/ppermute | solution.py:383
  94.3 20.9 %collective-permute-start.21 = (bf16[2,64,512]{2,1,0:T(8,128)(2,1)S(1)}, bf16[2,64,512]{2,1,0:T(8,128)(2,1)S(1)}, u32[]{:S(2)}, u32[]{:S(2)}) collective-permute-start(bf16[2,64,512]{2,1,0:T(8,128)(2,1)S(1)} %get-tuple-element.45), channel_id=1, source_target_pairs={{0,160},{32,128},{64,224},{96,192},{128,32},{160,0},{192,96},{224,... | collective-permute-start | bytes 393224 | tf_op jit(solution)/shard_map/ppermute | solution.py:383
  94.6 20.7 %collective-permute-start.22 = (bf16[2,64,512]{2,1,0:T(8,128)(2,1)S(1)}, bf16[2,64,512]{2,1,0:T(8,128)(2,1)S(1)}, u32[]{:S(2)}, u32[]{:S(2)}) collective-permute-start(bf16[2,64,512]{2,1,0:T(8,128)(2,1)S(1)} %get-tuple-element.46), channel_id=1, source_target_pairs={{0,192},{32,224},{64,128},{96,160},{128,64},{160,96},{192,0},{224,... | collective-permute-start | bytes 393224 | tf_op jit(solution)/shard_map/ppermute | solution.py:383
  104.9 12.7 %collective-permute-start.23 = (bf16[2,64,512]{2,1,0:T(8,128)(2,1)S(1)}, bf16[2,64,512]{2,1,0:T(8,128)(2,1)S(1)}, u32[]{:S(2)}, u32[]{:S(2)}) collective-permute-start(bf16[2,64,512]{2,1,0:T(8,128)(2,1)S(1)} %get-tuple-element.47), channel_id=1, source_target_pairs={{0,224},{32,192},{64,160},{96,128},{128,96},{160,64},{192,32},{224... | collective-permute-start | bytes 393224 | tf_op jit(solution)/shard_map/ppermute | solution.py:383
where the time goes:
time: 130 us
  starting transfers between devices  53.2 us (41%)
  waiting for transfers between devices  42.6 us (33%)
  Pallas kernels  30.5 us (23%)
  local copies, waits for them, and re-layouts  2.19 us (2%)
    ppermute x24, waiting for transfers between devices, exchange(): return lax.ppermute(value, 'dp', [(d, d ^ bits) for d in range(data_count)])  38.4 us
    ppermute x24, starting transfers between devices, exchange(): return lax.ppermute(value, 'dp', [(d, d ^ bits) for d in range(data_count)])  30.8 us
    all_to_all x1, starting transfers between devices, program(): lax.all_to_all(outgoing, 'mp', split_axis=0, concat_axis=0, tiled=True)  11.3 us
    all_to_all x1, starting transfers between devices, program(): lax.all_to_all(slots, 'dp', split_axis=0, concat_axis=0, tiled=True)  11 us
    pallas_call x1, Pallas kernels, owner_roots(): pl.pallas_call(functools.partial(owner_kernel, data_count, model_count),...  10.7 us
    pallas_call x2, Pallas kernels, gram_blocks(): pl.pallas_call(functools.partial(gram_kernel, model_count), out_shape=(sh...  6.14 us
    pallas_call x1, Pallas kernels, home_roots(): pl.pallas_call(functools.partial(home_kernel, data_count, model_count), i...  6.01 us
    all_to_all x1, waiting for transfers between devices, program(): lax.all_to_all(outgoing, 'mp', split_axis=0, concat_axis=0, tiled=True)  4.23 us
  transfers between devices with their start and end apart: 26, of which 15 were waited for; matrix products, arithmetic and copies ran while one was open for 1% of the time, Pallas kernels for 10%

commit v1 on v0

--- a/solution.py
+++ b/solution.py
@@ -12,16 +12,15 @@
 BLOCK = 512
 TILE = 128
 DEVICES = 8
-UPPER = [(0, 0), (0, 1), (0, 2), (0, 3), (1, 1), (1, 2), (1, 3), (2, 2), (2, 3), (3, 3)]
-PACKED_ROWS = len(UPPER) * TILE
+ABOVE = [(0, 1), (0, 2), (0, 3), (1, 2), (1, 3), (2, 3)]
+PACKED_ROWS = 9 * TILE
 CHUNK = PACKED_ROWS // DEVICES
-PIECE = CHUNK // 2
+CUTS = (80, 64)
 ROWS = BLOCK // DEVICES
 ORDERS = ((1, 2, 0, 3), (3, 2, 0, 1))
 FIRST_BITS = (2, 6)
 SECOND_BITS = (6, 2)
 VMEM_LIMIT = 24 * 2**20
-GRAM_VMEM_LIMIT = 24 * 2**20
 INTERPRET = False
 F32 = jnp.float32
 BF16 = jnp.bfloat16
@@ -43,8 +42,8 @@
     return pl.BlockSpec(memory_space=memory_space)
 
 
-def params(limit=None):
-    return pltpu.CompilerParams(vmem_limit_bytes=limit or VMEM_LIMIT)
+def params(limit=VMEM_LIMIT):
+    return pltpu.CompilerParams(vmem_limit_bytes=limit)
 
 
 def position(code_ref, model_count):
@@ -55,53 +54,67 @@
     return pl.CostEstimate(flops=int(flops), bytes_accessed=int(moved), transcendentals=0)
 
 
-def gram_kernel(model_count, code_ref, block_ref, own_ref, away_ref, stack_ref):
-    block = block_ref[0]
+def gram_step(code_ref, model_count, cut, block, own_ref, away_ref, stack_ref):
     half = BLOCK // 2
     device, _ = position(code_ref, model_count)
     core = device & 1
     along = device >> 1
+    row_ids, column_ids = iota((TILE, TILE), 0), iota((TILE, TILE), 1)
+    last_row = row_ids == TILE - 1
     for side in range(2):
         dims = ((1,), (1,)) if side == 0 else ((0,), (0,))
         low = block[:half] if side == 0 else block[:, :half]
         high = block[half:] if side == 0 else block[:, half:]
-        right = dot(block, high, dims).astype(BF16)
-        corner = dot(low, low, dims).astype(BF16)
-        for index, (row, column) in enumerate(UPPER):
+        right = dot(block, high, dims)
+        corner = dot(low, low, dims)
+
+        def tile(row, column):
             if column >= 2:
-                piece = right[rows_of(row), rows_of(column - 2)]
-            else:
-                piece = corner[rows_of(row), rows_of(column)]
-            stack_ref[rows_of(index)] = piece
+                return right[rows_of(row), rows_of(column - 2)]
+            return corner[rows_of(row), rows_of(column)]
+
+        tiles = [tile(row, column) for row, column in ABOVE]
+        inner = tile(1, 1)
+        diagonal = jnp.sum(jnp.where(row_ids == column_ids, inner, 0.0), axis=0, keepdims=True)
+        corner_end = inner[TILE - 1 :, TILE - 1 :]
+        tiles.append(jnp.where(column_ids >= row_ids, tile(0, 0), inner))
+        tiles.append(jnp.where(last_row & (column_ids < TILE - 1), diagonal, tile(2, 2)))
+        tiles.append(jnp.where(last_row & (column_ids == 0), corner_end, tile(3, 3)))
+        for index, value in enumerate(tiles):
+            stack_ref[rows_of(index)] = value.astype(BF16)
         for chip in range(4):
             offset = chip ^ along
-            for part in range(2):
+            for part, (start, stop) in enumerate(((0, cut), (cut, CHUNK))):
                 place = jnp.int32(0)
                 for spot, value in enumerate(ORDERS[part]):
                     place = jnp.where(offset == value, spot, place)
-                even = stack_ref[pl.ds((4 * chip + part) * PIECE, PIECE)]
-                odd = stack_ref[pl.ds((4 * chip + 2 + part) * PIECE, PIECE)]
-                own_ref[part, place, side] = jnp.where(core == 0, even, odd)
-                away_ref[part, place, side] = jnp.where(core == 0, odd, even)
-
-
-def gram_blocks(blocks, code, model_count, first, count):
-    shape = jax.ShapeDtypeStruct((2, 4, 2 * count, PIECE, TILE), BF16)
-    out_spec = pl.BlockSpec((2, 4, 2, PIECE, TILE), lambda step, code_ref: (0, 0, step, 0, 0))
-    return pl.pallas_call(
-        functools.partial(gram_kernel, model_count),
+                base = 2 * chip * CHUNK
+                even = stack_ref[base + start : base + stop]
+                odd = stack_ref[base + CHUNK + start : base + CHUNK + stop]
+                own_ref[place, side, start:stop] = jnp.where(core == 0, even, odd)
+                away_ref[place, side, start:stop] = jnp.where(core == 0, odd, even)
+
+
+def gram_kernel(model_count, cut, code_ref, block_ref, own_ref, away_ref, stack_ref):
+    gram_step(code_ref, model_count, cut, block_ref[0], own_ref, away_ref, stack_ref)
+
+
+def gram_blocks(blocks, code, model_count, first, count, cut):
+    shape = jax.ShapeDtypeStruct((4, 2 * count, CHUNK, TILE), BF16)
+    out_spec = pl.BlockSpec((4, 2, CHUNK, TILE), lambda step, code_ref: (0, step, 0, 0))
+    in_spec = pl.BlockSpec((1, BLOCK, BLOCK), lambda step, code_ref: (first + step, 0, 0))
+    return pl.pallas_call(
+        functools.partial(gram_kernel, model_count, cut),
         out_shape=(shape, shape),
         grid_spec=pltpu.PrefetchScalarGridSpec(
             num_scalar_prefetch=1,
             grid=(count,),
-            in_specs=[
-                pl.BlockSpec((1, BLOCK, BLOCK), lambda step, code_ref: (first + step, 0, 0))
-            ],
+            in_specs=[in_spec],
             out_specs=[out_spec, out_spec],
             scratch_shapes=[pltpu.VMEM((PACKED_ROWS, TILE), BF16)],
         ),
         interpret=INTERPRET,
-        compiler_params=params(GRAM_VMEM_LIMIT),
+        compiler_params=params(),
         cost_estimate=cost(3 * count * BLOCK**3, count * 5 * 2**18),
     )(code, blocks)
 
@@ -146,13 +159,11 @@
     device, model = position(code_ref, model_count)
     count = sources[0].shape[0]
     per_slab = 2 * count
-    for group in range(2):
-        for part in range(2):
+    for group, cut in enumerate(CUTS):
+        for part, (start, stop) in enumerate(((0, cut), (cut, CHUNK))):
             partial_ref, last_ref = sources[4 * group + 2 * part : 4 * group + 2 * part + 2]
             value = partial_ref[...] + last_ref[0].astype(F32)
-            mine_ref[group * count : (group + 1) * count, part * PIECE : (part + 1) * PIECE] = (
-                value.astype(BF16)
-            )
+            mine_ref[group * count : (group + 1) * count, start:stop] = value.astype(BF16)
     for owner in range(model_count):
         send_ref[owner] = 0
     for stat in range(per_slab):
@@ -226,18 +237,26 @@
     return jnp.sum(jnp.sum(value, axis=0, keepdims=True), axis=1, keepdims=True)
 
 
-def root_of(chunk_piece, data_count, stat_ref, pair_ref):
-    for index, (row, column) in enumerate(UPPER):
-        start, stop = index * TILE, (index + 1) * TILE
-        while start < stop:
-            chunk = start // CHUNK
-            end = min(stop, (chunk + 1) * CHUNK)
-            piece = chunk_piece(chunk, start - chunk * CHUNK, end - chunk * CHUNK)
-            base = row * TILE + start - index * TILE
-            stat_ref[base : base + end - start, rows_of(column)] = piece
-            start = end
-        if row != column:
-            stat_ref[rows_of(column), rows_of(row)] = stat_ref[rows_of(row), rows_of(column)].T
+def unpack(stack_ref, stat_ref):
+    row_ids, column_ids = iota((TILE, TILE), 0), iota((TILE, TILE), 1)
+    last_row = row_ids == TILE - 1
+    for index, (row, column) in enumerate(ABOVE):
+        value = stack_ref[rows_of(index)]
+        stat_ref[rows_of(row), rows_of(column)] = value
+        stat_ref[rows_of(column), rows_of(row)] = value.T
+    shared, third, fourth = [stack_ref[rows_of(index)] for index in (6, 7, 8)]
+    mirrored = shared.T
+    diagonal = jnp.where(column_ids == TILE - 1, fourth[TILE - 1 :, :1], third[TILE - 1 :])
+    stat_ref[rows_of(0), rows_of(0)] = jnp.where(column_ids >= row_ids, shared, mirrored)
+    stat_ref[rows_of(1), rows_of(1)] = jnp.where(
+        row_ids == column_ids, diagonal, jnp.where(column_ids < row_ids, shared, mirrored)
+    )
+    stat_ref[rows_of(2), rows_of(2)] = jnp.where(last_row, third.T, third)
+    stat_ref[rows_of(3), rows_of(3)] = jnp.where(last_row, fourth.T, fourth)
+
+
+def root_of(data_count, stack_ref, stat_ref, pair_ref):
+    unpack(stack_ref, stat_ref)
     on_diagonal = iota((BLOCK, BLOCK), 0) == iota((BLOCK, BLOCK), 1)
     statistic = stat_ref[...] * (1.0 / data_count)
     diagonal_mean = total(jnp.where(on_diagonal, statistic, 0.0)) * (1.0 / BLOCK)
@@ -271,10 +290,9 @@
     spare = (row_ids % ROWS == 1) & (iota((BLOCK, BLOCK), 1) == row_ids - 1)
     for stat in range(2):
         for bits, ref in enumerate(sources):
-            stack_ref[device ^ bits] = ref[stat].astype(F32)
-        rest, identity_part, on_diagonal = root_of(
-            lambda chunk, start, stop: stack_ref[chunk, start:stop], data_count, stat_ref, pair_ref
-        )
+            start = pl.multiple_of((device ^ bits) * CHUNK, 16)
+            stack_ref[pl.ds(start, CHUNK)] = ref[stat].astype(F32)
+        rest, identity_part, on_diagonal = root_of(data_count, stack_ref, stat_ref, pair_ref)
         rest_mean = total(jnp.where(on_diagonal, rest, 0.0)) * (1.0 / BLOCK)
         center = (identity_part + rest_mean).astype(BF16).astype(F32)
         rest = rest + jnp.where(on_diagonal, identity_part - center, 0.0)
@@ -293,7 +311,7 @@
         out_shape=[jax.ShapeDtypeStruct((2, ROWS, BLOCK), BF16)] * DEVICES,
         scratch_shapes=[
             pltpu.VMEM((DEVICES, ROWS, BLOCK), BF16),
-            pltpu.VMEM((DEVICES, CHUNK, TILE), F32),
+            pltpu.VMEM((PACKED_ROWS, TILE), F32),
             pltpu.VMEM((BLOCK, BLOCK), F32),
             pltpu.VMEM((2 * BLOCK, BLOCK), BF16),
         ],
@@ -304,19 +322,18 @@
     )(code, *sources)
 
 
-def owner_kernel(data_count, model_count, code_ref, plan_ref, source_ref, out_ref, stat_ref, pair_ref):
+def owner_kernel(
+    data_count, model_count, code_ref, plan_ref, source_ref, out_ref, stack_ref, stat_ref, pair_ref
+):
     device, _ = position(code_ref, model_count)
     slot = pl.program_id(0)
     keep = pl.num_programs(0) * device + slot < plan_ref[CAP]
 
     @pl.when(keep)
     def _():
-        rest, identity_part, on_diagonal = root_of(
-            lambda chunk, start, stop: source_ref[chunk, 0, start:stop].astype(F32),
-            data_count,
-            stat_ref,
-            pair_ref,
-        )
+        for chunk in range(DEVICES):
+            stack_ref[chunk * CHUNK : (chunk + 1) * CHUNK] = source_ref[chunk, 0].astype(F32)
+        rest, identity_part, on_diagonal = root_of(data_count, stack_ref, stat_ref, pair_ref)
         out_ref[0] = rest + jnp.where(on_diagonal, identity_part, 0.0)
 
     @pl.when(jnp.logical_not(keep))
@@ -337,6 +354,7 @@
         out_specs=pl.BlockSpec((1, BLOCK, BLOCK), lambda slot: (slot, 0, 0)),
         out_shape=jax.ShapeDtypeStruct((slots, BLOCK, BLOCK), F32),
         scratch_shapes=[
+            pltpu.VMEM((PACKED_ROWS, TILE), F32),
             pltpu.VMEM((BLOCK, BLOCK), F32),
             pltpu.VMEM((2 * BLOCK, BLOCK), BF16),
         ],
@@ -397,18 +415,21 @@
     code = (lax.axis_index("dp") * model_count + lax.axis_index("mp")).reshape(1)
 
     sources = []
-    for group in range(2):
-        own, away = gram_blocks(blocks, code, model_count, group * row_blocks // 2, row_blocks // 2)
+    half = row_blocks // 2
+    gram_code = code
+    for group, cut in enumerate(CUTS):
+        own, away = gram_blocks(blocks, gram_code, model_count, group * half, half, cut)
+        if group == 0:
+            gram_code, away = lax.optimization_barrier((gram_code, away))
         got = exchange(away, 1, data_count)
-        for part in range(2):
-            first = own[part, :2].astype(F32) + got[part, :2].astype(F32)
+        for part, rows in enumerate((slice(0, cut), slice(cut, CHUNK))):
+            first = own[:2, :, rows].astype(F32) + got[:2, :, rows].astype(F32)
             step = exchange(first.astype(BF16), FIRST_BITS[part], data_count)
-            second = own[part, 3:].astype(F32) + got[part, 3:].astype(F32) + step[1:].astype(F32)
+            second = own[3:, :, rows].astype(F32) + got[3:, :, rows].astype(F32)
+            second = second + step[1:].astype(F32)
             last = exchange(second.astype(BF16), SECOND_BITS[part], data_count)
-            sources.append(
-                own[part, 2].astype(F32) + got[part, 2].astype(F32) + step[0].astype(F32)
-            )
-            sources.append(last)
+            third = own[2, :, rows].astype(F32) + got[2, :, rows].astype(F32)
+            sources += [third + step[0].astype(F32), last]
 
     plan = make_plan(code, owner_table, model_count)
     outgoing, *home = sum_and_send(code, owner_table, sources, model_count)

time: 130 us -> 126 us (0.969)
  waiting for transfers between devices: 42.6 us -> 36.7 us
    ppermute x24, waiting for transfers between devices: 38.4 us -> 33.2 us  [exchange(): return lax.ppermute(value, 'dp', [(d, d ^ bits) for d in range(data_count)])]
  transfers between devices with their start and end apart: 26 -> 26, of which waited for: 15 -> 14; matrix products, arithmetic and copies ran while one was open for 1% -> 1% of each run, Pallas kernels for 10% -> 11%
where the time goes in v1:
time: 126 us; the launch traced here: 125 us
  starting transfers between devices  53.4 us (42%)
  waiting for transfers between devices  36.7 us (29%)
  Pallas kernels  31.3 us (25%)
  local copies, waits for them, and re-layouts  2.19 us (2%)
    ppermute x24, waiting for transfers between devices, exchange(): return lax.ppermute(value, 'dp', [(d, d ^ bits) for d in range(data_count)])  33.2 us
    ppermute x24, starting transfers between devices, exchange(): return lax.ppermute(value, 'dp', [(d, d ^ bits) for d in range(data_count)])  32 us
    all_to_all x1, starting transfers between devices, program(): lax.all_to_all(outgoing, 'mp', split_axis=0, concat_axis=0, tiled=True)  11.4 us
    pallas_call x1, Pallas kernels, owner_roots(): pl.pallas_call(functools.partial(owner_kernel, data_count, model_count),...  10.8 us
    all_to_all x1, starting transfers between devices, program(): lax.all_to_all(slots, 'dp', split_axis=0, concat_axis=0, tiled=True)  9.96 us
    pallas_call x2, Pallas kernels, gram_blocks(): pl.pallas_call(functools.partial(gram_kernel, model_count, cut), out_shap...  6.87 us
    pallas_call x1, Pallas kernels, home_roots(): pl.pallas_call(functools.partial(home_kernel, data_count, model_count), i...  6.15 us
    all_to_all x1, waiting for transfers between devices, program(): lax.all_to_all(outgoing, 'mp', split_axis=0, concat_axis=0, tiled=True)  3.47 us
  transfers between devices with their start and end apart: 26, of which 14 were waited for; matrix products, arithmetic and copies ran while one was open for 1% of the time, Pallas kernels for 11%

profile of v1, /device:TPU:1, one launch (start us, length us, event | category | flops | bytes accessed | tf_op | source)
XLA Modules:
  0.0 125.3 jit_solution(10199886703929688096)
XLA Ops:
  0.6 2.2 %copy-done.1 = bf16[1,4096,512]{2,1,0:T(8,128)(2,1)S(1)} copy-done((bf16[1,4096,512]{2,1,0:T(8,128)(2,1)S(1)}, bf16[1,4096,512]{2,1,0:T(8,128)(2,1)}, u32[]{:S(2)}) %copy-start.1) | copy-done | bytes 4194328
  2.8 3.4 %shard_map.41 = (bf16[4,8,144,128]{3,2,1,0:T(8,128)(2,1)S(1)}, bf16[4,8,144,128]{3,2,1,0:T(8,128)(2,1)S(1)}) custom-call(s32[1]{0:T(128)} %bitcast.code_ref, bf16[8,512,512]{2,1,0:T(8,128)(2,1)S(1)} %bitcast.13), custom_call_target="tpu_custom_call" | custom-call | flops 1610612736 | bytes 5242880 | tf_op jit(solution)/shard_map/pallas_call | solution.py:106
  6.3 3.3 %collective-permute-start = (bf16[4,8,144,128]{3,2,1,0:T(8,128)(2,1)S(1)}, bf16[4,8,144,128]{3,2,1,0:T(8,128)(2,1)S(1)}, u32[]{:S(2)}, u32[]{:S(2)}) collective-permute-start(bf16[4,8,144,128]{3,2,1,0:T(8,128)(2,1)S(1)} %get-tuple-element.29), channel_id=1, source_target_pairs={{0,32},{32,0},{64,96},{96,64},{128,160},{160,128},{192,224},{224,1... | collective-permute-start | bytes 3538952 | tf_op jit(solution)/shard_map/ppermute | solution.py:401
  9.6 3.4 %shard_map.42 = (bf16[4,8,144,128]{3,2,1,0:T(8,128)(2,1)S(1)}, bf16[4,8,144,128]{3,2,1,0:T(8,128)(2,1)S(1)}) custom-call(s32[1]{0:T(128)} %bitcast.code_ref, bf16[8,512,512]{2,1,0:T(8,128)(2,1)S(1)} %bitcast.14), custom_call_target="tpu_custom_call" | custom-call | flops 1610612736 | bytes 5242880 | tf_op jit(solution)/shard_map/pallas_call | solution.py:106
  14.3 1.7 %collective-permute-done.5 = bf16[4,8,144,128]{3,2,1,0:T(8,128)(2,1)S(1)} collective-permute-done((bf16[4,8,144,128]{3,2,1,0:T(8,128)(2,1)S(1)}, bf16[4,8,144,128]{3,2,1,0:T(8,128)(2,1)S(1)}, u32[]{:S(2)}, u32[]{:S(2)}) %collective-permute-start.5) | collective-permute-done | bytes 1179680 | tf_op jit(solution)/shard_map/ppermute | solution.py:401
  16.2 1.8 %collective-permute-start.8 = (bf16[2,8,80,128]{3,2,1,0:T(8,128)(2,1)S(1)}, bf16[2,8,80,128]{3,2,1,0:T(8,128)(2,1)S(1)}, u32[]{:S(2)}, u32[]{:S(2)}) collective-permute-start(bf16[2,8,80,128]{3,2,1,0:T(8,128)(2,1)S(1)} %add_convert_fusion), channel_id=1, source_target_pairs={{0,192},{32,224},{64,128},{96,160},{128,64},{160,96},{192,0},{224,... | collective-permute-start | bytes 983048 | tf_op jit(solution)/shard_map/ppermute | solution.py:401
  18.0 3.9 %collective-permute-done.3 = bf16[2,8,64,128]{3,2,1,0:T(8,128)(2,1)S(1)} collective-permute-done((bf16[2,8,64,128]{3,2,1,0:T(8,128)(2,1)S(1)}, bf16[2,8,64,128]{3,2,1,0:T(8,128)(2,1)S(1)}, u32[]{:S(2)}, u32[]{:S(2)}) %collective-permute-start.3) | collective-permute-done | bytes 262176 | tf_op jit(solution)/shard_map/ppermute | solution.py:401
  22.9 2.0 %collective-permute-start.2 = (bf16[1,8,80,128]{3,2,1,0:T(8,128)(2,1)S(1)}, bf16[1,8,80,128]{3,2,1,0:T(8,128)(2,1)S(1)}, u32[]{:S(2)}, u32[]{:S(2)}) collective-permute-start(bf16[1,8,80,128]{3,2,1,0:T(8,128)(2,1)S(1)} %get-tuple-element.54), channel_id=1, source_target_pairs={{0,192},{32,224},{64,128},{96,160},{128,64},{160,96},{192,0},{224,... | collective-permute-start | bytes 491528 | tf_op jit(solution)/shard_map/ppermute | solution.py:401
  24.9 4.0 %collective-permute-done.8 = bf16[2,8,80,128]{3,2,1,0:T(8,128)(2,1)S(1)} collective-permute-done((bf16[2,8,80,128]{3,2,1,0:T(8,128)(2,1)S(1)}, bf16[2,8,80,128]{3,2,1,0:T(8,128)(2,1)S(1)}, u32[]{:S(2)}, u32[]{:S(2)}) %collective-permute-start.8) | collective-permute-done | bytes 327712 | tf_op jit(solution)/shard_map/ppermute | solution.py:401
  31.2 3.3 %collective-permute-done.7.refs_5_ = bf16[1,8,64,128]{3,2,1,0:T(8,128)(2,1)S(1)} collective-permute-done((bf16[1,8,64,128]{3,2,1,0:T(8,128)(2,1)S(1)}, bf16[1,8,64,128]{3,2,1,0:T(8,128)(2,1)S(1)}, u32[]{:S(2)}, u32[]{:S(2)}) %collective-permute-start.7) | collective-permute-done | bytes 131104 | tf_op jit(solution)/shard_map/ppermute | solution.py:401
  34.5 2.1 %sum_and_send.1 = (bf16[32,144,128]{2,1,0:T(8,128)(2,1)}, bf16[2,144,128]{2,1,0:T(8,128)(2,1)S(1)}, bf16[2,144,128]{2,1,0:T(8,128)(2,1)S(1)}, bf16[2,144,128]{2,...) custom-call(s32[1]{0:T(128)} %bitcast.code_ref, ...), custom_call_target="tpu_custom_call" | custom-call | flops 2097152 | bytes 4194304 | tf_op jit(solution)/shard_map/sum_and_send/pallas_call | solution.py:192
  36.6 11.4 %all-to-all-start = ((bf16[32,144,128]{2,1,0:T(8,128)(2,1)}), bf16[32,144,128]{2,1,0:T(8,128)(2,1)S(1)}, u32[]{:S(2)}, u32[]{:S(2)}) async-start(bf16[32,144,128]{2,1,0:T(8,128)(2,1)} %get-tuple-element.33), calls=%async_computation | async-start | bytes 2359296 | tf_op jit(solution)/shard_map/all_to_all | solution.py:436
  48.0 3.3 %collective-permute-start.10 = (bf16[2,144,128]{2,1,0:T(8,128)(2,1)S(1)}, bf16[2,144,128]{2,1,0:T(8,128)(2,1)S(1)}, u32[]{:S(2)}, u32[]{:S(2)}) collective-permute-start(bf16[2,144,128]{2,1,0:T(8,128)(2,1)S(1)} %get-tuple-element.35), channel_id=1, source_target_pairs={{0,32},{32,0},{64,96},{96,64},{128,160},{160,128},{192,224},{224,1... | collective-permute-start | bytes 221192 | tf_op jit(solution)/shard_map/ppermute | solution.py:401
  51.3 1.7 %collective-permute-start.12 = (bf16[2,144,128]{2,1,0:T(8,128)(2,1)S(1)}, bf16[2,144,128]{2,1,0:T(8,128)(2,1)S(1)}, u32[]{:S(2)}, u32[]{:S(2)}) collective-permute-start(bf16[2,144,128]{2,1,0:T(8,128)(2,1)S(1)} %get-tuple-element.37), channel_id=1, source_target_pairs={{0,96},{32,64},{64,32},{96,0},{128,224},{160,192},{192,160},{224,1... | collective-permute-start | bytes 221192 | tf_op jit(solution)/shard_map/ppermute | solution.py:401
  54.2 2.0 %collective-permute-start.14 = (bf16[2,144,128]{2,1,0:T(8,128)(2,1)S(1)}, bf16[2,144,128]{2,1,0:T(8,128)(2,1)S(1)}, u32[]{:S(2)}, u32[]{:S(2)}) collective-permute-start(bf16[2,144,128]{2,1,0:T(8,128)(2,1)S(1)} %get-tuple-element.39), channel_id=1, source_target_pairs={{0,160},{32,128},{64,224},{96,192},{128,32},{160,0},{192,96},{224,... | collective-permute-start | bytes 221192 | tf_op jit(solution)/shard_map/ppermute | solution.py:401
  57.3 1.9 %collective-permute-start.16 = (bf16[2,144,128]{2,1,0:T(8,128)(2,1)S(1)}, bf16[2,144,128]{2,1,0:T(8,128)(2,1)S(1)}, u32[]{:S(2)}, u32[]{:S(2)}) collective-permute-start(bf16[2,144,128]{2,1,0:T(8,128)(2,1)S(1)} %get-tuple-element.41), channel_id=1, source_target_pairs={{0,224},{32,192},{64,160},{96,128},{128,96},{160,64},{192,32},{224... | collective-permute-start | bytes 221192 | tf_op jit(solution)/shard_map/ppermute | solution.py:401
  59.2 2.0 %make_plan.1.plan_ref = s32[25]{0:T(128)S(1)} custom-call(s32[1]{0:T(128)} %bitcast.code_ref, s32[512]{0:T(512)S(1)} %copy-done), custom_call_target="tpu_custom_call" | custom-call | flops 4194304 | bytes 4096 | tf_op jit(solution)/shard_map/make_plan/pallas_call | solution.py:143
  62.5 1.6 %collective-permute-done.16.refs_7_ = bf16[2,144,128]{2,1,0:T(8,128)(2,1)S(1)} collective-permute-done((bf16[2,144,128]{2,1,0:T(8,128)(2,1)S(1)}, bf16[2,144,128]{2,1,0:T(8,128)(2,1)S(1)}, u32[]{:S(2)}, u32[]{:S(2)}) %collective-permute-start.16) | collective-permute-done | bytes 73760 | tf_op jit(solution)/shard_map/ppermute | solution.py:401
  64.2 6.2 %home_roots.1 = (bf16[2,64,512]{2,1,0:T(8,128)(2,1)S(1)}, bf16[2,64,512]{2,1,0:T(8,128)(2,1)S(1)}, bf16[2,64,512]{2,1,0:T(8,128)(2,1)S(1)}, bf16[2,64,512]{2,1,0...) custom-call(s32[1]{0:T(128)} %bitcast.code_ref, ...), custom_call_target="tpu_custom_call" | custom-call | flops 4294967296 | bytes 4194304 | tf_op jit(solution)/shard_map/home_roots/pallas_call | solution.py:307
  70.3 3.5 %all-to-all-done.source_ref = bf16[32,144,128]{2,1,0:T(8,128)(2,1)S(1)} async-done(((bf16[32,144,128]{2,1,0:T(8,128)(2,1)}), bf16[32,144,128]{2,1,0:T(8,128)(2,1)S(1)}, u32[]{:S(2)}, u32[]{:S(2)}) %all-to-all-start) | async-done | bytes 1179680 | tf_op jit(solution)/shard_map/all_to_all | solution.py:436
  73.8 1.7 %slot_pick.1 = bf16[24,144,128]{2,1,0:T(8,128)(2,1)} custom-call(s32[25]{0:T(128)S(1)} %make_plan.1.plan_ref, bf16[32,144,128]{2,1,0:T(8,128)(2,1)S(1)} %all-to-all-done.source_ref), custom_call_target="tpu_custom_call" | custom-call | flops 2097152 | bytes 4194304 | tf_op jit(solution)/shard_map/slot_pick/pallas_call | solution.py:223
  75.5 10.0 %all-to-all-start.1 = ((bf16[24,144,128]{2,1,0:T(8,128)(2,1)}), bf16[24,144,128]{2,1,0:T(8,128)(2,1)S(1)}, u32[]{:S(2)}, u32[]{:S(2)}) async-start(bf16[24,144,128]{2,1,0:T(8,128)(2,1)} %slot_pick.1), calls=%async_computation.1 | async-start | bytes 1769472 | tf_op jit(solution)/shard_map/all_to_all | solution.py:444
  85.6 1.6 %collective-permute-start.18 = (bf16[2,64,512]{2,1,0:T(8,128)(2,1)S(1)}, bf16[2,64,512]{2,1,0:T(8,128)(2,1)S(1)}, u32[]{:S(2)}, u32[]{:S(2)}) collective-permute-start(bf16[2,64,512]{2,1,0:T(8,128)(2,1)S(1)} %get-tuple-element.46), channel_id=1, source_target_pairs={{0,64},{32,96},{64,0},{96,32},{128,192},{160,224},{192,128},{224,1... | collective-permute-start | bytes 393224 | tf_op jit(solution)/shard_map/ppermute | solution.py:401
  87.6 2.9 %collective-permute-start.20 = (bf16[2,64,512]{2,1,0:T(8,128)(2,1)S(1)}, bf16[2,64,512]{2,1,0:T(8,128)(2,1)S(1)}, u32[]{:S(2)}, u32[]{:S(2)}) collective-permute-start(bf16[2,64,512]{2,1,0:T(8,128)(2,1)S(1)} %get-tuple-element.48), channel_id=1, source_target_pairs={{0,128},{32,160},{64,192},{96,224},{128,0},{160,32},{192,64},{224,... | collective-permute-start | bytes 393224 | tf_op jit(solution)/shard_map/ppermute | solution.py:401
  90.7 2.7 %collective-permute-start.22 = (bf16[2,64,512]{2,1,0:T(8,128)(2,1)S(1)}, bf16[2,64,512]{2,1,0:T(8,128)(2,1)S(1)}, u32[]{:S(2)}, u32[]{:S(2)}) collective-permute-start(bf16[2,64,512]{2,1,0:T(8,128)(2,1)S(1)} %get-tuple-element.50), channel_id=1, source_target_pairs={{0,192},{32,224},{64,128},{96,160},{128,64},{160,96},{192,0},{224,... | collective-permute-start | bytes 393224 | tf_op jit(solution)/shard_map/ppermute | solution.py:401
  93.4 6.6 %collective-permute-done.18.refs_2_ = bf16[2,64,512]{2,1,0:T(8,128)(2,1)S(1)} collective-permute-done((bf16[2,64,512]{2,1,0:T(8,128)(2,1)S(1)}, bf16[2,64,512]{2,1,0:T(8,128)(2,1)S(1)}, u32[]{:S(2)}, u32[]{:S(2)}) %collective-permute-start.18) | collective-permute-done | bytes 131104 | tf_op jit(solution)/shard_map/ppermute | solution.py:401
  100.0 3.2 %collective-permute-start.23 = (bf16[2,64,512]{2,1,0:T(8,128)(2,1)S(1)}, bf16[2,64,512]{2,1,0:T(8,128)(2,1)S(1)}, u32[]{:S(2)}, u32[]{:S(2)}) collective-permute-start(bf16[2,64,512]{2,1,0:T(8,128)(2,1)S(1)} %get-tuple-element.51), channel_id=1, source_target_pairs={{0,224},{32,192},{64,160},{96,128},{128,96},{160,64},{192,32},{224... | collective-permute-start | bytes 393224 | tf_op jit(solution)/shard_map/ppermute | solution.py:401
  103.7 3.5 %collective-permute-done.20.refs_4_ = bf16[2,64,512]{2,1,0:T(8,128)(2,1)S(1)} collective-permute-done((bf16[2,64,512]{2,1,0:T(8,128)(2,1)S(1)}, bf16[2,64,512]{2,1,0:T(8,128)(2,1)S(1)}, u32[]{:S(2)}, u32[]{:S(2)}) %collective-permute-start.20) | collective-permute-done | bytes 131104 | tf_op jit(solution)/shard_map/ppermute | solution.py:401
  107.2 3.1 %collective-permute-done.21.refs_5_ = bf16[2,64,512]{2,1,0:T(8,128)(2,1)S(1)} collective-permute-done((bf16[2,64,512]{2,1,0:T(8,128)(2,1)S(1)}, bf16[2,64,512]{2,1,0:T(8,128)(2,1)S(1)}, u32[]{:S(2)}, u32[]{:S(2)}) %collective-permute-start.21) | collective-permute-done | bytes 131104 | tf_op jit(solution)/shard_map/ppermute | solution.py:401
  110.3 2.4 %collective-permute-done.23.refs_7_ = bf16[2,64,512]{2,1,0:T(8,128)(2,1)S(1)} collective-permute-done((bf16[2,64,512]{2,1,0:T(8,128)(2,1)S(1)}, bf16[2,64,512]{2,1,0:T(8,128)(2,1)S(1)}, u32[]{:S(2)}, u32[]{:S(2)}) %collective-permute-start.23) | collective-permute-done | bytes 131104 | tf_op jit(solution)/shard_map/ppermute | solution.py:401
  112.7 1.7 %finish_rows.1 = f32[16,64,512]{2,1,0:T(8,128)} custom-call(s32[1]{0:T(128)} %bitcast.code_ref, bf16[2,64,512]{2,1,0:T(8,128)(2,1)S(1)} %get-tuple-element.44.refs_0_, bf16[2,64,512]{2,1,0:T(8,128)(2,1)S(1)} %collective-permute-done.17.refs_1_, bf16[2,64,512]{2,1,0:T(8,128)(2,1)S(1)} %collective-permute-done.18.refs_2_, ...), custom_call_target="tpu_custom_call" | custom-call | flops 2097152 | bytes 4194304 | tf_op jit(solution)/shard_map/finish_rows/pallas_call | solution.py:388
  114.4 10.8 %owner_roots.1 = f32[3,512,512]{2,1,0:T(8,128)} custom-call(s32[1]{0:T(128)} %bitcast.code_ref, s32[25]{0:T(128)S(1)} %make_plan.1.plan_ref, bf16[8,3,144,128]{3,2,1,0:T(8,128)(2,1)S(1)} %bitcast.12), custom_call_target="tpu_custom_call" | custom-call | flops 6442450944 | bytes 4194304 | tf_op jit(solution)/shard_map/owner_roots/pallas_call | solution.py:346
  (40 shorter events, 9.6 us)
Async XLA Ops:
  0.6 2.2 %copy-start.1 = (bf16[1,4096,512]{2,1,0:T(8,128)(2,1)S(1)}, bf16[1,4096,512]{2,1,0:T(8,128)(2,1)}, u32[]{:S(2)}) copy-start(bf16[1,4096,512]{2,1,0:T(8,128)(2,1)} %param.2) | copy-start | bytes 12582916
  6.3 6.9 %collective-permute-start = (bf16[4,8,144,128]{3,2,1,0:T(8,128)(2,1)S(1)}, bf16[4,8,144,128]{3,2,1,0:T(8,128)(2,1)S(1)}, u32[]{:S(2)}, u32[]{:S(2)}) collective-permute-start(bf16[4,8,144,128]{3,2,1,0:T(8,128)(2,1)S(1)} %get-tuple-element.29), channel_id=1, source_target_pairs={{0,32},{32,0},{64,96},{96,64},{128,160},{160,128},{192,224},{224,1... | collective-permute-start | bytes 3538952 | tf_op jit(solution)/shard_map/ppermute | solution.py:401
  13.0 2.9 %collective-permute-start.5 = (bf16[4,8,144,128]{3,2,1,0:T(8,128)(2,1)S(1)}, bf16[4,8,144,128]{3,2,1,0:T(8,128)(2,1)S(1)}, u32[]{:S(2)}, u32[]{:S(2)}) collective-permute-start(bf16[4,8,144,128]{3,2,1,0:T(8,128)(2,1)S(1)} %get-tuple-element.32), channel_id=1, source_target_pairs={{0,32},{32,0},{64,96},{96,64},{128,160},{160,128},{192,224},{224,1... | collective-permute-start | bytes 3538952 | tf_op jit(solution)/shard_map/ppermute | solution.py:401
  13.2 8.7 %collective-permute-start.3 = (bf16[2,8,64,128]{3,2,1,0:T(8,128)(2,1)S(1)}, bf16[2,8,64,128]{3,2,1,0:T(8,128)(2,1)S(1)}, u32[]{:S(2)}, u32[]{:S(2)}) collective-permute-start(bf16[2,8,64,128]{3,2,1,0:T(8,128)(2,1)S(1)} %add_convert_fusion.3), channel_id=1, source_target_pairs={{0,192},{32,224},{64,128},{96,160},{128,64},{160,96},{192,0},{224,... | collective-permute-start | bytes 786440 | tf_op jit(solution)/shard_map/ppermute | solution.py:401
  14.2 8.6 %collective-permute-start.1 = (bf16[2,8,80,128]{3,2,1,0:T(8,128)(2,1)S(1)}, bf16[2,8,80,128]{3,2,1,0:T(8,128)(2,1)S(1)}, u32[]{:S(2)}, u32[]{:S(2)}) collective-permute-start(bf16[2,8,80,128]{3,2,1,0:T(8,128)(2,1)S(1)} %add_convert_fusion.1), channel_id=1, source_target_pairs={{0,64},{32,96},{64,0},{96,32},{128,192},{160,224},{192,128},{224,1... | collective-permute-start | bytes 983048 | tf_op jit(solution)/shard_map/ppermute | solution.py:401
  16.0 13.2 %collective-permute-start.6 = (bf16[2,8,64,128]{3,2,1,0:T(8,128)(2,1)S(1)}, bf16[2,8,64,128]{3,2,1,0:T(8,128)(2,1)S(1)}, u32[]{:S(2)}, u32[]{:S(2)}) collective-permute-start(bf16[2,8,64,128]{3,2,1,0:T(8,128)(2,1)S(1)} %add_convert_fusion.2), channel_id=1, source_target_pairs={{0,64},{32,96},{64,0},{96,32},{128,192},{160,224},{192,128},{224,1... | collective-permute-start | bytes 786440 | tf_op jit(solution)/shard_map/ppermute | solution.py:401
  16.2 12.7 %collective-permute-start.8 = (bf16[2,8,80,128]{3,2,1,0:T(8,128)(2,1)S(1)}, bf16[2,8,80,128]{3,2,1,0:T(8,128)(2,1)S(1)}, u32[]{:S(2)}, u32[]{:S(2)}) collective-permute-start(bf16[2,8,80,128]{3,2,1,0:T(8,128)(2,1)S(1)} %add_convert_fusion), channel_id=1, source_target_pairs={{0,192},{32,224},{64,128},{96,160},{128,64},{160,96},{192,0},{224,... | collective-permute-start | bytes 983048 | tf_op jit(solution)/shard_map/ppermute | solution.py:401
  22.0 9.2 %collective-permute-start.4 = (bf16[1,8,64,128]{3,2,1,0:T(8,128)(2,1)S(1)}, bf16[1,8,64,128]{3,2,1,0:T(8,128)(2,1)S(1)}, u32[]{:S(2)}, u32[]{:S(2)}) collective-permute-start(bf16[1,8,64,128]{3,2,1,0:T(8,128)(2,1)S(1)} %get-tuple-element.58), channel_id=1, source_target_pairs={{0,64},{32,96},{64,0},{96,32},{128,192},{160,224},{192,128},{224,1... | collective-permute-start | bytes 393224 | tf_op jit(solution)/shard_map/ppermute | solution.py:401
  22.9 11.6 %copy-start = (s32[512]{0:T(512)S(1)}, s32[512]{0:T(512)}, u32[]{:S(2)}) copy-start(s32[512]{0:T(512)} %table_ref.3) | copy-start | bytes 6148
  22.9 11.6 %collective-permute-start.2 = (bf16[1,8,80,128]{3,2,1,0:T(8,128)(2,1)S(1)}, bf16[1,8,80,128]{3,2,1,0:T(8,128)(2,1)S(1)}, u32[]{:S(2)}, u32[]{:S(2)}) collective-permute-start(bf16[1,8,80,128]{3,2,1,0:T(8,128)(2,1)S(1)} %get-tuple-element.54), channel_id=1, source_target_pairs={{0,192},{32,224},{64,128},{96,160},{128,64},{160,96},{192,0},{224,... | collective-permute-start | bytes 491528 | tf_op jit(solution)/shard_map/ppermute | solution.py:401
  29.1 5.4 %collective-permute-start.9 = (bf16[1,8,80,128]{3,2,1,0:T(8,128)(2,1)S(1)}, bf16[1,8,80,128]{3,2,1,0:T(8,128)(2,1)S(1)}, u32[]{:S(2)}, u32[]{:S(2)}) collective-permute-start(bf16[1,8,80,128]{3,2,1,0:T(8,128)(2,1)S(1)} %get-tuple-element.52), channel_id=1, source_target_pairs={{0,64},{32,96},{64,0},{96,32},{128,192},{160,224},{192,128},{224,1... | collective-permute-start | bytes 491528 | tf_op jit(solution)/shard_map/ppermute | solution.py:401
  29.3 5.2 %collective-permute-start.7 = (bf16[1,8,64,128]{3,2,1,0:T(8,128)(2,1)S(1)}, bf16[1,8,64,128]{3,2,1,0:T(8,128)(2,1)S(1)}, u32[]{:S(2)}, u32[]{:S(2)}) collective-permute-start(bf16[1,8,64,128]{3,2,1,0:T(8,128)(2,1)S(1)} %get-tuple-element.56), channel_id=1, source_target_pairs={{0,192},{32,224},{64,128},{96,160},{128,64},{160,96},{192,0},{224,... | collective-permute-start | bytes 393224 | tf_op jit(solution)/shard_map/ppermute | solution.py:401
  36.6 37.2 %all-to-all-start = ((bf16[32,144,128]{2,1,0:T(8,128)(2,1)}), bf16[32,144,128]{2,1,0:T(8,128)(2,1)S(1)}, u32[]{:S(2)}, u32[]{:S(2)}) async-start(bf16[32,144,128]{2,1,0:T(8,128)(2,1)} %get-tuple-element.33), calls=%async_computation | async-start | bytes 2359296 | tf_op jit(solution)/shard_map/all_to_all | solution.py:436
  48.0 8.3 %collective-permute-start.10 = (bf16[2,144,128]{2,1,0:T(8,128)(2,1)S(1)}, bf16[2,144,128]{2,1,0:T(8,128)(2,1)S(1)}, u32[]{:S(2)}, u32[]{:S(2)}) collective-permute-start(bf16[2,144,128]{2,1,0:T(8,128)(2,1)S(1)} %get-tuple-element.35), channel_id=1, source_target_pairs={{0,32},{32,0},{64,96},{96,64},{128,160},{160,128},{192,224},{224,1... | collective-permute-start | bytes 221192 | tf_op jit(solution)/shard_map/ppermute | solution.py:401
  51.3 6.0 %collective-permute-start.11 = (bf16[2,144,128]{2,1,0:T(8,128)(2,1)S(1)}, bf16[2,144,128]{2,1,0:T(8,128)(2,1)S(1)}, u32[]{:S(2)}, u32[]{:S(2)}) collective-permute-start(bf16[2,144,128]{2,1,0:T(8,128)(2,1)S(1)} %get-tuple-element.36), channel_id=1, source_target_pairs={{0,64},{32,96},{64,0},{96,32},{128,192},{160,224},{192,128},{224,1... | collective-permute-start | bytes 221192 | tf_op jit(solution)/shard_map/ppermute | solution.py:401
  51.3 9.9 %collective-permute-start.12 = (bf16[2,144,128]{2,1,0:T(8,128)(2,1)S(1)}, bf16[2,144,128]{2,1,0:T(8,128)(2,1)S(1)}, u32[]{:S(2)}, u32[]{:S(2)}) collective-permute-start(bf16[2,144,128]{2,1,0:T(8,128)(2,1)S(1)} %get-tuple-element.37), channel_id=1, source_target_pairs={{0,96},{32,64},{64,32},{96,0},{128,224},{160,192},{192,160},{224,1... | collective-permute-start | bytes 221192 | tf_op jit(solution)/shard_map/ppermute | solution.py:401
  53.0 8.2 %collective-permute-start.13 = (bf16[2,144,128]{2,1,0:T(8,128)(2,1)S(1)}, bf16[2,144,128]{2,1,0:T(8,128)(2,1)S(1)}, u32[]{:S(2)}, u32[]{:S(2)}) collective-permute-start(bf16[2,144,128]{2,1,0:T(8,128)(2,1)S(1)} %get-tuple-element.38), channel_id=1, source_target_pairs={{0,128},{32,160},{64,192},{96,224},{128,0},{160,32},{192,64},{224,... | collective-permute-start | bytes 221192 | tf_op jit(solution)/shard_map/ppermute | solution.py:401
  54.2 7.0 %collective-permute-start.14 = (bf16[2,144,128]{2,1,0:T(8,128)(2,1)S(1)}, bf16[2,144,128]{2,1,0:T(8,128)(2,1)S(1)}, u32[]{:S(2)}, u32[]{:S(2)}) collective-permute-start(bf16[2,144,128]{2,1,0:T(8,128)(2,1)S(1)} %get-tuple-element.39), channel_id=1, source_target_pairs={{0,160},{32,128},{64,224},{96,192},{128,32},{160,0},{192,96},{224,... | collective-permute-start | bytes 221192 | tf_op jit(solution)/shard_map/ppermute | solution.py:401
  56.3 6.3 %collective-permute-start.15 = (bf16[2,144,128]{2,1,0:T(8,128)(2,1)S(1)}, bf16[2,144,128]{2,1,0:T(8,128)(2,1)S(1)}, u32[]{:S(2)}, u32[]{:S(2)}) collective-permute-start(bf16[2,144,128]{2,1,0:T(8,128)(2,1)S(1)} %get-tuple-element.40), channel_id=1, source_target_pairs={{0,192},{32,224},{64,128},{96,160},{128,64},{160,96},{192,0},{224,... | collective-permute-start | bytes 221192 | tf_op jit(solution)/shard_map/ppermute | solution.py:401
  57.3 6.9 %collective-permute-start.16 = (bf16[2,144,128]{2,1,0:T(8,128)(2,1)S(1)}, bf16[2,144,128]{2,1,0:T(8,128)(2,1)S(1)}, u32[]{:S(2)}, u32[]{:S(2)}) collective-permute-start(bf16[2,144,128]{2,1,0:T(8,128)(2,1)S(1)} %get-tuple-element.41), channel_id=1, source_target_pairs={{0,224},{32,192},{64,160},{96,128},{128,96},{160,64},{192,32},{224... | collective-permute-start | bytes 221192 | tf_op jit(solution)/shard_map/ppermute | solution.py:401
  75.5 39.0 %all-to-all-start.1 = ((bf16[24,144,128]{2,1,0:T(8,128)(2,1)}), bf16[24,144,128]{2,1,0:T(8,128)(2,1)S(1)}, u32[]{:S(2)}, u32[]{:S(2)}) async-start(bf16[24,144,128]{2,1,0:T(8,128)(2,1)} %slot_pick.1), calls=%async_computation.1 | async-start | bytes 1769472 | tf_op jit(solution)/shard_map/all_to_all | solution.py:444
  85.4 5.3 %collective-permute-start.17 = (bf16[2,64,512]{2,1,0:T(8,128)(2,1)S(1)}, bf16[2,64,512]{2,1,0:T(8,128)(2,1)S(1)}, u32[]{:S(2)}, u32[]{:S(2)}) collective-permute-start(bf16[2,64,512]{2,1,0:T(8,128)(2,1)S(1)} %get-tuple-element.45), channel_id=1, source_target_pairs={{0,32},{32,0},{64,96},{96,64},{128,160},{160,128},{192,224},{224,1... | collective-permute-start | bytes 393224 | tf_op jit(solution)/shard_map/ppermute | solution.py:401
  85.6 14.4 %collective-permute-start.18 = (bf16[2,64,512]{2,1,0:T(8,128)(2,1)S(1)}, bf16[2,64,512]{2,1,0:T(8,128)(2,1)S(1)}, u32[]{:S(2)}, u32[]{:S(2)}) collective-permute-start(bf16[2,64,512]{2,1,0:T(8,128)(2,1)S(1)} %get-tuple-element.46), channel_id=1, source_target_pairs={{0,64},{32,96},{64,0},{96,32},{128,192},{160,224},{192,128},{224,1... | collective-permute-start | bytes 393224 | tf_op jit(solution)/shard_map/ppermute | solution.py:401
  87.2 16.5 %collective-permute-start.19 = (bf16[2,64,512]{2,1,0:T(8,128)(2,1)S(1)}, bf16[2,64,512]{2,1,0:T(8,128)(2,1)S(1)}, u32[]{:S(2)}, u32[]{:S(2)}) collective-permute-start(bf16[2,64,512]{2,1,0:T(8,128)(2,1)S(1)} %get-tuple-element.47), channel_id=1, source_target_pairs={{0,96},{32,64},{64,32},{96,0},{128,224},{160,192},{192,160},{224,1... | collective-permute-start | bytes 393224 | tf_op jit(solution)/shard_map/ppermute | solution.py:401
  87.6 19.6 %collective-permute-start.20 = (bf16[2,64,512]{2,1,0:T(8,128)(2,1)S(1)}, bf16[2,64,512]{2,1,0:T(8,128)(2,1)S(1)}, u32[]{:S(2)}, u32[]{:S(2)}) collective-permute-start(bf16[2,64,512]{2,1,0:T(8,128)(2,1)S(1)} %get-tuple-element.48), channel_id=1, source_target_pairs={{0,128},{32,160},{64,192},{96,224},{128,0},{160,32},{192,64},{224,... | collective-permute-start | bytes 393224 | tf_op jit(solution)/shard_map/ppermute | solution.py:401
  90.5 19.9 %collective-permute-start.21 = (bf16[2,64,512]{2,1,0:T(8,128)(2,1)S(1)}, bf16[2,64,512]{2,1,0:T(8,128)(2,1)S(1)}, u32[]{:S(2)}, u32[]{:S(2)}) collective-permute-start(bf16[2,64,512]{2,1,0:T(8,128)(2,1)S(1)} %get-tuple-element.49), channel_id=1, source_target_pairs={{0,160},{32,128},{64,224},{96,192},{128,32},{160,0},{192,96},{224,... | collective-permute-start | bytes 393224 | tf_op jit(solution)/shard_map/ppermute | solution.py:401
  90.7 19.6 %collective-permute-start.22 = (bf16[2,64,512]{2,1,0:T(8,128)(2,1)S(1)}, bf16[2,64,512]{2,1,0:T(8,128)(2,1)S(1)}, u32[]{:S(2)}, u32[]{:S(2)}) collective-permute-start(bf16[2,64,512]{2,1,0:T(8,128)(2,1)S(1)} %get-tuple-element.50), channel_id=1, source_target_pairs={{0,192},{32,224},{64,128},{96,160},{128,64},{160,96},{192,0},{224,... | collective-permute-start | bytes 393224 | tf_op jit(solution)/shard_map/ppermute | solution.py:401
  100.0 12.7 %collective-permute-start.23 = (bf16[2,64,512]{2,1,0:T(8,128)(2,1)S(1)}, bf16[2,64,512]{2,1,0:T(8,128)(2,1)S(1)}, u32[]{:S(2)}, u32[]{:S(2)}) collective-permute-start(bf16[2,64,512]{2,1,0:T(8,128)(2,1)S(1)} %get-tuple-element.51), channel_id=1, source_target_pairs={{0,224},{32,192},{64,160},{96,128},{128,96},{160,64},{192,32},{224... | collective-permute-start | bytes 393224 | tf_op jit(solution)/shard_map/ppermute | solution.py:401

commit v2 on v1

--- a/solution.py
+++ b/solution.py
@@ -16,6 +16,7 @@
 PACKED_ROWS = 9 * TILE
 CHUNK = PACKED_ROWS // DEVICES
 CUTS = (80, 64)
+PARTNERS = (0, 4, 5, 6, 7, 2, 3, 1)
 ROWS = BLOCK // DEVICES
 ORDERS = ((1, 2, 0, 3), (3, 2, 0, 1))
 FIRST_BITS = (2, 6)
@@ -121,9 +122,11 @@
 
 def plan_kernel(model_count, code_ref, table_ref, plan_ref):
     _, model = position(code_ref, model_count)
-    for slot in range(CAP + 1):
-        plan_ref[slot] = 0
+    for entry in range(plan_ref.shape[0]):
+        plan_ref[entry] = 0
     per_slab = table_ref.shape[0] // model_count
+    for stat in range(per_slab):
+        plan_ref[CAP + 1 + table_ref[model * per_slab + stat]] = stat
 
     def slab_step(slab, count):
         named = jnp.int32(0)
@@ -144,7 +147,7 @@
         functools.partial(plan_kernel, model_count),
         in_specs=[whole(pltpu.SMEM), whole(pltpu.SMEM)],
         out_specs=whole(pltpu.SMEM),
-        out_shape=jax.ShapeDtypeStruct((CAP + 1,), jnp.int32),
+        out_shape=jax.ShapeDtypeStruct((CAP + 1 + model_count,), jnp.int32),
         interpret=INTERPRET,
         compiler_params=params(2**20),
         name="make_plan",
@@ -152,30 +155,26 @@
     )(code, owner_table)
 
 
-def sum_kernel(model_count, code_ref, table_ref, *refs):
+def sum_kernel(model_count, code_ref, plan_ref, *refs):
     sources = refs[:8]
     outgoing_ref, *home_refs = refs[8 : 9 + DEVICES]
-    mine_ref, send_ref, out_sems, home_sems = refs[9 + DEVICES :]
-    device, model = position(code_ref, model_count)
-    count = sources[0].shape[0]
-    per_slab = 2 * count
+    mine_ref, out_sems, home_sems = refs[9 + DEVICES :]
+    device, _ = position(code_ref, model_count)
+    base = 0
     for group, cut in enumerate(CUTS):
         for part, (start, stop) in enumerate(((0, cut), (cut, CHUNK))):
             partial_ref, last_ref = sources[4 * group + 2 * part : 4 * group + 2 * part + 2]
             value = partial_ref[...] + last_ref[0].astype(F32)
-            mine_ref[group * count : (group + 1) * count, start:stop] = value.astype(BF16)
-    for owner in range(model_count):
-        send_ref[owner] = 0
-    for stat in range(per_slab):
-        send_ref[table_ref[model * per_slab + stat]] = stat
+            mine_ref[base : base + value.shape[0], start:stop] = value.astype(BF16)
+        base += value.shape[0]
     copies = []
     for owner in range(model_count):
         copies.append(
             pltpu.make_async_copy(
-                mine_ref.at[send_ref[owner]], outgoing_ref.at[owner], out_sems.at[owner]
+                mine_ref.at[plan_ref[CAP + 1 + owner]], outgoing_ref.at[owner], out_sems.at[owner]
             )
         )
-    for bits, home_ref in enumerate(home_refs):
+    for bits, home_ref in zip(PARTNERS, home_refs):
         home = device ^ bits
         copies.append(
             pltpu.make_async_copy(mine_ref.at[pl.ds(2 * home, 2)], home_ref, home_sems.at[bits])
@@ -186,8 +185,7 @@
         copy.wait()
 
 
-def sum_and_send(code, owner_table, sources, model_count):
-    count = sources[0].shape[0]
+def sum_and_send(code, plan, sources, model_count):
     home = jax.ShapeDtypeStruct((2, CHUNK, TILE), BF16)
     return pl.pallas_call(
         functools.partial(sum_kernel, model_count),
@@ -195,8 +193,7 @@
         out_specs=[whole(pltpu.HBM)] * (1 + DEVICES),
         out_shape=[jax.ShapeDtypeStruct((model_count, CHUNK, TILE), BF16)] + [home] * DEVICES,
         scratch_shapes=[
-            pltpu.VMEM((2 * count, CHUNK, TILE), BF16),
-            pltpu.SMEM((model_count,), jnp.int32),
+            pltpu.VMEM((2 * DEVICES, CHUNK, TILE), BF16),
             pltpu.SemaphoreType.DMA((model_count,)),
             pltpu.SemaphoreType.DMA((DEVICES,)),
         ],
@@ -204,33 +201,30 @@
         compiler_params=params(),
         name="sum_and_send",
         cost_estimate=cost(2**21, 2**22),
-    )(code, owner_table, *sources)
-
-
-def slot_kernel(plan_ref, source_ref, out_ref, sems):
-    copies = []
-    for slot in range(CAP):
-        copies.append(
-            pltpu.make_async_copy(source_ref.at[plan_ref[slot]], out_ref.at[slot], sems.at[slot])
-        )
-    for copy in copies:
-        copy.start()
-    for copy in copies:
-        copy.wait()
-
-
-def slot_pick(plan, incoming):
-    return pl.pallas_call(
-        slot_kernel,
-        in_specs=[whole(pltpu.SMEM), whole()],
-        out_specs=whole(pltpu.HBM),
-        out_shape=jax.ShapeDtypeStruct((CAP, CHUNK, TILE), BF16),
-        scratch_shapes=[pltpu.SemaphoreType.DMA((CAP,))],
+    )(code, plan, *sources)
+
+
+def slot_kernel(model_count, code_ref, plan_ref, source_ref, *slot_refs):
+    device, _ = position(code_ref, model_count)
+    slots = slot_refs[0].shape[0]
+    for bits, slot_ref in zip(PARTNERS, slot_refs):
+        home = device ^ bits
+        for slot in range(slots):
+            slot_ref[slot] = source_ref[plan_ref[slots * home + slot]]
+
+
+def slot_pick(code, plan, incoming, model_count):
+    slots = CAP // DEVICES
+    return pl.pallas_call(
+        functools.partial(slot_kernel, model_count),
+        in_specs=[whole(pltpu.SMEM), whole(pltpu.SMEM), whole()],
+        out_specs=[whole()] * DEVICES,
+        out_shape=[jax.ShapeDtypeStruct((slots, CHUNK, TILE), BF16)] * DEVICES,
         interpret=INTERPRET,
         compiler_params=params(8 * 2**20),
         name="slot_pick",
         cost_estimate=cost(2**21, 2**22),
-    )(plan, incoming)
+    )(code, plan, incoming)
 
 
 def total(value):
@@ -255,31 +249,42 @@
     stat_ref[rows_of(3), rows_of(3)] = jnp.where(last_row, fourth.T, fourth)
 
 
-def root_of(data_count, stack_ref, stat_ref, pair_ref):
-    unpack(stack_ref, stat_ref)
+def roots_of(data_count, stack_ref, stat_ref, pair_ref):
+    stats = range(stack_ref.shape[0])
     on_diagonal = iota((BLOCK, BLOCK), 0) == iota((BLOCK, BLOCK), 1)
-    statistic = stat_ref[...] * (1.0 / data_count)
-    diagonal_mean = total(jnp.where(on_diagonal, statistic, 0.0)) * (1.0 / BLOCK)
-    damped = statistic + jnp.where(on_diagonal, 0.1 * diagonal_mean, 0.0)
-    mean_square = total(damped * damped) * (1.0 / BLOCK**2)
-    norm_scale = BLOCK * jnp.sqrt(mean_square + 1e-06)
-    root_scale = lax.rsqrt(jnp.sqrt(norm_scale))
-    first = damped * (1.0 / norm_scale)
-    first_small = first.astype(BF16)
-    part = (dot(first_small, first_small) * 0.0625 - 0.625 * first).astype(BF16)
-    twice = 1.5625 * first + dot(part, first_small)
-    twice_small = twice.astype(BF16)
-    pair_ref[:BLOCK] = part
-    pair_ref[BLOCK:] = twice_small
-    both = dot(pair_ref[...], twice_small)
-    second = 1.5625 * twice + both[:BLOCK]
-    pair = (both[BLOCK:] * 0.0625 - 0.3125 * (first + second)).astype(BF16)
-    second_small = second.astype(BF16)
-    part = (dot(second_small, second_small) * 0.0625 - 0.625 * second).astype(BF16)
-    twice = 1.5625 * second + dot(part, second_small)
-    third = 1.5625 * twice + dot(part, twice.astype(BF16))
-    rest = 1.25 * pair.astype(F32) - 0.390625 * third - 0.25 * dot(pair, third.astype(BF16))
-    return rest * root_scale, 1.953125 * root_scale, on_diagonal
+    scales, first, small = [], [], []
+    for k in stats:
+        unpack(stack_ref.at[k], stat_ref.at[k])
+        statistic = stat_ref[k] * (1.0 / data_count)
+        diagonal_mean = total(jnp.where(on_diagonal, statistic, 0.0)) * (1.0 / BLOCK)
+        damped = statistic + jnp.where(on_diagonal, 0.1 * diagonal_mean, 0.0)
+        mean_square = total(damped * damped) * (1.0 / BLOCK**2)
+        norm_scale = BLOCK * jnp.sqrt(mean_square + 1e-06)
+        scales.append(lax.rsqrt(jnp.sqrt(norm_scale)))
+        first.append(damped * (1.0 / norm_scale))
+        small.append(first[k].astype(BF16))
+    square = [dot(small[k], small[k]) for k in stats]
+    part = [(square[k] * 0.0625 - 0.625 * first[k]).astype(BF16) for k in stats]
+    twice = [1.5625 * first[k] + dot(part[k], small[k]) for k in stats]
+    for k in stats:
+        pair_ref[k, :BLOCK] = part[k]
+        pair_ref[k, BLOCK:] = twice[k].astype(BF16)
+    both = [dot(pair_ref[k], pair_ref[k, BLOCK:]) for k in stats]
+    second = [1.5625 * twice[k] + both[k][:BLOCK] for k in stats]
+    pair = [
+        (both[k][BLOCK:] * 0.0625 - 0.3125 * (first[k] + second[k])).astype(BF16) for k in stats
+    ]
+    small = [second[k].astype(BF16) for k in stats]
+    square = [dot(small[k], small[k]) for k in stats]
+    part = [(square[k] * 0.0625 - 0.625 * second[k]).astype(BF16) for k in stats]
+    twice = [1.5625 * second[k] + dot(part[k], small[k]) for k in stats]
+    third = [1.5625 * twice[k] + dot(part[k], twice[k].astype(BF16)) for k in stats]
+    result = []
+    for k in stats:
+        rest = 1.25 * pair[k].astype(F32) - 0.390625 * third[k]
+        rest = rest - 0.25 * dot(pair[k], third[k].astype(BF16))
+        result.append((rest * scales[k], 1.953125 * scales[k]))
+    return result, on_diagonal
 
 
 def home_kernel(data_count, model_count, code_ref, *refs):
@@ -288,18 +293,19 @@
     device, _ = position(code_ref, model_count)
     row_ids = iota((BLOCK, BLOCK), 0)
     spare = (row_ids % ROWS == 1) & (iota((BLOCK, BLOCK), 1) == row_ids - 1)
-    for stat in range(2):
-        for bits, ref in enumerate(sources):
-            start = pl.multiple_of((device ^ bits) * CHUNK, 16)
-            stack_ref[pl.ds(start, CHUNK)] = ref[stat].astype(F32)
-        rest, identity_part, on_diagonal = root_of(data_count, stack_ref, stat_ref, pair_ref)
+    for bits, ref in zip(PARTNERS, sources):
+        start = pl.multiple_of((device ^ bits) * CHUNK, 16)
+        for stat in range(2):
+            stack_ref[stat, pl.ds(start, CHUNK)] = ref[stat].astype(F32)
+    roots, on_diagonal = roots_of(data_count, stack_ref, stat_ref, pair_ref)
+    for stat, (rest, identity_part) in enumerate(roots):
         rest_mean = total(jnp.where(on_diagonal, rest, 0.0)) * (1.0 / BLOCK)
         center = (identity_part + rest_mean).astype(BF16).astype(F32)
         rest = rest + jnp.where(on_diagonal, identity_part - center, 0.0)
         sent = jnp.where(spare, center, rest).astype(BF16)
         for home in range(DEVICES):
             rows_ref[home] = sent[home * ROWS : (home + 1) * ROWS]
-        for bits, row_ref in enumerate(row_refs):
+        for bits, row_ref in zip(PARTNERS, row_refs):
             row_ref[stat] = rows_ref[device ^ bits]
 
 
@@ -311,9 +317,9 @@
         out_shape=[jax.ShapeDtypeStruct((2, ROWS, BLOCK), BF16)] * DEVICES,
         scratch_shapes=[
             pltpu.VMEM((DEVICES, ROWS, BLOCK), BF16),
-            pltpu.VMEM((PACKED_ROWS, TILE), F32),
-            pltpu.VMEM((BLOCK, BLOCK), F32),
-            pltpu.VMEM((2 * BLOCK, BLOCK), BF16),
+            pltpu.VMEM((2, PACKED_ROWS, TILE), F32),
+            pltpu.VMEM((2, BLOCK, BLOCK), F32),
+            pltpu.VMEM((2, 2 * BLOCK, BLOCK), BF16),
         ],
         interpret=INTERPRET,
         compiler_params=params(),
@@ -323,46 +329,49 @@
 
 
 def owner_kernel(
-    data_count, model_count, code_ref, plan_ref, source_ref, out_ref, stack_ref, stat_ref, pair_ref
+    data_count,
+    model_count,
+    code_ref,
+    plan_ref,
+    *refs,
 ):
-    device, _ = position(code_ref, model_count)
-    slot = pl.program_id(0)
-    keep = pl.num_programs(0) * device + slot < plan_ref[CAP]
-
-    @pl.when(keep)
-    def _():
-        for chunk in range(DEVICES):
-            stack_ref[chunk * CHUNK : (chunk + 1) * CHUNK] = source_ref[chunk, 0].astype(F32)
-        rest, identity_part, on_diagonal = root_of(data_count, stack_ref, stat_ref, pair_ref)
-        out_ref[0] = rest + jnp.where(on_diagonal, identity_part, 0.0)
-
-    @pl.when(jnp.logical_not(keep))
-    def _():
-        out_ref[...] = jnp.zeros_like(out_ref)
-
-
-def owner_roots(code, plan, source, data_count, model_count):
-    slots = source.shape[1]
+    sources = refs[:DEVICES]
+    out_ref, stack_ref, stat_ref, pair_ref, root_ref, sems = refs[DEVICES:]
+    device, _ = position(code_ref, model_count)
+    slots = out_ref.shape[0]
+    for bits, ref in zip(PARTNERS, sources):
+        start = pl.multiple_of((device ^ bits) * CHUNK, 16)
+        for slot in range(slots):
+            stack_ref[slot, pl.ds(start, CHUNK)] = ref[slot].astype(F32)
+    roots, on_diagonal = roots_of(data_count, stack_ref, stat_ref, pair_ref)
+    for slot, (rest, identity_part) in enumerate(roots):
+        keep = slots * device + slot < plan_ref[CAP]
+        root = rest + jnp.where(on_diagonal, identity_part, 0.0)
+        root_ref[slot] = jnp.where(keep, root, 0.0)
+        pltpu.make_async_copy(root_ref.at[slot], out_ref.at[slot], sems.at[slot]).start()
+    for slot in range(slots):
+        pltpu.make_async_copy(root_ref.at[slot], out_ref.at[slot], sems.at[slot]).wait()
+
+
+def owner_roots(code, plan, sources, data_count, model_count):
+    slots = sources[0].shape[0]
     return pl.pallas_call(
         functools.partial(owner_kernel, data_count, model_count),
-        grid=(slots,),
-        in_specs=[
-            whole(pltpu.SMEM),
-            whole(pltpu.SMEM),
-            pl.BlockSpec((DEVICES, 1, CHUNK, TILE), lambda slot: (0, slot, 0, 0)),
-        ],
-        out_specs=pl.BlockSpec((1, BLOCK, BLOCK), lambda slot: (slot, 0, 0)),
+        in_specs=[whole(pltpu.SMEM), whole(pltpu.SMEM)] + [whole()] * DEVICES,
+        out_specs=whole(pltpu.HBM),
         out_shape=jax.ShapeDtypeStruct((slots, BLOCK, BLOCK), F32),
         scratch_shapes=[
-            pltpu.VMEM((PACKED_ROWS, TILE), F32),
-            pltpu.VMEM((BLOCK, BLOCK), F32),
-            pltpu.VMEM((2 * BLOCK, BLOCK), BF16),
+            pltpu.VMEM((slots, PACKED_ROWS, TILE), F32),
+            pltpu.VMEM((slots, BLOCK, BLOCK), F32),
+            pltpu.VMEM((slots, 2 * BLOCK, BLOCK), BF16),
+            pltpu.VMEM((slots, BLOCK, BLOCK), F32),
+            pltpu.SemaphoreType.DMA((slots,)),
         ],
         interpret=INTERPRET,
-        compiler_params=params(),
+        compiler_params=params(40 * 2**20),
         name="owner_roots",
         cost_estimate=cost(3 * 8 * 2 * BLOCK**3, 2**22),
-    )(code, plan, source)
+    )(code, plan, *sources)
 
 
 def finish_kernel(model_count, code_ref, *refs):
@@ -374,7 +383,7 @@
     spare = (row_ids == 1) & (column_ids == 0)
     mirror = (row_ids == 0) & (column_ids == 1)
     on_diagonal = row_ids == column_ids
-    for bits, ref in enumerate(refs[:-1]):
+    for bits, ref in zip(PARTNERS, refs[:-1]):
         home = device ^ bits
         for stat in range(2):
             value = ref[stat].astype(F32)
@@ -403,7 +412,7 @@
 
 def exchange_all(values, data_count):
     return [values[0]] + [
-        exchange(values[bits], bits, data_count) for bits in range(1, data_count)
+        exchange(value, bits, data_count) for value, bits in zip(values[1:], PARTNERS[1:])
     ]
 
 
@@ -415,8 +424,8 @@
     code = (lax.axis_index("dp") * model_count + lax.axis_index("mp")).reshape(1)
 
     sources = []
+    gram_code = code
     half = row_blocks // 2
-    gram_code = code
     for group, cut in enumerate(CUTS):
         own, away = gram_blocks(blocks, gram_code, model_count, group * half, half, cut)
         if group == 0:
@@ -432,7 +441,7 @@
             sources += [third + step[0].astype(F32), last]
 
     plan = make_plan(code, owner_table, model_count)
-    outgoing, *home = sum_and_send(code, owner_table, sources, model_count)
+    outgoing, *home = sum_and_send(code, plan, sources, model_count)
     incoming = lax.all_to_all(outgoing, "mp", split_axis=0, concat_axis=0, tiled=True)
 
     rows = list(home_roots(code, exchange_all(home, data_count), data_count, model_count))
@@ -440,9 +449,8 @@
     rows = exchange_all(rows, data_count)
     slab_roots = finish_rows(code, rows, model_count)
 
-    slots = slot_pick(plan, incoming)
-    stacked = lax.all_to_all(slots, "dp", split_axis=0, concat_axis=0, tiled=True)
-    stacked = stacked.reshape(data_count, CAP // data_count, CHUNK, TILE)
+    slots = slot_pick(code, plan, incoming, model_count)
+    stacked = exchange_all(slots, data_count)
     root_stacks = owner_roots(code, plan, stacked, data_count, model_count)
     return (root_stacks[None], slab_roots)
 

time: 126 us -> 105 us (0.83)
  waiting for transfers between devices: 36.7 us -> 25.7 us
  starting transfers between devices: 53.4 us -> 46.6 us
  Pallas kernels: 31.3 us -> 28.9 us
    all_to_all x1 -> x0, starting transfers between devices: 9.96 us -> none  [program(): lax.all_to_all(slots, 'dp', split_axis=0, concat_axis=0, tiled=True)]
    ppermute x24 -> x31, waiting for transfers between devices: 33.2 us -> 25.7 us  [exchange(): return lax.ppermute(value, 'dp', [(d, d ^ bits) for d in range(data_count)])]
    all_to_all x1, waiting for transfers between devices: 3.47 us -> 0.01 us  [program(): lax.all_to_all(outgoing, 'mp', split_axis=0, concat_axis=0, tiled=True)]
    ppermute x24 -> x31, starting transfers between devices: 32 us -> 35.2 us  [exchange(): return lax.ppermute(value, 'dp', [(d, d ^ bits) for d in range(data_count)])]
  transfers between devices with their start and end apart: 26 -> 32, of which waited for: 14 -> 15; matrix products, arithmetic and copies ran while one was open for 1% -> 1% of each run, Pallas kernels for 11% -> 13%
where the time goes in v2:
time: 105 us
  starting transfers between devices  46.6 us (44%)
  Pallas kernels  28.9 us (28%)
  waiting for transfers between devices  25.7 us (24%)
  local copies, waits for them, and re-layouts  2.19 us (2%)
    ppermute x31, starting transfers between devices, exchange(): return lax.ppermute(value, 'dp', [(d, d ^ bits) for d in range(data_count)])  35.2 us
    ppermute x31, waiting for transfers between devices, exchange(): return lax.ppermute(value, 'dp', [(d, d ^ bits) for d in range(data_count)])  25.7 us
    all_to_all x1, starting transfers between devices, program(): lax.all_to_all(outgoing, 'mp', split_axis=0, concat_axis=0, tiled=True)  11.4 us
    pallas_call x1, Pallas kernels, owner_roots(): pl.pallas_call(functools.partial(owner_kernel, data_count, model_count),...  9.76 us
    pallas_call x2, Pallas kernels, gram_blocks(): pl.pallas_call(functools.partial(gram_kernel, model_count, cut), out_shap...  6.87 us
    pallas_call x1, Pallas kernels, home_roots(): pl.pallas_call(functools.partial(home_kernel, data_count, model_count), i...  5.87 us
    unnamed x4, local copies, waits for them, and re-layouts  2.19 us
  transfers between devices with their start and end apart: 32, of which 15 were waited for; matrix products, arithmetic and copies ran while one was open for 1% of the time, Pallas kernels for 13%

profile of v2, /device:TPU:1, one launch (start us, length us, event | category | flops | bytes accessed | tf_op | source)
XLA Modules:
  0.0 105.2 jit_solution(2910302810050729490)
XLA Ops:
  0.6 2.2 %copy-done = bf16[1,4096,512]{2,1,0:T(8,128)(2,1)S(1)} copy-done((bf16[1,4096,512]{2,1,0:T(8,128)(2,1)S(1)}, bf16[1,4096,512]{2,1,0:T(8,128)(2,1)}, u32[]{:S(2)}) %copy-start) | copy-done | bytes 4194328
  2.8 3.4 %shard_map.41 = (bf16[4,8,144,128]{3,2,1,0:T(8,128)(2,1)S(1)}, bf16[4,8,144,128]{3,2,1,0:T(8,128)(2,1)S(1)}) custom-call(s32[1]{0:T(128)} %bitcast.code_ref, bf16[8,512,512]{2,1,0:T(8,128)(2,1)S(1)} %bitcast.11), custom_call_target="tpu_custom_call" | custom-call | flops 1610612736 | bytes 5242880 | tf_op jit(solution)/shard_map/pallas_call | solution.py:107
  6.3 3.3 %collective-permute-start = (bf16[4,8,144,128]{3,2,1,0:T(8,128)(2,1)S(1)}, bf16[4,8,144,128]{3,2,1,0:T(8,128)(2,1)S(1)}, u32[]{:S(2)}, u32[]{:S(2)}) collective-permute-start(bf16[4,8,144,128]{3,2,1,0:T(8,128)(2,1)S(1)} %get-tuple-element.37), channel_id=1, source_target_pairs={{0,32},{32,0},{64,96},{96,64},{128,160},{160,128},{192,224},{224,1... | collective-permute-start | bytes 3538952 | tf_op jit(solution)/shard_map/ppermute | solution.py:410
  9.6 3.4 %shard_map.42 = (bf16[4,8,144,128]{3,2,1,0:T(8,128)(2,1)S(1)}, bf16[4,8,144,128]{3,2,1,0:T(8,128)(2,1)S(1)}) custom-call(s32[1]{0:T(128)} %bitcast.code_ref, bf16[8,512,512]{2,1,0:T(8,128)(2,1)S(1)} %bitcast.12), custom_call_target="tpu_custom_call" | custom-call | flops 1610612736 | bytes 5242880 | tf_op jit(solution)/shard_map/pallas_call | solution.py:107
  14.3 1.7 %collective-permute-done.5 = bf16[4,8,144,128]{3,2,1,0:T(8,128)(2,1)S(1)} collective-permute-done((bf16[4,8,144,128]{3,2,1,0:T(8,128)(2,1)S(1)}, bf16[4,8,144,128]{3,2,1,0:T(8,128)(2,1)S(1)}, u32[]{:S(2)}, u32[]{:S(2)}) %collective-permute-start.5) | collective-permute-done | bytes 1179680 | tf_op jit(solution)/shard_map/ppermute | solution.py:410
  16.2 1.8 %collective-permute-start.8 = (bf16[2,8,80,128]{3,2,1,0:T(8,128)(2,1)S(1)}, bf16[2,8,80,128]{3,2,1,0:T(8,128)(2,1)S(1)}, u32[]{:S(2)}, u32[]{:S(2)}) collective-permute-start(bf16[2,8,80,128]{3,2,1,0:T(8,128)(2,1)S(1)} %add_convert_fusion), channel_id=1, source_target_pairs={{0,192},{32,224},{64,128},{96,160},{128,64},{160,96},{192,0},{224,... | collective-permute-start | bytes 983048 | tf_op jit(solution)/shard_map/ppermute | solution.py:410
  18.0 3.9 %collective-permute-done.3 = bf16[2,8,64,128]{3,2,1,0:T(8,128)(2,1)S(1)} collective-permute-done((bf16[2,8,64,128]{3,2,1,0:T(8,128)(2,1)S(1)}, bf16[2,8,64,128]{3,2,1,0:T(8,128)(2,1)S(1)}, u32[]{:S(2)}, u32[]{:S(2)}) %collective-permute-start.3) | collective-permute-done | bytes 262176 | tf_op jit(solution)/shard_map/ppermute | solution.py:410
  22.9 2.0 %collective-permute-start.2 = (bf16[1,8,80,128]{3,2,1,0:T(8,128)(2,1)S(1)}, bf16[1,8,80,128]{3,2,1,0:T(8,128)(2,1)S(1)}, u32[]{:S(2)}, u32[]{:S(2)}) collective-permute-start(bf16[1,8,80,128]{3,2,1,0:T(8,128)(2,1)S(1)} %get-tuple-element.70), channel_id=1, source_target_pairs={{0,192},{32,224},{64,128},{96,160},{128,64},{160,96},{192,0},{224,... | collective-permute-start | bytes 491528 | tf_op jit(solution)/shard_map/ppermute | solution.py:410
  24.9 4.0 %collective-permute-done.8 = bf16[2,8,80,128]{3,2,1,0:T(8,128)(2,1)S(1)} collective-permute-done((bf16[2,8,80,128]{3,2,1,0:T(8,128)(2,1)S(1)}, bf16[2,8,80,128]{3,2,1,0:T(8,128)(2,1)S(1)}, u32[]{:S(2)}, u32[]{:S(2)}) %collective-permute-start.8) | collective-permute-done | bytes 327712 | tf_op jit(solution)/shard_map/ppermute | solution.py:410
  29.3 1.2 %collective-permute-start.7 = (bf16[1,8,64,128]{3,2,1,0:T(8,128)(2,1)S(1)}, bf16[1,8,64,128]{3,2,1,0:T(8,128)(2,1)S(1)}, u32[]{:S(2)}, u32[]{:S(2)}) collective-permute-start(bf16[1,8,64,128]{3,2,1,0:T(8,128)(2,1)S(1)} %get-tuple-element.72), channel_id=1, source_target_pairs={{0,192},{32,224},{64,128},{96,160},{128,64},{160,96},{192,0},{224,... | collective-permute-start | bytes 393224 | tf_op jit(solution)/shard_map/ppermute | solution.py:410
  30.5 2.0 %make_plan.1.plan_ref = s32[57]{0:T(128)S(1)} custom-call(s32[1]{0:T(128)} %bitcast.code_ref, s32[512]{0:T(512)S(1)} %copy-done.1), custom_call_target="tpu_custom_call" | custom-call | flops 4194304 | bytes 4096 | tf_op jit(solution)/shard_map/make_plan/pallas_call | solution.py:146
  32.6 1.9 %collective-permute-done.7.refs_5_ = bf16[1,8,64,128]{3,2,1,0:T(8,128)(2,1)S(1)} collective-permute-done((bf16[1,8,64,128]{3,2,1,0:T(8,128)(2,1)S(1)}, bf16[1,8,64,128]{3,2,1,0:T(8,128)(2,1)S(1)}, u32[]{:S(2)}, u32[]{:S(2)}) %collective-permute-start.7) | collective-permute-done | bytes 131104 | tf_op jit(solution)/shard_map/ppermute | solution.py:410
  34.5 2.0 %sum_and_send.1 = (bf16[32,144,128]{2,1,0:T(8,128)(2,1)}, bf16[2,144,128]{2,1,0:T(8,128)(2,1)S(1)}, bf16[2,144,128]{2,1,0:T(8,128)(2,1)S(1)}, bf16[2,144,128]{2,...) custom-call(s32[1]{0:T(128)} %bitcast.code_ref, ...), custom_call_target="tpu_custom_call" | custom-call | flops 2097152 | bytes 4194304 | tf_op jit(solution)/shard_map/sum_and_send/pallas_call | solution.py:190
  36.5 11.4 %all-to-all-start = ((bf16[32,144,128]{2,1,0:T(8,128)(2,1)}), bf16[32,144,128]{2,1,0:T(8,128)(2,1)S(1)}, u32[]{:S(2)}, u32[]{:S(2)}) async-start(bf16[32,144,128]{2,1,0:T(8,128)(2,1)} %get-tuple-element.41), calls=%async_computation | async-start | bytes 2359296 | tf_op jit(solution)/shard_map/all_to_all | solution.py:445
  48.8 5.6 %collective-permute-start.11 = (bf16[2,144,128]{2,1,0:T(8,128)(2,1)S(1)}, bf16[2,144,128]{2,1,0:T(8,128)(2,1)S(1)}, u32[]{:S(2)}, u32[]{:S(2)}) collective-permute-start(bf16[2,144,128]{2,1,0:T(8,128)(2,1)S(1)} %get-tuple-element.44), channel_id=1, source_target_pairs={{0,160},{32,128},{64,224},{96,192},{128,32},{160,0},{192,96},{224,... | collective-permute-start | bytes 221192 | tf_op jit(solution)/shard_map/ppermute | solution.py:410
  55.6 3.5 %collective-permute-start.15 = (bf16[2,144,128]{2,1,0:T(8,128)(2,1)S(1)}, bf16[2,144,128]{2,1,0:T(8,128)(2,1)S(1)}, u32[]{:S(2)}, u32[]{:S(2)}) collective-permute-start(bf16[2,144,128]{2,1,0:T(8,128)(2,1)S(1)} %get-tuple-element.48), channel_id=1, source_target_pairs={{0,96},{32,64},{64,32},{96,0},{128,224},{160,192},{192,160},{224,1... | collective-permute-start | bytes 221192 | tf_op jit(solution)/shard_map/ppermute | solution.py:410
  59.8 1.6 %collective-permute-done.13.refs_4_ = bf16[2,144,128]{2,1,0:T(8,128)(2,1)S(1)} collective-permute-done((bf16[2,144,128]{2,1,0:T(8,128)(2,1)S(1)}, bf16[2,144,128]{2,1,0:T(8,128)(2,1)S(1)}, u32[]{:S(2)}, u32[]{:S(2)}) %collective-permute-start.13) | collective-permute-done | bytes 73760 | tf_op jit(solution)/shard_map/ppermute | solution.py:410
  62.4 5.9 %home_roots.1 = (bf16[2,64,512]{2,1,0:T(8,128)(2,1)S(1)}, bf16[2,64,512]{2,1,0:T(8,128)(2,1)S(1)}, bf16[2,64,512]{2,1,0:T(8,128)(2,1)S(1)}, bf16[2,64,512]{2,1,0...) custom-call(s32[1]{0:T(128)} %bitcast.code_ref, ...), custom_call_target="tpu_custom_call" | custom-call | flops 4294967296 | bytes 4194304 | tf_op jit(solution)/shard_map/home_roots/pallas_call | solution.py:313
  68.7 2.4 %collective-permute-start.25 = (bf16[2,64,512]{2,1,0:T(8,128)(2,1)S(1)}, bf16[2,64,512]{2,1,0:T(8,128)(2,1)S(1)}, u32[]{:S(2)}, u32[]{:S(2)}) collective-permute-start(bf16[2,64,512]{2,1,0:T(8,128)(2,1)S(1)} %get-tuple-element.62), channel_id=1, source_target_pairs={{0,160},{32,128},{64,224},{96,192},{128,32},{160,0},{192,96},{224,... | collective-permute-start | bytes 393224 | tf_op jit(solution)/shard_map/ppermute | solution.py:410
  71.1 1.2 %collective-permute-start.26 = (bf16[2,64,512]{2,1,0:T(8,128)(2,1)S(1)}, bf16[2,64,512]{2,1,0:T(8,128)(2,1)S(1)}, u32[]{:S(2)}, u32[]{:S(2)}) collective-permute-start(bf16[2,64,512]{2,1,0:T(8,128)(2,1)S(1)} %get-tuple-element.63), channel_id=1, source_target_pairs={{0,192},{32,224},{64,128},{96,160},{128,64},{160,96},{192,0},{224,... | collective-permute-start | bytes 393224 | tf_op jit(solution)/shard_map/ppermute | solution.py:410
  72.4 2.2 %collective-permute-start.27 = (bf16[2,64,512]{2,1,0:T(8,128)(2,1)S(1)}, bf16[2,64,512]{2,1,0:T(8,128)(2,1)S(1)}, u32[]{:S(2)}, u32[]{:S(2)}) collective-permute-start(bf16[2,64,512]{2,1,0:T(8,128)(2,1)S(1)} %get-tuple-element.64), channel_id=1, source_target_pairs={{0,224},{32,192},{64,160},{96,128},{128,96},{160,64},{192,32},{224... | collective-permute-start | bytes 393224 | tf_op jit(solution)/shard_map/ppermute | solution.py:410
  75.3 1.1 %collective-permute-start.29 = (bf16[2,64,512]{2,1,0:T(8,128)(2,1)S(1)}, bf16[2,64,512]{2,1,0:T(8,128)(2,1)S(1)}, u32[]{:S(2)}, u32[]{:S(2)}) collective-permute-start(bf16[2,64,512]{2,1,0:T(8,128)(2,1)S(1)} %get-tuple-element.66), channel_id=1, source_target_pairs={{0,96},{32,64},{64,32},{96,0},{128,224},{160,192},{192,160},{224,1... | collective-permute-start | bytes 393224 | tf_op jit(solution)/shard_map/ppermute | solution.py:410
  76.5 1.7 %collective-permute-done.25.refs_2_ = bf16[2,64,512]{2,1,0:T(8,128)(2,1)S(1)} collective-permute-done((bf16[2,64,512]{2,1,0:T(8,128)(2,1)S(1)}, bf16[2,64,512]{2,1,0:T(8,128)(2,1)S(1)}, u32[]{:S(2)}, u32[]{:S(2)}) %collective-permute-start.25) | collective-permute-done | bytes 131104 | tf_op jit(solution)/shard_map/ppermute | solution.py:410
  79.2 1.7 %collective-permute-done.26.refs_3_ = bf16[2,64,512]{2,1,0:T(8,128)(2,1)S(1)} collective-permute-done((bf16[2,64,512]{2,1,0:T(8,128)(2,1)S(1)}, bf16[2,64,512]{2,1,0:T(8,128)(2,1)S(1)}, u32[]{:S(2)}, u32[]{:S(2)}) %collective-permute-start.26) | collective-permute-done | bytes 131104 | tf_op jit(solution)/shard_map/ppermute | solution.py:410
  81.5 2.2 %collective-permute-done.27.refs_4_ = bf16[2,64,512]{2,1,0:T(8,128)(2,1)S(1)} collective-permute-done((bf16[2,64,512]{2,1,0:T(8,128)(2,1)S(1)}, bf16[2,64,512]{2,1,0:T(8,128)(2,1)S(1)}, u32[]{:S(2)}, u32[]{:S(2)}) %collective-permute-start.27) | collective-permute-done | bytes 131104 | tf_op jit(solution)/shard_map/ppermute | solution.py:410
  84.6 1.6 %collective-permute-start.19 = (bf16[3,144,128]{2,1,0:T(8,128)(2,1)S(1)}, bf16[3,144,128]{2,1,0:T(8,128)(2,1)S(1)}, u32[]{:S(2)}, u32[]{:S(2)}) collective-permute-start(bf16[3,144,128]{2,1,0:T(8,128)(2,1)S(1)} %get-tuple-element.55), channel_id=1, source_target_pairs={{0,192},{32,224},{64,128},{96,160},{128,64},{160,96},{192,0},{224,... | collective-permute-start | bytes 331784 | tf_op jit(solution)/shard_map/ppermute | solution.py:410
  86.2 1.2 %collective-permute-start.20 = (bf16[3,144,128]{2,1,0:T(8,128)(2,1)S(1)}, bf16[3,144,128]{2,1,0:T(8,128)(2,1)S(1)}, u32[]{:S(2)}, u32[]{:S(2)}) collective-permute-start(bf16[3,144,128]{2,1,0:T(8,128)(2,1)S(1)} %get-tuple-element.56), channel_id=1, source_target_pairs={{0,224},{32,192},{64,160},{96,128},{128,96},{160,64},{192,32},{224... | collective-permute-start | bytes 331784 | tf_op jit(solution)/shard_map/ppermute | solution.py:410
  87.6 1.8 %collective-permute-start.22 = (bf16[3,144,128]{2,1,0:T(8,128)(2,1)S(1)}, bf16[3,144,128]{2,1,0:T(8,128)(2,1)S(1)}, u32[]{:S(2)}, u32[]{:S(2)}) collective-permute-start(bf16[3,144,128]{2,1,0:T(8,128)(2,1)S(1)} %get-tuple-element.58), channel_id=1, source_target_pairs={{0,96},{32,64},{64,32},{96,0},{128,224},{160,192},{192,160},{224,1... | collective-permute-start | bytes 331784 | tf_op jit(solution)/shard_map/ppermute | solution.py:410
  89.4 1.0 collective-permute-done.18.refs_2_
  90.8 1.7 %finish_rows.1 = f32[16,64,512]{2,1,0:T(8,128)} custom-call(s32[1]{0:T(128)} %bitcast.code_ref, bf16[2,64,512]{2,1,0:T(8,128)(2,1)S(1)} %get-tuple-element.60.refs_0_, bf16[2,64,512]{2,1,0:T(8,128)(2,1)S(1)} %collective-permute-done.24.refs_1_, bf16[2,64,512]{2,1,0:T(8,128)(2,1)S(1)} %collective-permute-done.25.refs_2_, ...), custom_call_target="tpu_custom_call" | custom-call | flops 2097152 | bytes 4194304 | tf_op jit(solution)/shard_map/finish_rows/pallas_call | solution.py:397
  92.9 2.4 %collective-permute-done.20.refs_4_ = bf16[3,144,128]{2,1,0:T(8,128)(2,1)S(1)} collective-permute-done((bf16[3,144,128]{2,1,0:T(8,128)(2,1)S(1)}, bf16[3,144,128]{2,1,0:T(8,128)(2,1)S(1)}, u32[]{:S(2)}, u32[]{:S(2)}) %collective-permute-start.20) | collective-permute-done | bytes 110624 | tf_op jit(solution)/shard_map/ppermute | solution.py:410
  95.3 9.8 %owner_roots.1 = f32[3,512,512]{2,1,0:T(8,128)} custom-call(s32[1]{0:T(128)} %bitcast.code_ref, s32[57]{0:T(128)S(1)} %make_plan.1.plan_ref, bf16[3,144,128]{2,1,0:T(8,128)(2,1)S(1)} %get-tuple-element.52.refs_0_, bf16[3,144,128]{2,1,0:T(8,128)(2,1)S(1)} %collective-permute-done.17.refs_1_, bf16[3,144,128]{2,1,0:T(8,128)(2,1)S(1)} %collective-permute-done.18.refs_2_, ...), custom_call_target="tpu_custom_call" | custom-call | flops 6442450944 | bytes 4194304 | tf_op jit(solution)/shard_map/owner_roots/pallas_call | solution.py:358
  (52 shorter events, 11.3 us)
Async XLA Ops:
  6.3 6.9 %collective-permute-start = (bf16[4,8,144,128]{3,2,1,0:T(8,128)(2,1)S(1)}, bf16[4,8,144,128]{3,2,1,0:T(8,128)(2,1)S(1)}, u32[]{:S(2)}, u32[]{:S(2)}) collective-permute-start(bf16[4,8,144,128]{3,2,1,0:T(8,128)(2,1)S(1)} %get-tuple-element.37), channel_id=1, source_target_pairs={{0,32},{32,0},{64,96},{96,64},{128,160},{160,128},{192,224},{224,1... | collective-permute-start | bytes 3538952 | tf_op jit(solution)/shard_map/ppermute | solution.py:410
  13.0 2.9 %collective-permute-start.5 = (bf16[4,8,144,128]{3,2,1,0:T(8,128)(2,1)S(1)}, bf16[4,8,144,128]{3,2,1,0:T(8,128)(2,1)S(1)}, u32[]{:S(2)}, u32[]{:S(2)}) collective-permute-start(bf16[4,8,144,128]{3,2,1,0:T(8,128)(2,1)S(1)} %get-tuple-element.40), channel_id=1, source_target_pairs={{0,32},{32,0},{64,96},{96,64},{128,160},{160,128},{192,224},{224,1... | collective-permute-start | bytes 3538952 | tf_op jit(solution)/shard_map/ppermute | solution.py:410
  13.2 8.7 %collective-permute-start.3 = (bf16[2,8,64,128]{3,2,1,0:T(8,128)(2,1)S(1)}, bf16[2,8,64,128]{3,2,1,0:T(8,128)(2,1)S(1)}, u32[]{:S(2)}, u32[]{:S(2)}) collective-permute-start(bf16[2,8,64,128]{3,2,1,0:T(8,128)(2,1)S(1)} %add_convert_fusion.3), channel_id=1, source_target_pairs={{0,192},{32,224},{64,128},{96,160},{128,64},{160,96},{192,0},{224,... | collective-permute-start | bytes 786440 | tf_op jit(solution)/shard_map/ppermute | solution.py:410
  14.2 8.6 %collective-permute-start.1 = (bf16[2,8,80,128]{3,2,1,0:T(8,128)(2,1)S(1)}, bf16[2,8,80,128]{3,2,1,0:T(8,128)(2,1)S(1)}, u32[]{:S(2)}, u32[]{:S(2)}) collective-permute-start(bf16[2,8,80,128]{3,2,1,0:T(8,128)(2,1)S(1)} %add_convert_fusion.1), channel_id=1, source_target_pairs={{0,64},{32,96},{64,0},{96,32},{128,192},{160,224},{192,128},{224,1... | collective-permute-start | bytes 983048 | tf_op jit(solution)/shard_map/ppermute | solution.py:410
  16.0 13.2 %collective-permute-start.6 = (bf16[2,8,64,128]{3,2,1,0:T(8,128)(2,1)S(1)}, bf16[2,8,64,128]{3,2,1,0:T(8,128)(2,1)S(1)}, u32[]{:S(2)}, u32[]{:S(2)}) collective-permute-start(bf16[2,8,64,128]{3,2,1,0:T(8,128)(2,1)S(1)} %add_convert_fusion.2), channel_id=1, source_target_pairs={{0,64},{32,96},{64,0},{96,32},{128,192},{160,224},{192,128},{224,1... | collective-permute-start | bytes 786440 | tf_op jit(solution)/shard_map/ppermute | solution.py:410
  16.2 12.7 %collective-permute-start.8 = (bf16[2,8,80,128]{3,2,1,0:T(8,128)(2,1)S(1)}, bf16[2,8,80,128]{3,2,1,0:T(8,128)(2,1)S(1)}, u32[]{:S(2)}, u32[]{:S(2)}) collective-permute-start(bf16[2,8,80,128]{3,2,1,0:T(8,128)(2,1)S(1)} %add_convert_fusion), channel_id=1, source_target_pairs={{0,192},{32,224},{64,128},{96,160},{128,64},{160,96},{192,0},{224,... | collective-permute-start | bytes 983048 | tf_op jit(solution)/shard_map/ppermute | solution.py:410
  22.0 10.5 %collective-permute-start.4 = (bf16[1,8,64,128]{3,2,1,0:T(8,128)(2,1)S(1)}, bf16[1,8,64,128]{3,2,1,0:T(8,128)(2,1)S(1)}, u32[]{:S(2)}, u32[]{:S(2)}) collective-permute-start(bf16[1,8,64,128]{3,2,1,0:T(8,128)(2,1)S(1)} %get-tuple-element.74), channel_id=1, source_target_pairs={{0,64},{32,96},{64,0},{96,32},{128,192},{160,224},{192,128},{224,1... | collective-permute-start | bytes 393224 | tf_op jit(solution)/shard_map/ppermute | solution.py:410
  22.9 11.6 %collective-permute-start.2 = (bf16[1,8,80,128]{3,2,1,0:T(8,128)(2,1)S(1)}, bf16[1,8,80,128]{3,2,1,0:T(8,128)(2,1)S(1)}, u32[]{:S(2)}, u32[]{:S(2)}) collective-permute-start(bf16[1,8,80,128]{3,2,1,0:T(8,128)(2,1)S(1)} %get-tuple-element.70), channel_id=1, source_target_pairs={{0,192},{32,224},{64,128},{96,160},{128,64},{160,96},{192,0},{224,... | collective-permute-start | bytes 491528 | tf_op jit(solution)/shard_map/ppermute | solution.py:410
  29.1 5.4 %collective-permute-start.9 = (bf16[1,8,80,128]{3,2,1,0:T(8,128)(2,1)S(1)}, bf16[1,8,80,128]{3,2,1,0:T(8,128)(2,1)S(1)}, u32[]{:S(2)}, u32[]{:S(2)}) collective-permute-start(bf16[1,8,80,128]{3,2,1,0:T(8,128)(2,1)S(1)} %get-tuple-element.68), channel_id=1, source_target_pairs={{0,64},{32,96},{64,0},{96,32},{128,192},{160,224},{192,128},{224,1... | collective-permute-start | bytes 491528 | tf_op jit(solution)/shard_map/ppermute | solution.py:410
  29.3 5.2 %collective-permute-start.7 = (bf16[1,8,64,128]{3,2,1,0:T(8,128)(2,1)S(1)}, bf16[1,8,64,128]{3,2,1,0:T(8,128)(2,1)S(1)}, u32[]{:S(2)}, u32[]{:S(2)}) collective-permute-start(bf16[1,8,64,128]{3,2,1,0:T(8,128)(2,1)S(1)} %get-tuple-element.72), channel_id=1, source_target_pairs={{0,192},{32,224},{64,128},{96,160},{128,64},{160,96},{192,0},{224,... | collective-permute-start | bytes 393224 | tf_op jit(solution)/shard_map/ppermute | solution.py:410
  36.5 42.1 %all-to-all-start = ((bf16[32,144,128]{2,1,0:T(8,128)(2,1)}), bf16[32,144,128]{2,1,0:T(8,128)(2,1)S(1)}, u32[]{:S(2)}, u32[]{:S(2)}) async-start(bf16[32,144,128]{2,1,0:T(8,128)(2,1)} %get-tuple-element.41), calls=%async_computation | async-start | bytes 2359296 | tf_op jit(solution)/shard_map/all_to_all | solution.py:445
  48.0 7.6 %collective-permute-start.10 = (bf16[2,144,128]{2,1,0:T(8,128)(2,1)S(1)}, bf16[2,144,128]{2,1,0:T(8,128)(2,1)S(1)}, u32[]{:S(2)}, u32[]{:S(2)}) collective-permute-start(bf16[2,144,128]{2,1,0:T(8,128)(2,1)S(1)} %get-tuple-element.43), channel_id=1, source_target_pairs={{0,128},{32,160},{64,192},{96,224},{128,0},{160,32},{192,64},{224,... | collective-permute-start | bytes 221192 | tf_op jit(solution)/shard_map/ppermute | solution.py:410
  48.8 10.3 %collective-permute-start.11 = (bf16[2,144,128]{2,1,0:T(8,128)(2,1)S(1)}, bf16[2,144,128]{2,1,0:T(8,128)(2,1)S(1)}, u32[]{:S(2)}, u32[]{:S(2)}) collective-permute-start(bf16[2,144,128]{2,1,0:T(8,128)(2,1)S(1)} %get-tuple-element.44), channel_id=1, source_target_pairs={{0,160},{32,128},{64,224},{96,192},{128,32},{160,0},{192,96},{224,... | collective-permute-start | bytes 221192 | tf_op jit(solution)/shard_map/ppermute | solution.py:410
  54.4 5.5 %collective-permute-start.12 = (bf16[2,144,128]{2,1,0:T(8,128)(2,1)S(1)}, bf16[2,144,128]{2,1,0:T(8,128)(2,1)S(1)}, u32[]{:S(2)}, u32[]{:S(2)}) collective-permute-start(bf16[2,144,128]{2,1,0:T(8,128)(2,1)S(1)} %get-tuple-element.45), channel_id=1, source_target_pairs={{0,192},{32,224},{64,128},{96,160},{128,64},{160,96},{192,0},{224,... | collective-permute-start | bytes 221192 | tf_op jit(solution)/shard_map/ppermute | solution.py:410
  55.4 6.1 %collective-permute-start.13 = (bf16[2,144,128]{2,1,0:T(8,128)(2,1)S(1)}, bf16[2,144,128]{2,1,0:T(8,128)(2,1)S(1)}, u32[]{:S(2)}, u32[]{:S(2)}) collective-permute-start(bf16[2,144,128]{2,1,0:T(8,128)(2,1)S(1)} %get-tuple-element.46), channel_id=1, source_target_pairs={{0,224},{32,192},{64,160},{96,128},{128,96},{160,64},{192,32},{224... | collective-permute-start | bytes 221192 | tf_op jit(solution)/shard_map/ppermute | solution.py:410
  55.6 5.8 %collective-permute-start.14 = (bf16[2,144,128]{2,1,0:T(8,128)(2,1)S(1)}, bf16[2,144,128]{2,1,0:T(8,128)(2,1)S(1)}, u32[]{:S(2)}, u32[]{:S(2)}) collective-permute-start(bf16[2,144,128]{2,1,0:T(8,128)(2,1)S(1)} %get-tuple-element.47), channel_id=1, source_target_pairs={{0,64},{32,96},{64,0},{96,32},{128,192},{160,224},{192,128},{224,1... | collective-permute-start | bytes 221192 | tf_op jit(solution)/shard_map/ppermute | solution.py:410
  55.6 6.8 %collective-permute-start.15 = (bf16[2,144,128]{2,1,0:T(8,128)(2,1)S(1)}, bf16[2,144,128]{2,1,0:T(8,128)(2,1)S(1)}, u32[]{:S(2)}, u32[]{:S(2)}) collective-permute-start(bf16[2,144,128]{2,1,0:T(8,128)(2,1)S(1)} %get-tuple-element.48), channel_id=1, source_target_pairs={{0,96},{32,64},{64,32},{96,0},{128,224},{160,192},{192,160},{224,1... | collective-permute-start | bytes 221192 | tf_op jit(solution)/shard_map/ppermute | solution.py:410
  59.1 3.3 %collective-permute-start.16 = (bf16[2,144,128]{2,1,0:T(8,128)(2,1)S(1)}, bf16[2,144,128]{2,1,0:T(8,128)(2,1)S(1)}, u32[]{:S(2)}, u32[]{:S(2)}) collective-permute-start(bf16[2,144,128]{2,1,0:T(8,128)(2,1)S(1)} %get-tuple-element.49), channel_id=1, source_target_pairs={{0,32},{32,0},{64,96},{96,64},{128,160},{160,128},{192,224},{224,1... | collective-permute-start | bytes 221192 | tf_op jit(solution)/shard_map/ppermute | solution.py:410
  68.3 7.0 %collective-permute-start.24 = (bf16[2,64,512]{2,1,0:T(8,128)(2,1)S(1)}, bf16[2,64,512]{2,1,0:T(8,128)(2,1)S(1)}, u32[]{:S(2)}, u32[]{:S(2)}) collective-permute-start(bf16[2,64,512]{2,1,0:T(8,128)(2,1)S(1)} %get-tuple-element.61), channel_id=1, source_target_pairs={{0,128},{32,160},{64,192},{96,224},{128,0},{160,32},{192,64},{224,... | collective-permute-start | bytes 393224 | tf_op jit(solution)/shard_map/ppermute | solution.py:410
  68.7 9.5 %collective-permute-start.25 = (bf16[2,64,512]{2,1,0:T(8,128)(2,1)S(1)}, bf16[2,64,512]{2,1,0:T(8,128)(2,1)S(1)}, u32[]{:S(2)}, u32[]{:S(2)}) collective-permute-start(bf16[2,64,512]{2,1,0:T(8,128)(2,1)S(1)} %get-tuple-element.62), channel_id=1, source_target_pairs={{0,160},{32,128},{64,224},{96,192},{128,32},{160,0},{192,96},{224,... | collective-permute-start | bytes 393224 | tf_op jit(solution)/shard_map/ppermute | solution.py:410
  71.1 9.8 %collective-permute-start.26 = (bf16[2,64,512]{2,1,0:T(8,128)(2,1)S(1)}, bf16[2,64,512]{2,1,0:T(8,128)(2,1)S(1)}, u32[]{:S(2)}, u32[]{:S(2)}) collective-permute-start(bf16[2,64,512]{2,1,0:T(8,128)(2,1)S(1)} %get-tuple-element.63), channel_id=1, source_target_pairs={{0,192},{32,224},{64,128},{96,160},{128,64},{160,96},{192,0},{224,... | collective-permute-start | bytes 393224 | tf_op jit(solution)/shard_map/ppermute | solution.py:410
  72.4 11.4 %collective-permute-start.27 = (bf16[2,64,512]{2,1,0:T(8,128)(2,1)S(1)}, bf16[2,64,512]{2,1,0:T(8,128)(2,1)S(1)}, u32[]{:S(2)}, u32[]{:S(2)}) collective-permute-start(bf16[2,64,512]{2,1,0:T(8,128)(2,1)S(1)} %get-tuple-element.64), channel_id=1, source_target_pairs={{0,224},{32,192},{64,160},{96,128},{128,96},{160,64},{192,32},{224... | collective-permute-start | bytes 393224 | tf_op jit(solution)/shard_map/ppermute | solution.py:410
  74.6 10.1 %collective-permute-start.28 = (bf16[2,64,512]{2,1,0:T(8,128)(2,1)S(1)}, bf16[2,64,512]{2,1,0:T(8,128)(2,1)S(1)}, u32[]{:S(2)}, u32[]{:S(2)}) collective-permute-start(bf16[2,64,512]{2,1,0:T(8,128)(2,1)S(1)} %get-tuple-element.65), channel_id=1, source_target_pairs={{0,64},{32,96},{64,0},{96,32},{128,192},{160,224},{192,128},{224,1... | collective-permute-start | bytes 393224 | tf_op jit(solution)/shard_map/ppermute | solution.py:410
  75.3 10.9 %collective-permute-start.29 = (bf16[2,64,512]{2,1,0:T(8,128)(2,1)S(1)}, bf16[2,64,512]{2,1,0:T(8,128)(2,1)S(1)}, u32[]{:S(2)}, u32[]{:S(2)}) collective-permute-start(bf16[2,64,512]{2,1,0:T(8,128)(2,1)S(1)} %get-tuple-element.66), channel_id=1, source_target_pairs={{0,96},{32,64},{64,32},{96,0},{128,224},{160,192},{192,160},{224,1... | collective-permute-start | bytes 393224 | tf_op jit(solution)/shard_map/ppermute | solution.py:410
  78.2 9.3 %collective-permute-start.30 = (bf16[2,64,512]{2,1,0:T(8,128)(2,1)S(1)}, bf16[2,64,512]{2,1,0:T(8,128)(2,1)S(1)}, u32[]{:S(2)}, u32[]{:S(2)}) collective-permute-start(bf16[2,64,512]{2,1,0:T(8,128)(2,1)S(1)} %get-tuple-element.67), channel_id=1, source_target_pairs={{0,32},{32,0},{64,96},{96,64},{128,160},{160,128},{192,224},{224,1... | collective-permute-start | bytes 393224 | tf_op jit(solution)/shard_map/ppermute | solution.py:410
  80.9 6.7 %collective-permute-start.17 = (bf16[3,144,128]{2,1,0:T(8,128)(2,1)S(1)}, bf16[3,144,128]{2,1,0:T(8,128)(2,1)S(1)}, u32[]{:S(2)}, u32[]{:S(2)}) collective-permute-start(bf16[3,144,128]{2,1,0:T(8,128)(2,1)S(1)} %get-tuple-element.53), channel_id=1, source_target_pairs={{0,128},{32,160},{64,192},{96,224},{128,0},{160,32},{192,64},{224,... | collective-permute-start | bytes 331784 | tf_op jit(solution)/shard_map/ppermute | solution.py:410
  83.7 6.7 %collective-permute-start.18 = (bf16[3,144,128]{2,1,0:T(8,128)(2,1)S(1)}, bf16[3,144,128]{2,1,0:T(8,128)(2,1)S(1)}, u32[]{:S(2)}, u32[]{:S(2)}) collective-permute-start(bf16[3,144,128]{2,1,0:T(8,128)(2,1)S(1)} %get-tuple-element.54), channel_id=1, source_target_pairs={{0,160},{32,128},{64,224},{96,192},{128,32},{160,0},{192,96},{224,... | collective-permute-start | bytes 331784 | tf_op jit(solution)/shard_map/ppermute | solution.py:410
  84.6 8.3 %collective-permute-start.19 = (bf16[3,144,128]{2,1,0:T(8,128)(2,1)S(1)}, bf16[3,144,128]{2,1,0:T(8,128)(2,1)S(1)}, u32[]{:S(2)}, u32[]{:S(2)}) collective-permute-start(bf16[3,144,128]{2,1,0:T(8,128)(2,1)S(1)} %get-tuple-element.55), channel_id=1, source_target_pairs={{0,192},{32,224},{64,128},{96,160},{128,64},{160,96},{192,0},{224,... | collective-permute-start | bytes 331784 | tf_op jit(solution)/shard_map/ppermute | solution.py:410
  86.2 9.0 %collective-permute-start.20 = (bf16[3,144,128]{2,1,0:T(8,128)(2,1)S(1)}, bf16[3,144,128]{2,1,0:T(8,128)(2,1)S(1)}, u32[]{:S(2)}, u32[]{:S(2)}) collective-permute-start(bf16[3,144,128]{2,1,0:T(8,128)(2,1)S(1)} %get-tuple-element.56), channel_id=1, source_target_pairs={{0,224},{32,192},{64,160},{96,128},{128,96},{160,64},{192,32},{224... | collective-permute-start | bytes 331784 | tf_op jit(solution)/shard_map/ppermute | solution.py:410
  87.5 7.8 %collective-permute-start.21 = (bf16[3,144,128]{2,1,0:T(8,128)(2,1)S(1)}, bf16[3,144,128]{2,1,0:T(8,128)(2,1)S(1)}, u32[]{:S(2)}, u32[]{:S(2)}) collective-permute-start(bf16[3,144,128]{2,1,0:T(8,128)(2,1)S(1)} %get-tuple-element.57), channel_id=1, source_target_pairs={{0,64},{32,96},{64,0},{96,32},{128,192},{160,224},{192,128},{224,1... | collective-permute-start | bytes 331784 | tf_op jit(solution)/shard_map/ppermute | solution.py:410
  87.6 7.7 %collective-permute-start.22 = (bf16[3,144,128]{2,1,0:T(8,128)(2,1)S(1)}, bf16[3,144,128]{2,1,0:T(8,128)(2,1)S(1)}, u32[]{:S(2)}, u32[]{:S(2)}) collective-permute-start(bf16[3,144,128]{2,1,0:T(8,128)(2,1)S(1)} %get-tuple-element.58), channel_id=1, source_target_pairs={{0,96},{32,64},{64,32},{96,0},{128,224},{160,192},{192,160},{224,1... | collective-permute-start | bytes 331784 | tf_op jit(solution)/shard_map/ppermute | solution.py:410
  90.4 4.9 %collective-permute-start.23 = (bf16[3,144,128]{2,1,0:T(8,128)(2,1)S(1)}, bf16[3,144,128]{2,1,0:T(8,128)(2,1)S(1)}, u32[]{:S(2)}, u32[]{:S(2)}) collective-permute-start(bf16[3,144,128]{2,1,0:T(8,128)(2,1)S(1)} %get-tuple-element.59), channel_id=1, source_target_pairs={{0,32},{32,0},{64,96},{96,64},{128,160},{160,128},{192,224},{224,1... | collective-permute-start | bytes 331784 | tf_op jit(solution)/shard_map/ppermute | solution.py:410
  (2 other events, 9.8 us)

commit v3 on v2

--- a/solution.py
+++ b/solution.py
@@ -16,7 +16,7 @@
 PACKED_ROWS = 9 * TILE
 CHUNK = PACKED_ROWS // DEVICES
 CUTS = (80, 64)
-PARTNERS = (0, 4, 5, 6, 7, 2, 3, 1)
+PARTNERS = (0, 4, 5, 6, 2, 7, 3, 1)
 ROWS = BLOCK // DEVICES
 ORDERS = ((1, 2, 0, 3), (3, 2, 0, 1))
 FIRST_BITS = (2, 6)
@@ -158,7 +158,7 @@
 def sum_kernel(model_count, code_ref, plan_ref, *refs):
     sources = refs[:8]
     outgoing_ref, *home_refs = refs[8 : 9 + DEVICES]
-    mine_ref, out_sems, home_sems = refs[9 + DEVICES :]
+    (mine_ref,) = refs[9 + DEVICES :]
     device, _ = position(code_ref, model_count)
     base = 0
     for group, cut in enumerate(CUTS):
@@ -167,22 +167,10 @@
             value = partial_ref[...] + last_ref[0].astype(F32)
             mine_ref[base : base + value.shape[0], start:stop] = value.astype(BF16)
         base += value.shape[0]
-    copies = []
     for owner in range(model_count):
-        copies.append(
-            pltpu.make_async_copy(
-                mine_ref.at[plan_ref[CAP + 1 + owner]], outgoing_ref.at[owner], out_sems.at[owner]
-            )
-        )
+        outgoing_ref[owner] = mine_ref[plan_ref[CAP + 1 + owner]]
     for bits, home_ref in zip(PARTNERS, home_refs):
-        home = device ^ bits
-        copies.append(
-            pltpu.make_async_copy(mine_ref.at[pl.ds(2 * home, 2)], home_ref, home_sems.at[bits])
-        )
-    for copy in copies:
-        copy.start()
-    for copy in copies:
-        copy.wait()
+        home_ref[...] = mine_ref[pl.ds(2 * (device ^ bits), 2)]
 
 
 def sum_and_send(code, plan, sources, model_count):
@@ -190,12 +178,10 @@
     return pl.pallas_call(
         functools.partial(sum_kernel, model_count),
         in_specs=[whole(pltpu.SMEM), whole(pltpu.SMEM)] + [whole()] * 8,
-        out_specs=[whole(pltpu.HBM)] * (1 + DEVICES),
+        out_specs=[whole()] * (1 + DEVICES),
         out_shape=[jax.ShapeDtypeStruct((model_count, CHUNK, TILE), BF16)] + [home] * DEVICES,
         scratch_shapes=[
             pltpu.VMEM((2 * DEVICES, CHUNK, TILE), BF16),
-            pltpu.SemaphoreType.DMA((model_count,)),
-            pltpu.SemaphoreType.DMA((DEVICES,)),
         ],
         interpret=INTERPRET,
         compiler_params=params(),

time: 105 us -> 104 us (level)
  waiting for transfers between devices: 25.7 us -> 22.8 us
  starting transfers between devices: 46.6 us -> 48.1 us
    ppermute x31, waiting for transfers between devices: 25.7 us -> 22.8 us  [exchange(): return lax.ppermute(value, 'dp', [(d, d ^ bits) for d in range(data_count)])]
    ppermute x31, starting transfers between devices: 35.2 us -> 36.7 us  [exchange(): return lax.ppermute(value, 'dp', [(d, d ^ bits) for d in range(data_count)])]
  transfers between devices with their start and end apart: 32 -> 32, of which waited for: 15 -> 12; matrix products, arithmetic and copies ran while one was open for 1% -> 1% of each run, Pallas kernels for 13% -> 13%
where the time goes in v3:
time: 104 us
  starting transfers between devices  48.1 us (46%)
  Pallas kernels  28.7 us (28%)
  waiting for transfers between devices  22.8 us (22%)
  local copies, waits for them, and re-layouts  2.19 us (2%)
    ppermute x31, starting transfers between devices, exchange(): return lax.ppermute(value, 'dp', [(d, d ^ bits) for d in range(data_count)])  36.7 us
    ppermute x31, waiting for transfers between devices, exchange(): return lax.ppermute(value, 'dp', [(d, d ^ bits) for d in range(data_count)])  22.8 us
    all_to_all x1, starting transfers between devices, program(): lax.all_to_all(outgoing, 'mp', split_axis=0, concat_axis=0, tiled=True)  11.4 us
    pallas_call x1, Pallas kernels, owner_roots(): pl.pallas_call(functools.partial(owner_kernel, data_count, model_count),...  9.76 us
    pallas_call x2, Pallas kernels, gram_blocks(): pl.pallas_call(functools.partial(gram_kernel, model_count, cut), out_shap...  6.87 us
    pallas_call x1, Pallas kernels, home_roots(): pl.pallas_call(functools.partial(home_kernel, data_count, model_count), i...  5.86 us
    unnamed x4, local copies, waits for them, and re-layouts  2.19 us
  transfers between devices with their start and end apart: 32, of which 12 were waited for; matrix products, arithmetic and copies ran while one was open for 1% of the time, Pallas kernels for 13%

profile of v3, /device:TPU:1, one launch (start us, length us, event | category | flops | bytes accessed | tf_op | source)
XLA Modules:
  0.0 103.6 jit_solution(15434658865277547031)
XLA Ops:
  0.6 2.2 %copy-done = bf16[1,4096,512]{2,1,0:T(8,128)(2,1)S(1)} copy-done((bf16[1,4096,512]{2,1,0:T(8,128)(2,1)S(1)}, bf16[1,4096,512]{2,1,0:T(8,128)(2,1)}, u32[]{:S(2)}) %copy-start) | copy-done | bytes 4194328
  2.8 3.4 %shard_map.41 = (bf16[4,8,144,128]{3,2,1,0:T(8,128)(2,1)S(1)}, bf16[4,8,144,128]{3,2,1,0:T(8,128)(2,1)S(1)}) custom-call(s32[1]{0:T(128)} %bitcast.code_ref, bf16[8,512,512]{2,1,0:T(8,128)(2,1)S(1)} %bitcast.11), custom_call_target="tpu_custom_call" | custom-call | flops 1610612736 | bytes 5242880 | tf_op jit(solution)/shard_map/pallas_call | solution.py:107
  6.3 3.3 %collective-permute-start = (bf16[4,8,144,128]{3,2,1,0:T(8,128)(2,1)S(1)}, bf16[4,8,144,128]{3,2,1,0:T(8,128)(2,1)S(1)}, u32[]{:S(2)}, u32[]{:S(2)}) collective-permute-start(bf16[4,8,144,128]{3,2,1,0:T(8,128)(2,1)S(1)} %get-tuple-element.37), channel_id=1, source_target_pairs={{0,32},{32,0},{64,96},{96,64},{128,160},{160,128},{192,224},{224,1... | collective-permute-start | bytes 3538952 | tf_op jit(solution)/shard_map/ppermute | solution.py:396
  9.6 3.4 %shard_map.42 = (bf16[4,8,144,128]{3,2,1,0:T(8,128)(2,1)S(1)}, bf16[4,8,144,128]{3,2,1,0:T(8,128)(2,1)S(1)}) custom-call(s32[1]{0:T(128)} %bitcast.code_ref, bf16[8,512,512]{2,1,0:T(8,128)(2,1)S(1)} %bitcast.12), custom_call_target="tpu_custom_call" | custom-call | flops 1610612736 | bytes 5242880 | tf_op jit(solution)/shard_map/pallas_call | solution.py:107
  14.3 1.7 %collective-permute-done.5 = bf16[4,8,144,128]{3,2,1,0:T(8,128)(2,1)S(1)} collective-permute-done((bf16[4,8,144,128]{3,2,1,0:T(8,128)(2,1)S(1)}, bf16[4,8,144,128]{3,2,1,0:T(8,128)(2,1)S(1)}, u32[]{:S(2)}, u32[]{:S(2)}) %collective-permute-start.5) | collective-permute-done | bytes 1179680 | tf_op jit(solution)/shard_map/ppermute | solution.py:396
  16.2 1.8 %collective-permute-start.8 = (bf16[2,8,80,128]{3,2,1,0:T(8,128)(2,1)S(1)}, bf16[2,8,80,128]{3,2,1,0:T(8,128)(2,1)S(1)}, u32[]{:S(2)}, u32[]{:S(2)}) collective-permute-start(bf16[2,8,80,128]{3,2,1,0:T(8,128)(2,1)S(1)} %add_convert_fusion), channel_id=1, source_target_pairs={{0,192},{32,224},{64,128},{96,160},{128,64},{160,96},{192,0},{224,... | collective-permute-start | bytes 983048 | tf_op jit(solution)/shard_map/ppermute | solution.py:396
  18.0 3.9 %collective-permute-done.3 = bf16[2,8,64,128]{3,2,1,0:T(8,128)(2,1)S(1)} collective-permute-done((bf16[2,8,64,128]{3,2,1,0:T(8,128)(2,1)S(1)}, bf16[2,8,64,128]{3,2,1,0:T(8,128)(2,1)S(1)}, u32[]{:S(2)}, u32[]{:S(2)}) %collective-permute-start.3) | collective-permute-done | bytes 262176 | tf_op jit(solution)/shard_map/ppermute | solution.py:396
  22.9 2.0 %collective-permute-start.2 = (bf16[1,8,80,128]{3,2,1,0:T(8,128)(2,1)S(1)}, bf16[1,8,80,128]{3,2,1,0:T(8,128)(2,1)S(1)}, u32[]{:S(2)}, u32[]{:S(2)}) collective-permute-start(bf16[1,8,80,128]{3,2,1,0:T(8,128)(2,1)S(1)} %get-tuple-element.70), channel_id=1, source_target_pairs={{0,192},{32,224},{64,128},{96,160},{128,64},{160,96},{192,0},{224,... | collective-permute-start | bytes 491528 | tf_op jit(solution)/shard_map/ppermute | solution.py:396
  24.9 4.0 %collective-permute-done.8 = bf16[2,8,80,128]{3,2,1,0:T(8,128)(2,1)S(1)} collective-permute-done((bf16[2,8,80,128]{3,2,1,0:T(8,128)(2,1)S(1)}, bf16[2,8,80,128]{3,2,1,0:T(8,128)(2,1)S(1)}, u32[]{:S(2)}, u32[]{:S(2)}) %collective-permute-start.8) | collective-permute-done | bytes 327712 | tf_op jit(solution)/shard_map/ppermute | solution.py:396
  29.3 1.2 %collective-permute-start.7 = (bf16[1,8,64,128]{3,2,1,0:T(8,128)(2,1)S(1)}, bf16[1,8,64,128]{3,2,1,0:T(8,128)(2,1)S(1)}, u32[]{:S(2)}, u32[]{:S(2)}) collective-permute-start(bf16[1,8,64,128]{3,2,1,0:T(8,128)(2,1)S(1)} %get-tuple-element.72), channel_id=1, source_target_pairs={{0,192},{32,224},{64,128},{96,160},{128,64},{160,96},{192,0},{224,... | collective-permute-start | bytes 393224 | tf_op jit(solution)/shard_map/ppermute | solution.py:396
  30.5 2.0 %make_plan.1.plan_ref = s32[57]{0:T(128)S(1)} custom-call(s32[1]{0:T(128)} %bitcast.code_ref, s32[512]{0:T(512)S(1)} %copy-done.1), custom_call_target="tpu_custom_call" | custom-call | flops 4194304 | bytes 4096 | tf_op jit(solution)/shard_map/make_plan/pallas_call | solution.py:146
  32.6 1.9 %collective-permute-done.7.refs_5_ = bf16[1,8,64,128]{3,2,1,0:T(8,128)(2,1)S(1)} collective-permute-done((bf16[1,8,64,128]{3,2,1,0:T(8,128)(2,1)S(1)}, bf16[1,8,64,128]{3,2,1,0:T(8,128)(2,1)S(1)}, u32[]{:S(2)}, u32[]{:S(2)}) %collective-permute-start.7) | collective-permute-done | bytes 131104 | tf_op jit(solution)/shard_map/ppermute | solution.py:396
  34.5 1.8 %sum_and_send.1 = (bf16[32,144,128]{2,1,0:T(8,128)(2,1)}, bf16[2,144,128]{2,1,0:T(8,128)(2,1)S(1)}, bf16[2,144,128]{2,1,0:T(8,128)(2,1)S(1)}, bf16[2,144,128]{2,...) custom-call(s32[1]{0:T(128)} %bitcast.code_ref, ...), custom_call_target="tpu_custom_call" | custom-call | flops 2097152 | bytes 4194304 | tf_op jit(solution)/shard_map/sum_and_send/pallas_call | solution.py:178
  36.3 11.4 %all-to-all-start = ((bf16[32,144,128]{2,1,0:T(8,128)(2,1)}), bf16[32,144,128]{2,1,0:T(8,128)(2,1)S(1)}, u32[]{:S(2)}, u32[]{:S(2)}) async-start(bf16[32,144,128]{2,1,0:T(8,128)(2,1)} %get-tuple-element.41), calls=%async_computation | async-start | bytes 2359296 | tf_op jit(solution)/shard_map/all_to_all | solution.py:431
  48.6 5.6 %collective-permute-start.11 = (bf16[2,144,128]{2,1,0:T(8,128)(2,1)S(1)}, bf16[2,144,128]{2,1,0:T(8,128)(2,1)S(1)}, u32[]{:S(2)}, u32[]{:S(2)}) collective-permute-start(bf16[2,144,128]{2,1,0:T(8,128)(2,1)S(1)} %get-tuple-element.44), channel_id=1, source_target_pairs={{0,160},{32,128},{64,224},{96,192},{128,32},{160,0},{192,96},{224,... | collective-permute-start | bytes 221192 | tf_op jit(solution)/shard_map/ppermute | solution.py:396
  55.4 2.6 %collective-permute-start.15 = (bf16[2,144,128]{2,1,0:T(8,128)(2,1)S(1)}, bf16[2,144,128]{2,1,0:T(8,128)(2,1)S(1)}, u32[]{:S(2)}, u32[]{:S(2)}) collective-permute-start(bf16[2,144,128]{2,1,0:T(8,128)(2,1)S(1)} %get-tuple-element.48), channel_id=1, source_target_pairs={{0,96},{32,64},{64,32},{96,0},{128,224},{160,192},{192,160},{224,1... | collective-permute-start | bytes 221192 | tf_op jit(solution)/shard_map/ppermute | solution.py:396
  58.5 1.1 %collective-permute-done.12.refs_3_ = bf16[2,144,128]{2,1,0:T(8,128)(2,1)S(1)} collective-permute-done((bf16[2,144,128]{2,1,0:T(8,128)(2,1)S(1)}, bf16[2,144,128]{2,1,0:T(8,128)(2,1)S(1)}, u32[]{:S(2)}, u32[]{:S(2)}) %collective-permute-start.12) | collective-permute-done | bytes 73760 | tf_op jit(solution)/shard_map/ppermute | solution.py:396
  59.6 1.6 %collective-permute-done.14.refs_5_ = bf16[2,144,128]{2,1,0:T(8,128)(2,1)S(1)} collective-permute-done((bf16[2,144,128]{2,1,0:T(8,128)(2,1)S(1)}, bf16[2,144,128]{2,1,0:T(8,128)(2,1)S(1)}, u32[]{:S(2)}, u32[]{:S(2)}) %collective-permute-start.14) | collective-permute-done | bytes 73760 | tf_op jit(solution)/shard_map/ppermute | solution.py:396
  61.2 5.9 %home_roots.1 = (bf16[2,64,512]{2,1,0:T(8,128)(2,1)S(1)}, bf16[2,64,512]{2,1,0:T(8,128)(2,1)S(1)}, bf16[2,64,512]{2,1,0:T(8,128)(2,1)S(1)}, bf16[2,64,512]{2,1,0...) custom-call(s32[1]{0:T(128)} %bitcast.code_ref, ...), custom_call_target="tpu_custom_call" | custom-call | flops 4294967296 | bytes 4194304 | tf_op jit(solution)/shard_map/home_roots/pallas_call | solution.py:299
  67.1 1.7 %collective-permute-start.24 = (bf16[2,64,512]{2,1,0:T(8,128)(2,1)S(1)}, bf16[2,64,512]{2,1,0:T(8,128)(2,1)S(1)}, u32[]{:S(2)}, u32[]{:S(2)}) collective-permute-start(bf16[2,64,512]{2,1,0:T(8,128)(2,1)S(1)} %get-tuple-element.61), channel_id=1, source_target_pairs={{0,128},{32,160},{64,192},{96,224},{128,0},{160,32},{192,64},{224,... | collective-permute-start | bytes 393224 | tf_op jit(solution)/shard_map/ppermute | solution.py:396
  68.7 1.9 %collective-permute-start.25 = (bf16[2,64,512]{2,1,0:T(8,128)(2,1)S(1)}, bf16[2,64,512]{2,1,0:T(8,128)(2,1)S(1)}, u32[]{:S(2)}, u32[]{:S(2)}) collective-permute-start(bf16[2,64,512]{2,1,0:T(8,128)(2,1)S(1)} %get-tuple-element.62), channel_id=1, source_target_pairs={{0,160},{32,128},{64,224},{96,192},{128,32},{160,0},{192,96},{224,... | collective-permute-start | bytes 393224 | tf_op jit(solution)/shard_map/ppermute | solution.py:396
  72.0 1.3 %collective-permute-start.28 = (bf16[2,64,512]{2,1,0:T(8,128)(2,1)S(1)}, bf16[2,64,512]{2,1,0:T(8,128)(2,1)S(1)}, u32[]{:S(2)}, u32[]{:S(2)}) collective-permute-start(bf16[2,64,512]{2,1,0:T(8,128)(2,1)S(1)} %get-tuple-element.65), channel_id=1, source_target_pairs={{0,224},{32,192},{64,160},{96,128},{128,96},{160,64},{192,32},{224... | collective-permute-start | bytes 393224 | tf_op jit(solution)/shard_map/ppermute | solution.py:396
  73.4 1.8 %collective-permute-start.29 = (bf16[2,64,512]{2,1,0:T(8,128)(2,1)S(1)}, bf16[2,64,512]{2,1,0:T(8,128)(2,1)S(1)}, u32[]{:S(2)}, u32[]{:S(2)}) collective-permute-start(bf16[2,64,512]{2,1,0:T(8,128)(2,1)S(1)} %get-tuple-element.66), channel_id=1, source_target_pairs={{0,96},{32,64},{64,32},{96,0},{128,224},{160,192},{192,160},{224,1... | collective-permute-start | bytes 393224 | tf_op jit(solution)/shard_map/ppermute | solution.py:396
  75.2 2.1 %collective-permute-done.25.refs_2_ = bf16[2,64,512]{2,1,0:T(8,128)(2,1)S(1)} collective-permute-done((bf16[2,64,512]{2,1,0:T(8,128)(2,1)S(1)}, bf16[2,64,512]{2,1,0:T(8,128)(2,1)S(1)}, u32[]{:S(2)}, u32[]{:S(2)}) %collective-permute-start.25) | collective-permute-done | bytes 131104 | tf_op jit(solution)/shard_map/ppermute | solution.py:396
  77.9 1.8 %collective-permute-done.26.refs_3_ = bf16[2,64,512]{2,1,0:T(8,128)(2,1)S(1)} collective-permute-done((bf16[2,64,512]{2,1,0:T(8,128)(2,1)S(1)}, bf16[2,64,512]{2,1,0:T(8,128)(2,1)S(1)}, u32[]{:S(2)}, u32[]{:S(2)}) %collective-permute-start.26) | collective-permute-done | bytes 131104 | tf_op jit(solution)/shard_map/ppermute | solution.py:396
  79.8 1.6 %collective-permute-start.17 = (bf16[3,144,128]{2,1,0:T(8,128)(2,1)S(1)}, bf16[3,144,128]{2,1,0:T(8,128)(2,1)S(1)}, u32[]{:S(2)}, u32[]{:S(2)}) collective-permute-start(bf16[3,144,128]{2,1,0:T(8,128)(2,1)S(1)} %get-tuple-element.53), channel_id=1, source_target_pairs={{0,128},{32,160},{64,192},{96,224},{128,0},{160,32},{192,64},{224,... | collective-permute-start | bytes 331784 | tf_op jit(solution)/shard_map/ppermute | solution.py:396
  81.4 2.5 %collective-permute-start.18 = (bf16[3,144,128]{2,1,0:T(8,128)(2,1)S(1)}, bf16[3,144,128]{2,1,0:T(8,128)(2,1)S(1)}, u32[]{:S(2)}, u32[]{:S(2)}) collective-permute-start(bf16[3,144,128]{2,1,0:T(8,128)(2,1)S(1)} %get-tuple-element.54), channel_id=1, source_target_pairs={{0,160},{32,128},{64,224},{96,192},{128,32},{160,0},{192,96},{224,... | collective-permute-start | bytes 331784 | tf_op jit(solution)/shard_map/ppermute | solution.py:396
  84.6 1.5 %collective-permute-start.21 = (bf16[3,144,128]{2,1,0:T(8,128)(2,1)S(1)}, bf16[3,144,128]{2,1,0:T(8,128)(2,1)S(1)}, u32[]{:S(2)}, u32[]{:S(2)}) collective-permute-start(bf16[3,144,128]{2,1,0:T(8,128)(2,1)S(1)} %get-tuple-element.57), channel_id=1, source_target_pairs={{0,224},{32,192},{64,160},{96,128},{128,96},{160,64},{192,32},{224... | collective-permute-start | bytes 331784 | tf_op jit(solution)/shard_map/ppermute | solution.py:396
  86.1 1.6 %collective-permute-start.22 = (bf16[3,144,128]{2,1,0:T(8,128)(2,1)S(1)}, bf16[3,144,128]{2,1,0:T(8,128)(2,1)S(1)}, u32[]{:S(2)}, u32[]{:S(2)}) collective-permute-start(bf16[3,144,128]{2,1,0:T(8,128)(2,1)S(1)} %get-tuple-element.58), channel_id=1, source_target_pairs={{0,96},{32,64},{64,32},{96,0},{128,224},{160,192},{192,160},{224,1... | collective-permute-start | bytes 331784 | tf_op jit(solution)/shard_map/ppermute | solution.py:396
  89.0 1.7 %finish_rows.1 = f32[16,64,512]{2,1,0:T(8,128)} custom-call(s32[1]{0:T(128)} %bitcast.code_ref, bf16[2,64,512]{2,1,0:T(8,128)(2,1)S(1)} %get-tuple-element.60.refs_0_, bf16[2,64,512]{2,1,0:T(8,128)(2,1)S(1)} %collective-permute-done.24.refs_1_, bf16[2,64,512]{2,1,0:T(8,128)(2,1)S(1)} %collective-permute-done.25.refs_2_, ...), custom_call_target="tpu_custom_call" | custom-call | flops 2097152 | bytes 4194304 | tf_op jit(solution)/shard_map/finish_rows/pallas_call | solution.py:383
  91.3 2.4 %collective-permute-done.21.refs_5_ = bf16[3,144,128]{2,1,0:T(8,128)(2,1)S(1)} collective-permute-done((bf16[3,144,128]{2,1,0:T(8,128)(2,1)S(1)}, bf16[3,144,128]{2,1,0:T(8,128)(2,1)S(1)}, u32[]{:S(2)}, u32[]{:S(2)}) %collective-permute-start.21) | collective-permute-done | bytes 110624 | tf_op jit(solution)/shard_map/ppermute | solution.py:396
  93.7 9.8 %owner_roots.1 = f32[3,512,512]{2,1,0:T(8,128)} custom-call(s32[1]{0:T(128)} %bitcast.code_ref, s32[57]{0:T(128)S(1)} %make_plan.1.plan_ref, bf16[3,144,128]{2,1,0:T(8,128)(2,1)S(1)} %get-tuple-element.52.refs_0_, bf16[3,144,128]{2,1,0:T(8,128)(2,1)S(1)} %collective-permute-done.17.refs_1_, bf16[3,144,128]{2,1,0:T(8,128)(2,1)S(1)} %collective-permute-done.18.refs_2_, ...), custom_call_target="tpu_custom_call" | custom-call | flops 6442450944 | bytes 4194304 | tf_op jit(solution)/shard_map/owner_roots/pallas_call | solution.py:344
  (52 shorter events, 10.0 us)
Async XLA Ops:
  6.3 6.9 %collective-permute-start = (bf16[4,8,144,128]{3,2,1,0:T(8,128)(2,1)S(1)}, bf16[4,8,144,128]{3,2,1,0:T(8,128)(2,1)S(1)}, u32[]{:S(2)}, u32[]{:S(2)}) collective-permute-start(bf16[4,8,144,128]{3,2,1,0:T(8,128)(2,1)S(1)} %get-tuple-element.37), channel_id=1, source_target_pairs={{0,32},{32,0},{64,96},{96,64},{128,160},{160,128},{192,224},{224,1... | collective-permute-start | bytes 3538952 | tf_op jit(solution)/shard_map/ppermute | solution.py:396
  13.0 2.9 %collective-permute-start.5 = (bf16[4,8,144,128]{3,2,1,0:T(8,128)(2,1)S(1)}, bf16[4,8,144,128]{3,2,1,0:T(8,128)(2,1)S(1)}, u32[]{:S(2)}, u32[]{:S(2)}) collective-permute-start(bf16[4,8,144,128]{3,2,1,0:T(8,128)(2,1)S(1)} %get-tuple-element.40), channel_id=1, source_target_pairs={{0,32},{32,0},{64,96},{96,64},{128,160},{160,128},{192,224},{224,1... | collective-permute-start | bytes 3538952 | tf_op jit(solution)/shard_map/ppermute | solution.py:396
  13.2 8.7 %collective-permute-start.3 = (bf16[2,8,64,128]{3,2,1,0:T(8,128)(2,1)S(1)}, bf16[2,8,64,128]{3,2,1,0:T(8,128)(2,1)S(1)}, u32[]{:S(2)}, u32[]{:S(2)}) collective-permute-start(bf16[2,8,64,128]{3,2,1,0:T(8,128)(2,1)S(1)} %add_convert_fusion.3), channel_id=1, source_target_pairs={{0,192},{32,224},{64,128},{96,160},{128,64},{160,96},{192,0},{224,... | collective-permute-start | bytes 786440 | tf_op jit(solution)/shard_map/ppermute | solution.py:396
  14.2 8.6 %collective-permute-start.1 = (bf16[2,8,80,128]{3,2,1,0:T(8,128)(2,1)S(1)}, bf16[2,8,80,128]{3,2,1,0:T(8,128)(2,1)S(1)}, u32[]{:S(2)}, u32[]{:S(2)}) collective-permute-start(bf16[2,8,80,128]{3,2,1,0:T(8,128)(2,1)S(1)} %add_convert_fusion.1), channel_id=1, source_target_pairs={{0,64},{32,96},{64,0},{96,32},{128,192},{160,224},{192,128},{224,1... | collective-permute-start | bytes 983048 | tf_op jit(solution)/shard_map/ppermute | solution.py:396
  16.0 13.2 %collective-permute-start.6 = (bf16[2,8,64,128]{3,2,1,0:T(8,128)(2,1)S(1)}, bf16[2,8,64,128]{3,2,1,0:T(8,128)(2,1)S(1)}, u32[]{:S(2)}, u32[]{:S(2)}) collective-permute-start(bf16[2,8,64,128]{3,2,1,0:T(8,128)(2,1)S(1)} %add_convert_fusion.2), channel_id=1, source_target_pairs={{0,64},{32,96},{64,0},{96,32},{128,192},{160,224},{192,128},{224,1... | collective-permute-start | bytes 786440 | tf_op jit(solution)/shard_map/ppermute | solution.py:396
  16.2 12.7 %collective-permute-start.8 = (bf16[2,8,80,128]{3,2,1,0:T(8,128)(2,1)S(1)}, bf16[2,8,80,128]{3,2,1,0:T(8,128)(2,1)S(1)}, u32[]{:S(2)}, u32[]{:S(2)}) collective-permute-start(bf16[2,8,80,128]{3,2,1,0:T(8,128)(2,1)S(1)} %add_convert_fusion), channel_id=1, source_target_pairs={{0,192},{32,224},{64,128},{96,160},{128,64},{160,96},{192,0},{224,... | collective-permute-start | bytes 983048 | tf_op jit(solution)/shard_map/ppermute | solution.py:396
  22.0 10.5 %collective-permute-start.4 = (bf16[1,8,64,128]{3,2,1,0:T(8,128)(2,1)S(1)}, bf16[1,8,64,128]{3,2,1,0:T(8,128)(2,1)S(1)}, u32[]{:S(2)}, u32[]{:S(2)}) collective-permute-start(bf16[1,8,64,128]{3,2,1,0:T(8,128)(2,1)S(1)} %get-tuple-element.74), channel_id=1, source_target_pairs={{0,64},{32,96},{64,0},{96,32},{128,192},{160,224},{192,128},{224,1... | collective-permute-start | bytes 393224 | tf_op jit(solution)/shard_map/ppermute | solution.py:396
  22.9 11.6 %collective-permute-start.2 = (bf16[1,8,80,128]{3,2,1,0:T(8,128)(2,1)S(1)}, bf16[1,8,80,128]{3,2,1,0:T(8,128)(2,1)S(1)}, u32[]{:S(2)}, u32[]{:S(2)}) collective-permute-start(bf16[1,8,80,128]{3,2,1,0:T(8,128)(2,1)S(1)} %get-tuple-element.70), channel_id=1, source_target_pairs={{0,192},{32,224},{64,128},{96,160},{128,64},{160,96},{192,0},{224,... | collective-permute-start | bytes 491528 | tf_op jit(solution)/shard_map/ppermute | solution.py:396
  29.1 5.4 %collective-permute-start.9 = (bf16[1,8,80,128]{3,2,1,0:T(8,128)(2,1)S(1)}, bf16[1,8,80,128]{3,2,1,0:T(8,128)(2,1)S(1)}, u32[]{:S(2)}, u32[]{:S(2)}) collective-permute-start(bf16[1,8,80,128]{3,2,1,0:T(8,128)(2,1)S(1)} %get-tuple-element.68), channel_id=1, source_target_pairs={{0,64},{32,96},{64,0},{96,32},{128,192},{160,224},{192,128},{224,1... | collective-permute-start | bytes 491528 | tf_op jit(solution)/shard_map/ppermute | solution.py:396
  29.3 5.2 %collective-permute-start.7 = (bf16[1,8,64,128]{3,2,1,0:T(8,128)(2,1)S(1)}, bf16[1,8,64,128]{3,2,1,0:T(8,128)(2,1)S(1)}, u32[]{:S(2)}, u32[]{:S(2)}) collective-permute-start(bf16[1,8,64,128]{3,2,1,0:T(8,128)(2,1)S(1)} %get-tuple-element.72), channel_id=1, source_target_pairs={{0,192},{32,224},{64,128},{96,160},{128,64},{160,96},{192,0},{224,... | collective-permute-start | bytes 393224 | tf_op jit(solution)/shard_map/ppermute | solution.py:396
  36.3 41.0 %all-to-all-start = ((bf16[32,144,128]{2,1,0:T(8,128)(2,1)}), bf16[32,144,128]{2,1,0:T(8,128)(2,1)S(1)}, u32[]{:S(2)}, u32[]{:S(2)}) async-start(bf16[32,144,128]{2,1,0:T(8,128)(2,1)} %get-tuple-element.41), calls=%async_computation | async-start | bytes 2359296 | tf_op jit(solution)/shard_map/all_to_all | solution.py:431
  47.7 7.6 %collective-permute-start.10 = (bf16[2,144,128]{2,1,0:T(8,128)(2,1)S(1)}, bf16[2,144,128]{2,1,0:T(8,128)(2,1)S(1)}, u32[]{:S(2)}, u32[]{:S(2)}) collective-permute-start(bf16[2,144,128]{2,1,0:T(8,128)(2,1)S(1)} %get-tuple-element.43), channel_id=1, source_target_pairs={{0,128},{32,160},{64,192},{96,224},{128,0},{160,32},{192,64},{224,... | collective-permute-start | bytes 221192 | tf_op jit(solution)/shard_map/ppermute | solution.py:396
  48.6 9.4 %collective-permute-start.11 = (bf16[2,144,128]{2,1,0:T(8,128)(2,1)S(1)}, bf16[2,144,128]{2,1,0:T(8,128)(2,1)S(1)}, u32[]{:S(2)}, u32[]{:S(2)}) collective-permute-start(bf16[2,144,128]{2,1,0:T(8,128)(2,1)S(1)} %get-tuple-element.44), channel_id=1, source_target_pairs={{0,160},{32,128},{64,224},{96,192},{128,32},{160,0},{192,96},{224,... | collective-permute-start | bytes 221192 | tf_op jit(solution)/shard_map/ppermute | solution.py:396
  54.1 5.5 %collective-permute-start.12 = (bf16[2,144,128]{2,1,0:T(8,128)(2,1)S(1)}, bf16[2,144,128]{2,1,0:T(8,128)(2,1)S(1)}, u32[]{:S(2)}, u32[]{:S(2)}) collective-permute-start(bf16[2,144,128]{2,1,0:T(8,128)(2,1)S(1)} %get-tuple-element.45), channel_id=1, source_target_pairs={{0,192},{32,224},{64,128},{96,160},{128,64},{160,96},{192,0},{224,... | collective-permute-start | bytes 221192 | tf_op jit(solution)/shard_map/ppermute | solution.py:396
  55.1 4.5 %collective-permute-start.13 = (bf16[2,144,128]{2,1,0:T(8,128)(2,1)S(1)}, bf16[2,144,128]{2,1,0:T(8,128)(2,1)S(1)}, u32[]{:S(2)}, u32[]{:S(2)}) collective-permute-start(bf16[2,144,128]{2,1,0:T(8,128)(2,1)S(1)} %get-tuple-element.46), channel_id=1, source_target_pairs={{0,64},{32,96},{64,0},{96,32},{128,192},{160,224},{192,128},{224,1... | collective-permute-start | bytes 221192 | tf_op jit(solution)/shard_map/ppermute | solution.py:396
  55.1 6.1 %collective-permute-start.14 = (bf16[2,144,128]{2,1,0:T(8,128)(2,1)S(1)}, bf16[2,144,128]{2,1,0:T(8,128)(2,1)S(1)}, u32[]{:S(2)}, u32[]{:S(2)}) collective-permute-start(bf16[2,144,128]{2,1,0:T(8,128)(2,1)S(1)} %get-tuple-element.47), channel_id=1, source_target_pairs={{0,224},{32,192},{64,160},{96,128},{128,96},{160,64},{192,32},{224... | collective-permute-start | bytes 221192 | tf_op jit(solution)/shard_map/ppermute | solution.py:396
  55.4 5.8 %collective-permute-start.15 = (bf16[2,144,128]{2,1,0:T(8,128)(2,1)S(1)}, bf16[2,144,128]{2,1,0:T(8,128)(2,1)S(1)}, u32[]{:S(2)}, u32[]{:S(2)}) collective-permute-start(bf16[2,144,128]{2,1,0:T(8,128)(2,1)S(1)} %get-tuple-element.48), channel_id=1, source_target_pairs={{0,96},{32,64},{64,32},{96,0},{128,224},{160,192},{192,160},{224,1... | collective-permute-start | bytes 221192 | tf_op jit(solution)/shard_map/ppermute | solution.py:396
  58.0 3.2 %collective-permute-start.16 = (bf16[2,144,128]{2,1,0:T(8,128)(2,1)S(1)}, bf16[2,144,128]{2,1,0:T(8,128)(2,1)S(1)}, u32[]{:S(2)}, u32[]{:S(2)}) collective-permute-start(bf16[2,144,128]{2,1,0:T(8,128)(2,1)S(1)} %get-tuple-element.49), channel_id=1, source_target_pairs={{0,32},{32,0},{64,96},{96,64},{128,160},{160,128},{192,224},{224,1... | collective-permute-start | bytes 221192 | tf_op jit(solution)/shard_map/ppermute | solution.py:396
  67.1 6.3 %collective-permute-start.24 = (bf16[2,64,512]{2,1,0:T(8,128)(2,1)S(1)}, bf16[2,64,512]{2,1,0:T(8,128)(2,1)S(1)}, u32[]{:S(2)}, u32[]{:S(2)}) collective-permute-start(bf16[2,64,512]{2,1,0:T(8,128)(2,1)S(1)} %get-tuple-element.61), channel_id=1, source_target_pairs={{0,128},{32,160},{64,192},{96,224},{128,0},{160,32},{192,64},{224,... | collective-permute-start | bytes 393224 | tf_op jit(solution)/shard_map/ppermute | solution.py:396
  68.7 8.6 %collective-permute-start.25 = (bf16[2,64,512]{2,1,0:T(8,128)(2,1)S(1)}, bf16[2,64,512]{2,1,0:T(8,128)(2,1)S(1)}, u32[]{:S(2)}, u32[]{:S(2)}) collective-permute-start(bf16[2,64,512]{2,1,0:T(8,128)(2,1)S(1)} %get-tuple-element.62), channel_id=1, source_target_pairs={{0,160},{32,128},{64,224},{96,192},{128,32},{160,0},{192,96},{224,... | collective-permute-start | bytes 393224 | tf_op jit(solution)/shard_map/ppermute | solution.py:396
  70.7 9.1 %collective-permute-start.26 = (bf16[2,64,512]{2,1,0:T(8,128)(2,1)S(1)}, bf16[2,64,512]{2,1,0:T(8,128)(2,1)S(1)}, u32[]{:S(2)}, u32[]{:S(2)}) collective-permute-start(bf16[2,64,512]{2,1,0:T(8,128)(2,1)S(1)} %get-tuple-element.63), channel_id=1, source_target_pairs={{0,192},{32,224},{64,128},{96,160},{128,64},{160,96},{192,0},{224,... | collective-permute-start | bytes 393224 | tf_op jit(solution)/shard_map/ppermute | solution.py:396
  71.6 9.8 %collective-permute-start.27 = (bf16[2,64,512]{2,1,0:T(8,128)(2,1)S(1)}, bf16[2,64,512]{2,1,0:T(8,128)(2,1)S(1)}, u32[]{:S(2)}, u32[]{:S(2)}) collective-permute-start(bf16[2,64,512]{2,1,0:T(8,128)(2,1)S(1)} %get-tuple-element.64), channel_id=1, source_target_pairs={{0,64},{32,96},{64,0},{96,32},{128,192},{160,224},{192,128},{224,1... | collective-permute-start | bytes 393224 | tf_op jit(solution)/shard_map/ppermute | solution.py:396
  72.0 11.9 %collective-permute-start.28 = (bf16[2,64,512]{2,1,0:T(8,128)(2,1)S(1)}, bf16[2,64,512]{2,1,0:T(8,128)(2,1)S(1)}, u32[]{:S(2)}, u32[]{:S(2)}) collective-permute-start(bf16[2,64,512]{2,1,0:T(8,128)(2,1)S(1)} %get-tuple-element.65), channel_id=1, source_target_pairs={{0,224},{32,192},{64,160},{96,128},{128,96},{160,64},{192,32},{224... | collective-permute-start | bytes 393224 | tf_op jit(solution)/shard_map/ppermute | solution.py:396
  73.4 11.1 %collective-permute-start.29 = (bf16[2,64,512]{2,1,0:T(8,128)(2,1)S(1)}, bf16[2,64,512]{2,1,0:T(8,128)(2,1)S(1)}, u32[]{:S(2)}, u32[]{:S(2)}) collective-permute-start(bf16[2,64,512]{2,1,0:T(8,128)(2,1)S(1)} %get-tuple-element.66), channel_id=1, source_target_pairs={{0,96},{32,64},{64,32},{96,0},{128,224},{160,192},{192,160},{224,1... | collective-permute-start | bytes 393224 | tf_op jit(solution)/shard_map/ppermute | solution.py:396
  77.3 7.3 %collective-permute-start.30 = (bf16[2,64,512]{2,1,0:T(8,128)(2,1)S(1)}, bf16[2,64,512]{2,1,0:T(8,128)(2,1)S(1)}, u32[]{:S(2)}, u32[]{:S(2)}) collective-permute-start(bf16[2,64,512]{2,1,0:T(8,128)(2,1)S(1)} %get-tuple-element.67), channel_id=1, source_target_pairs={{0,32},{32,0},{64,96},{96,64},{128,160},{160,128},{192,224},{224,1... | collective-permute-start | bytes 393224 | tf_op jit(solution)/shard_map/ppermute | solution.py:396
  79.8 6.3 %collective-permute-start.17 = (bf16[3,144,128]{2,1,0:T(8,128)(2,1)S(1)}, bf16[3,144,128]{2,1,0:T(8,128)(2,1)S(1)}, u32[]{:S(2)}, u32[]{:S(2)}) collective-permute-start(bf16[3,144,128]{2,1,0:T(8,128)(2,1)S(1)} %get-tuple-element.53), channel_id=1, source_target_pairs={{0,128},{32,160},{64,192},{96,224},{128,0},{160,32},{192,64},{224,... | collective-permute-start | bytes 331784 | tf_op jit(solution)/shard_map/ppermute | solution.py:396
  81.4 7.4 %collective-permute-start.18 = (bf16[3,144,128]{2,1,0:T(8,128)(2,1)S(1)}, bf16[3,144,128]{2,1,0:T(8,128)(2,1)S(1)}, u32[]{:S(2)}, u32[]{:S(2)}) collective-permute-start(bf16[3,144,128]{2,1,0:T(8,128)(2,1)S(1)} %get-tuple-element.54), channel_id=1, source_target_pairs={{0,160},{32,128},{64,224},{96,192},{128,32},{160,0},{192,96},{224,... | collective-permute-start | bytes 331784 | tf_op jit(solution)/shard_map/ppermute | solution.py:396
  83.9 7.4 %collective-permute-start.19 = (bf16[3,144,128]{2,1,0:T(8,128)(2,1)S(1)}, bf16[3,144,128]{2,1,0:T(8,128)(2,1)S(1)}, u32[]{:S(2)}, u32[]{:S(2)}) collective-permute-start(bf16[3,144,128]{2,1,0:T(8,128)(2,1)S(1)} %get-tuple-element.55), channel_id=1, source_target_pairs={{0,192},{32,224},{64,128},{96,160},{128,64},{160,96},{192,0},{224,... | collective-permute-start | bytes 331784 | tf_op jit(solution)/shard_map/ppermute | solution.py:396
  84.5 6.9 %collective-permute-start.20 = (bf16[3,144,128]{2,1,0:T(8,128)(2,1)S(1)}, bf16[3,144,128]{2,1,0:T(8,128)(2,1)S(1)}, u32[]{:S(2)}, u32[]{:S(2)}) collective-permute-start(bf16[3,144,128]{2,1,0:T(8,128)(2,1)S(1)} %get-tuple-element.56), channel_id=1, source_target_pairs={{0,64},{32,96},{64,0},{96,32},{128,192},{160,224},{192,128},{224,1... | collective-permute-start | bytes 331784 | tf_op jit(solution)/shard_map/ppermute | solution.py:396
  84.6 9.1 %collective-permute-start.21 = (bf16[3,144,128]{2,1,0:T(8,128)(2,1)S(1)}, bf16[3,144,128]{2,1,0:T(8,128)(2,1)S(1)}, u32[]{:S(2)}, u32[]{:S(2)}) collective-permute-start(bf16[3,144,128]{2,1,0:T(8,128)(2,1)S(1)} %get-tuple-element.57), channel_id=1, source_target_pairs={{0,224},{32,192},{64,160},{96,128},{128,96},{160,64},{192,32},{224... | collective-permute-start | bytes 331784 | tf_op jit(solution)/shard_map/ppermute | solution.py:396
  86.1 7.6 %collective-permute-start.22 = (bf16[3,144,128]{2,1,0:T(8,128)(2,1)S(1)}, bf16[3,144,128]{2,1,0:T(8,128)(2,1)S(1)}, u32[]{:S(2)}, u32[]{:S(2)}) collective-permute-start(bf16[3,144,128]{2,1,0:T(8,128)(2,1)S(1)} %get-tuple-element.58), channel_id=1, source_target_pairs={{0,96},{32,64},{64,32},{96,0},{128,224},{160,192},{192,160},{224,1... | collective-permute-start | bytes 331784 | tf_op jit(solution)/shard_map/ppermute | solution.py:396
  88.8 4.9 %collective-permute-start.23 = (bf16[3,144,128]{2,1,0:T(8,128)(2,1)S(1)}, bf16[3,144,128]{2,1,0:T(8,128)(2,1)S(1)}, u32[]{:S(2)}, u32[]{:S(2)}) collective-permute-start(bf16[3,144,128]{2,1,0:T(8,128)(2,1)S(1)} %get-tuple-element.59), channel_id=1, source_target_pairs={{0,32},{32,0},{64,96},{96,64},{128,160},{160,128},{192,224},{224,1... | collective-permute-start | bytes 331784 | tf_op jit(solution)/shard_map/ppermute | solution.py:396
  (2 other events, 9.8 us)
